TPU v7x, 16 devices: a whole 2x2x2 slice. The times are simulated.
16 devices in a mesh: dp: 4 (over z, y), emb: 4 (over x, core).
Axes of the slice: x: 2, y: 2, z: 2, core: 2. Of those that a mesh axis runs over, the one named last changes fastest.
Arguments:
- tok_ids: int32 [8192], P(('dp', 'emb'))
- resid_in: bfloat16 [8192, 1024], P(('dp', 'emb'))
- cot_out: bfloat16 [8192, 1024], P(('dp', 'emb'))
- tables: bfloat16 [3, 65536, 1024], P(None, 'emb')
- w_up: bfloat16 [3, 1024, 4096], replicated
- w_down: bfloat16 [3, 4096, 1024], replicated
- w_gate: bfloat16 [3, 1024, 1024], replicated
- w_proj: bfloat16 [3, 1024, 1024], replicated
Outputs:
- output 1: bfloat16 [8192, 1024], P(('dp', 'emb'))
- output 2: float32 [3, 65536, 1024], P(None, 'emb')
All inputs are finite; a program needn't handle non-finite values.
Results may differ from a plain program's by a relative error of at most 0.00918168.
Values are sent between devices in bfloat16 or wider.
A program may use at most 1.5 GiB of HBM per device.

v0:
```python
import jax
import jax.numpy as jnp
from jax import lax
from jax.sharding import PartitionSpec as P

NORM_EPS = 1e-6


def rms_norm(x_f32):
    return x_f32 * lax.rsqrt(jnp.mean(x_f32 * x_f32, axis=-1, keepdims=True) + NORM_EPS)


def layer_forward(resid_cur, fetched, w_up_l, w_down_l, w_gate_l, w_proj_l):
    x_f32 = resid_cur.astype(jnp.float32)
    normed = rms_norm(x_f32).astype(jnp.bfloat16)
    up_pre = jnp.dot(normed, w_up_l, preferred_element_type=jnp.float32)
    hidden = jax.nn.gelu(up_pre).astype(jnp.bfloat16)
    mlp_out = jnp.dot(hidden, w_down_l, preferred_element_type=jnp.float32)
    gate_pre = jnp.dot(normed, w_gate_l, preferred_element_type=jnp.float32)
    gate_act = jax.nn.gelu(gate_pre)
    mixed_in = (gate_act * fetched.astype(jnp.float32)).astype(jnp.bfloat16)
    proj_out = jnp.dot(mixed_in, w_proj_l, preferred_element_type=jnp.float32)
    resid_next = (x_f32 + mlp_out + proj_out).astype(jnp.bfloat16)
    return resid_next, (resid_cur, up_pre, gate_pre, gate_act, fetched)


def layer_backward(cot_next, layer_saved, w_up_l, w_down_l, w_gate_l, w_proj_l):
    resid_cur, up_pre, gate_pre, gate_act, fetched = layer_saved
    d_mixed = jnp.einsum('td,ed->te', cot_next, w_proj_l, preferred_element_type=jnp.float32).astype(jnp.bfloat16).astype(jnp.float32)
    grad_rows = gate_act * d_mixed
    d_gate_act = d_mixed * fetched.astype(jnp.float32)
    d_gate_pre = jax.vjp(jax.nn.gelu, gate_pre)[1](d_gate_act)[0]
    d_hidden = jnp.einsum('td,fd->tf', cot_next, w_down_l, preferred_element_type=jnp.float32).astype(jnp.bfloat16)
    d_up_pre = jax.vjp(jax.nn.gelu, up_pre)[1](d_hidden.astype(jnp.float32))[0]
    d_norm_mlp = jnp.einsum('tf,df->td', d_up_pre.astype(jnp.bfloat16), w_up_l, preferred_element_type=jnp.float32).astype(jnp.bfloat16)
    d_norm_gate = jnp.einsum('te,de->td', d_gate_pre.astype(jnp.bfloat16), w_gate_l, preferred_element_type=jnp.float32).astype(jnp.bfloat16)
    d_normed = (d_norm_mlp + d_norm_gate).astype(jnp.float32)
    d_x_norm = jax.vjp(rms_norm, resid_cur.astype(jnp.float32))[1](d_normed)[0]
    cot_cur = (cot_next.astype(jnp.float32) + d_x_norm).astype(jnp.bfloat16)
    return cot_cur, grad_rows


def route_plan(tok_ids, range_rows, n_emb, cap_rows):
    owner_ids = tok_ids // range_rows
    local_off = tok_ids - owner_ids * range_rows
    one_hot = (owner_ids[:, None] == jnp.arange(n_emb, dtype=jnp.int32)[None, :]).astype(jnp.int32)
    rank_in = jnp.sum((jnp.cumsum(one_hot, axis=0) - one_hot) * one_hot, axis=1)
    slot_of = owner_ids * cap_rows + rank_in
    tok_count = tok_ids.shape[0]
    slot_token = jnp.zeros((n_emb * cap_rows,), jnp.int32).at[slot_of].set(jnp.arange(tok_count, dtype=jnp.int32))
    slot_mask = jnp.zeros((n_emb * cap_rows,), jnp.float32).at[slot_of].set(1.0)
    send_ids = jnp.where(slot_mask > 0, jnp.take(local_off, slot_token), 0)
    return slot_of, slot_token, slot_mask, send_ids


def solution(mesh):
    n_emb = mesh.shape['emb']
    tok_spec = P(('dp', 'emb'))
    act_spec = P(('dp', 'emb'), None)
    table_spec = P(None, 'emb', None)
    full_spec = P(None, None, None)

    def device_body(tok_ids, resid_in, cot_out, tables, w_up, w_down, w_gate, w_proj):
        n_layers = tables.shape[0]
        range_rows = tables.shape[1]
        tok_count = tok_ids.shape[0]
        cap_rows = min(2 * tok_count // n_emb, 3 * tok_count // 4)
        slot_of, slot_token, slot_mask, send_ids = route_plan(tok_ids, range_rows, n_emb, cap_rows)
        recv_ids = lax.all_to_all(send_ids, 'emb', 0, 0, tiled=True)
        resid_cur = resid_in
        saved_acts = []
        for l_idx in range(n_layers):
            served = jnp.take(tables[l_idx], recv_ids, axis=0)
            returned = lax.all_to_all(served, 'emb', 0, 0, tiled=True)
            fetched = jnp.take(returned, slot_of, axis=0)
            resid_cur, layer_saved = layer_forward(resid_cur, fetched, w_up[l_idx], w_down[l_idx], w_gate[l_idx], w_proj[l_idx])
            saved_acts.append(layer_saved)
        cot_cur = cot_out
        grad_list = [None] * n_layers
        for l_idx in reversed(range(n_layers)):
            cot_cur, grad_rows = layer_backward(cot_cur, saved_acts[l_idx], w_up[l_idx], w_down[l_idx], w_gate[l_idx], w_proj[l_idx])
            outgoing = jnp.take(grad_rows, slot_token, axis=0) * slot_mask[:, None]
            incoming = lax.all_to_all(outgoing, 'emb', 0, 0, tiled=True)
            shard_grad = jax.ops.segment_sum(incoming, recv_ids, num_segments=range_rows)
            grad_list[l_idx] = lax.psum(shard_grad, 'dp')
        return resid_cur, jnp.stack(grad_list)

    return jax.shard_map(device_body, mesh=mesh, in_specs=(tok_spec, act_spec, act_spec, table_spec, full_spec, full_spec, full_spec, full_spec), out_specs=(act_spec, table_spec), check_vma=False)
```

profile of v0, /device:TPU:0, one launch (start us, length us, event | category | flops | bytes accessed | tf_op | source)
XLA Modules:
  0.0 4120.8 jit_solution(9676625337405901386)
XLA Ops:
  14.6 6.9 gather_fusion
  22.1 4.5 all-to-all-start
  26.6 64.8 %slice_bitcast_fusion = (bf16[16384,1024]{1,0:T(8,128)(2,1)}, bf16[16384,1024]{1,0:T(8,128)(2,1)}, bf16[16384,1024]{1,0:T(8,128)(2,1)}) fusion(bf16[3,16384,1024]{2,1,0:T(8,128)(2,1)} %param.17), kind=kLoop, calls=%fused_computation.16 | loop fusion | bytes 201326592 | tf_op jit(solution)/shard_map/squeeze | solution.py:73
  92.0 30.3 gather_fusion.5
  122.3 35.6 gather_fusion.1
  157.9 35.4 gather_fusion.3
  193.3 4.7 broadcast_select_fusion
  198.0 3.7 all-to-all-start.1
  202.1 4.6 fusion.116
  206.6 20.5 all-to-all-done.1
  228.5 3.8 all-to-all-start.2
  232.3 4.6 gather_fusion.2
  236.9 4.8 fusion.149
  241.8 16.1 fusion.121
  257.9 4.6 fusion.145
  262.5 10.3 fusion.42
  272.8 4.4 all-to-all-start.3
  279.8 4.3 fusion.141
  284.1 11.2 fusion.126
  295.3 4.6 fusion.137
  299.9 10.2 fusion.34
  310.1 4.8 gather_fusion.6
  315.0 5.9 convert_multiply_fusion.18
  320.9 15.5 fusion.194
  336.4 5.5 fusion.130
  342.6 15.9 fusion.187
  358.5 4.8 convert_multiply_fusion.15
  363.3 8.2 gather_fusion.9
  371.6 5.9 fusion.125
  377.5 4.5 convert_multiply_fusion.22
  382.0 7.9 gather_fusion.7
  389.9 5.4 gather_fusion.8
  395.3 8.2 select_multiply_fusion.2
  403.5 51.4 %all_to_all.84 = f32[4,256,1024]{2,1,0:T(8,128)} all-to-all(f32[4,256,1024]{2,1,0:T(8,128)S(1)} %bitcast.174), channel_id=1, replica_groups=mesh['dp'=4,'emb'=4] {'emb'}, dimensions={0} | all-to-all | bytes 8388608 | tf_op jit(solution)/shard_map/all_to_all | solution.py:83
  454.9 21.3 broadcast.157.clone.1
  476.2 152.4 %scatter_fusion.1 = f32[16384,1024]{1,0:T(8,128)} fusion(f32[16384,1024]{1,0:T(8,128)} %broadcast.157.clone.1, s32[1024]{0:T(1024)S(1)} %bitcast.180, f32[1024,1024]{1,0:T(8,128)} %bitcast.170), kind=kCustom, calls=%fused_computation.13 | custom fusion | flops 1048576 | bytes 12587008 | tf_op jit(solution)/shard_map/scatter-add | solution.py:84
  628.7 53.5 %all_to_all.85 = f32[4,256,1024]{2,1,0:T(8,128)} all-to-all(f32[4,256,1024]{2,1,0:T(8,128)} %bitcast.173), channel_id=1, replica_groups=mesh['dp'=4,'emb'=4] {'emb'}, dimensions={0} | all-to-all | bytes 8388608 | tf_op jit(solution)/shard_map/all_to_all | solution.py:83
  682.2 21.3 broadcast.157.clone.2
  703.5 152.5 %scatter_fusion = f32[16384,1024]{1,0:T(8,128)} fusion(f32[16384,1024]{1,0:T(8,128)} %broadcast.157.clone.2, s32[1024]{0:T(1024)S(1)} %bitcast.181, f32[1024,1024]{1,0:T(8,128)} %bitcast.171), kind=kCustom, calls=%fused_computation.12 | custom fusion | flops 1048576 | bytes 12587008 | tf_op jit(solution)/shard_map/scatter-add | solution.py:84
  856.1 53.8 %all_to_all.86 = f32[4,256,1024]{2,1,0:T(8,128)} all-to-all(f32[4,256,1024]{2,1,0:T(8,128)} %bitcast.172), channel_id=1, replica_groups=mesh['dp'=4,'emb'=4] {'emb'}, dimensions={0} | all-to-all | bytes 8388608 | tf_op jit(solution)/shard_map/all_to_all | solution.py:83
  909.8 21.6 broadcast.157.clone
  931.4 152.5 %scatter_fusion.2 = f32[16384,1024]{1,0:T(8,128)} fusion(f32[16384,1024]{1,0:T(8,128)} %broadcast.157.clone, s32[1024]{0:T(1024)S(1)} %bitcast.182, f32[1024,1024]{1,0:T(8,128)} %bitcast.169), kind=kCustom, calls=%fused_computation.14 | custom fusion | flops 1048576 | bytes 12587008 | tf_op jit(solution)/shard_map/scatter-add | solution.py:84
  1085.8 3.3 fusion.133
  1089.2 11.9 fusion.129
  1101.1 654.8 %all-reduce.6.cloned.1.call-done = f32[1,16384,1024]{2,1,0:T(8,128)} async-done(((f32[1,16384,1024]{2,1,0:T(8,128)}), f32[1,16384,1024]{2,1,0:T(8,128)}) %all-reduce.6.cloned.1.call-update) | async-done | bytes 67108880 | tf_op jit(solution)/shard_map/psum | solution.py:85
  1755.9 1113.7 %all-reduce.4.cloned.1.call-done = f32[1,16384,1024]{2,1,0:T(8,128)} async-done(((f32[1,16384,1024]{2,1,0:T(8,128)}), f32[1,16384,1024]{2,1,0:T(8,128)}) %all-reduce.4.cloned.1.call-update) | async-done | bytes 67108880 | tf_op jit(solution)/shard_map/psum | solution.py:85
  2869.7 1114.3 %all-reduce.8.cloned.1.call-done = f32[1,16384,1024]{2,1,0:T(8,128)} async-done(((f32[1,16384,1024]{2,1,0:T(8,128)}), f32[1,16384,1024]{2,1,0:T(8,128)}) %all-reduce.8.cloned.1.call-update) | async-done | bytes 67108880 | tf_op jit(solution)/shard_map/psum | solution.py:85
  3984.0 129.8 %pad_maximum_fusion = f32[3,16384,1024]{2,1,0:T(8,128)} fusion(f32[1,16384,1024]{2,1,0:T(8,128)} %all-reduce.8.cloned.1.call-done, f32[1,16384,1024]{2,1,0:T(8,128)} %all-reduce.6.cloned.1.call-done, f32[1,16384,1024]{2,1,0:T(8,128)} %all-reduce.4.cloned.1.call-done), kind=kLoop, calls=%fused_computation.15 | loop fusion | flops 100663296 | bytes 402653184 | tf_op jit(solution)/shard_map/stack | solution.py:86
  (84 shorter events, 15.4 us)
Async XLA Ops:
  9.6 361.9 %copy-start.18 = (pred[512]{0:T(512)(128)(4,1)}, pred[512]{0:T(512)(128)(4,1)S(1)}, u32[]{:S(2)}) copy-start(pred[512]{0:T(512)(128)(4,1)S(1)} %get-tuple-element.4) | copy-start | bytes 1540
  12.1 9.4 copy-start.13
  14.6 6.9 copy-start.15
  22.1 69.3 %all-to-all-start = ((s32[4,256,1]{1,2,0:T(1,128)}), s32[4,256,1]{1,2,0:T(1,128)S(1)}, u32[]{:S(2)}, u32[]{:S(2)}) async-start(s32[4,256,1]{1,2,0:T(1,128)} %bitcast.5), calls=%async_computation | async-start | bytes 8192 | tf_op jit(solution)/shard_map/all_to_all | solution.py:69
  91.4 0.6 copy-start.11
  198.0 3.8 copy-start.10
  198.0 29.2 all-to-all-start.1
  227.2 1.3 copy-start
  228.5 44.3 %all-to-all-start.2 = ((bf16[4,256,1024]{2,1,0:T(8,128)(2,1)}), bf16[4,256,1024]{2,1,0:T(8,128)(2,1)S(1)}, u32[]{:S(2)}, u32[]{:S(2)}) async-start(bf16[4,256,1024]{2,1,0:T(8,128)(2,1)} %bitcast.176), calls=%async_computation.2 | async-start | bytes 4194304 | tf_op jit(solution)/shard_map/all_to_all | solution.py:74
  257.9 4.6 copy-start.21
  272.8 37.3 all-to-all-start.3
  277.2 1478.7 %all-reduce.6.cloned.1.call-start = ((), (), s32[]{:S(2)}) async-start(), calls=%async_computation.8 | async-start | bytes 134217728 | tf_op jit(solution)/shard_map/psum | solution.py:85
  279.8 4.3 copy-start.6
  279.8 4.3 copy-start.22
  295.2 46.6 %copy-start.2 = (bf16[512,1024]{1,0:T(8,128)(2,1)}, bf16[512,1024]{1,0:T(8,128)(2,1)S(1)}, u32[]{:S(2)}) copy-start(bf16[512,1024]{1,0:T(8,128)(2,1)S(1)} %get-tuple-element.23) | copy-start | bytes 3145732
  310.1 4.9 copy-start.1
  314.9 21.4 copy-start.4
  342.5 15.9 copy-start.8
  358.5 4.8 copy-start.14
  363.3 8.2 copy-start.7
  371.5 6.0 copy-start.9
  371.5 6.0 copy-start.20
  371.5 6.0 copy-start.23
  389.9 5.4 copy-start.16
  389.9 5.4 copy-start.17
  454.9 21.3 copy-start.12
  628.6 2241.0 %all-reduce.4.cloned.1.call-start = ((), (), s32[]{:S(2)}) async-start(), calls=%async_computation.7 | async-start | bytes 134217728 | tf_op jit(solution)/shard_map/psum | solution.py:85
  856.0 3128.0 %all-reduce.8.cloned.1.call-start = ((), (), s32[]{:S(2)}) async-start(), calls=%async_computation.9 | async-start | bytes 134217728 | tf_op jit(solution)/shard_map/psum | solution.py:85
  1083.9 1.2 copy-start.5
  1083.9 1.2 copy-start.19
  1083.9 1.9 copy-start.24
  1085.8 3.4 copy-start.3
Sparse Core Ops, SparseCore 0:
  628.7 1127.1 all-reduce.5
  1759.5 1110.1 all-reduce.3
  2873.8 1110.1 all-reduce.7
where the time goes:
time: 4140 us; the launch traced here: 4120 us
  waiting for transfers between devices  2900 us (70%)
  other arithmetic  604 us (15%)
  local copies, waits for them, and re-layouts  280 us (7%)
  blocking collectives  159 us (4%)
  matrix products  144 us (3%)
    psum x3, waiting for transfers between devices, device_body(): grad_list[l_idx] = lax.psum(shard_grad, 'dp')  2880 us
    scatter-add x3, other arithmetic, device_body(): jax.ops.segment_sum(incoming, recv_ids, num_segments=range_rows)  457 us
    all_to_all x3, blocking collectives, device_body(): incoming = lax.all_to_all(outgoing, 'emb', 0, 0, tiled=True)  159 us
    another operation x1, other arithmetic, device_body(): return (resid_cur, jnp.stack(grad_list))  130 us
    gather x3, local copies, waits for them, and re-layouts, device_body(): served = jnp.take(tables[l_idx], recv_ids, axis=0)  101 us
  transfers between devices with their start and end apart: 7, of which 4 were waited for; matrix products, arithmetic and copies ran while one was open for 12% of the time, Pallas kernels for 0%

commit v1 on v0

v1 whole, which is shorter than its diff:
```python
import functools

import jax
import jax.numpy as jnp
from jax import lax
from jax.experimental import pallas as pl
from jax.experimental.pallas import tpu as pltpu
from jax.sharding import PartitionSpec as P


NORM_EPS = 1e-6
BF = jnp.bfloat16
F32 = jnp.float32

CHUNK = 16
BLK = 256
TILE_ROWS = 1024


def rms_norm(x_f32):
    return x_f32 * lax.rsqrt(jnp.mean(x_f32 * x_f32, axis=-1, keepdims=True) + NORM_EPS)


def layer_forward(x, normed, fetched, w_up, w_down, w_gate, w_proj):
    x_f32 = x.astype(F32)
    up_pre = jnp.dot(normed, w_up, preferred_element_type=F32)
    hidden = jax.nn.gelu(up_pre).astype(BF)
    mlp_out = jnp.dot(hidden, w_down, preferred_element_type=F32)
    gate_pre = jnp.dot(normed, w_gate, preferred_element_type=F32)
    gate_act = jax.nn.gelu(gate_pre)
    mixed_in = (gate_act * fetched.astype(F32)).astype(BF)
    proj_out = jnp.dot(mixed_in, w_proj, preferred_element_type=F32)
    x_next = (x_f32 + mlp_out + proj_out).astype(BF)
    return x_next, (x, up_pre, gate_pre, fetched)


def mixed_cot(cot_next, w_proj):
    return jnp.einsum('td,ed->te', cot_next, w_proj, preferred_element_type=F32).astype(BF)


def layer_backward(cot_next, d_mixed, saved, w_up, w_down, w_gate):
    x, up_pre, gate_pre, fetched = saved
    d_gate_act = d_mixed.astype(F32) * fetched.astype(F32)
    d_gate_pre = jax.vjp(jax.nn.gelu, gate_pre)[1](d_gate_act)[0]
    d_hidden = jnp.einsum('td,fd->tf', cot_next, w_down, preferred_element_type=F32).astype(BF)
    d_up_pre = jax.vjp(jax.nn.gelu, up_pre)[1](d_hidden.astype(F32))[0]
    d_norm_mlp = jnp.einsum('tf,df->td', d_up_pre.astype(BF), w_up, preferred_element_type=F32).astype(BF)
    d_norm_gate = jnp.einsum('te,de->td', d_gate_pre.astype(BF), w_gate, preferred_element_type=F32).astype(BF)
    d_normed = (d_norm_mlp + d_norm_gate).astype(F32)
    d_x_norm = jax.vjp(rms_norm, x.astype(F32))[1](d_normed)[0]
    return (cot_next.astype(F32) + d_x_norm).astype(BF)


def serve_kernel(n_layers, cap, cnt_ref, start_ref, ids_ref, tables, out_ref, blocks, tmp, rows, sem):
    n_emb = out_ref.shape[0]
    groups = [(l, e) for l in range(n_layers) for e in range(n_emb)]

    def copy_of(l, slot, row, buf):
        return pltpu.make_async_copy(
            tables.at[l, pl.ds(pl.multiple_of(row, 8), 8), :], blocks.at[buf, slot], sem.at[buf])

    def issue(g):
        l, e = groups[g]

        def body(s, _):
            row = ids_ref[start_ref[e] + s]
            copy_of(l, s, lax.div(row, 8) * 8, g % 2).start()
            return 0

        lax.fori_loop(0, cnt_ref[e], body, 0)

    issue(0)
    for g, (l, e) in enumerate(groups):
        buf = g % 2
        if g + 1 < len(groups):
            issue(g + 1)
        cnt = cnt_ref[e]

        def drain(s, _):
            copy_of(l, 0, 0, buf).wait()
            return 0

        lax.fori_loop(0, cnt, drain, 0)
        rows[...] = jnp.zeros_like(rows)

        def take(s4, _):
            for u in range(4):
                s = jnp.minimum(s4 * 4 + u, cnt - 1)
                q = lax.rem(ids_ref[start_ref[e] + s], 8)
                val = blocks[buf, s].astype(F32)
                for j in range(8):
                    tmp[pl.ds(u * 64 + j * 8, 8), :] = val[:, j * 128:(j + 1) * 128]
                rows[pl.ds(pl.multiple_of(s * 8, 8), 8), :] = tmp[pl.ds(u * 64 + q, 8, stride=8), :]
            return 0

        lax.fori_loop(0, lax.div(cnt + 3, 4), take, 0)
        for j in range(8):
            out_ref[e, l * cap:(l + 1) * cap, j * 128:(j + 1) * 128] = rows[pl.ds(j, cap, stride=8), :].astype(BF)


def serve_rows(tables, counts, starts, local_ids, cap):
    n_layers, _, width = tables.shape
    n_emb = counts.shape[0]
    smem = pl.BlockSpec(memory_space=pltpu.SMEM)
    return pl.pallas_call(
        functools.partial(serve_kernel, n_layers, cap),
        out_shape=jax.ShapeDtypeStruct((n_emb, n_layers * cap, width), BF),
        in_specs=[smem, smem, smem, pl.BlockSpec(memory_space=pl.ANY)],
        out_specs=pl.BlockSpec(memory_space=pltpu.VMEM),
        scratch_shapes=[
            pltpu.VMEM((2, cap, 8, width), BF),
            pltpu.VMEM((256, 128), F32),
            pltpu.VMEM((cap * 8, 128), F32),
            pltpu.SemaphoreType.DMA((2,)),
        ],
        compiler_params=pltpu.CompilerParams(vmem_limit_bytes=40 << 20),
        cost_estimate=pl.CostEstimate(flops=20_000_000_000, bytes_accessed=30_000_000, transcendentals=0),
        name="serve_rows",
    )(counts, starts, local_ids, tables)


def owner_kernel(layer, meta_ref, bound_ref, ids_ref, u_hbm, d_hbm, w_ref, *rest):
    out, uc, dc, prod, acc, sem_u, sem_d, sem_o = rest[-8:]
    n_src = 16
    tile_rows = TILE_ROWS
    n_tiles = bound_ref.shape[0] // n_src - 1
    src_rows = u_hbm.shape[0] // n_src

    def pull(src, dst, sem):
        def run(k, _):
            lo, off = meta_ref[k], meta_ref[2 * n_src + k]

            def chunk(c, _):
                a = pl.multiple_of(k * src_rows + lo + c * CHUNK, CHUNK)
                b = pl.multiple_of((off + c) * CHUNK, CHUNK)
                pltpu.make_async_copy(src.at[pl.ds(a, CHUNK), :], dst.at[pl.ds(b, CHUNK), :], sem).start()
                return 0

            return lax.fori_loop(0, meta_ref[n_src + k], chunk, 0)

        lax.fori_loop(0, n_src, run, 0)

    def drain(src, dst, sem):
        def one(c, _):
            pltpu.make_async_copy(src.at[pl.ds(0, CHUNK), :], dst.at[pl.ds(0, CHUNK), :], sem).wait()
            return 0

        lax.fori_loop(0, meta_ref[3 * n_src], one, 0)

    pull(u_hbm, uc, sem_u)
    pull(d_hbm, dc, sem_d)
    drain(u_hbm, uc, sem_u)
    drain(d_hbm, dc, sem_d)

    def block(b, _):
        r0 = pl.multiple_of(b * BLK, BLK)
        u = uc[pl.ds(r0, BLK), :]
        for n in range(4):
            pre = jnp.dot(u, w_ref[:, n * 256:(n + 1) * 256], preferred_element_type=F32)
            val = jax.nn.gelu(pre) * dc[pl.ds(r0, BLK), n * 256:(n + 1) * 256].astype(F32)
            for j in range(2):
                col = n * 2 + j
                for t in range(BLK // 8):
                    prod[pl.ds(pl.multiple_of(b * (BLK * 8) + t * 64 + col * 8, 8), 8), :] = (
                        val[t * 8:(t + 1) * 8, j * 128:(j + 1) * 128])
        return 0

    lax.fori_loop(0, lax.div(meta_ref[3 * n_src] * CHUNK + BLK - 1, BLK), block, 0)

    def out_copy(t, buf):
        return pltpu.make_async_copy(
            acc.at[buf].reshape(tile_rows // 8, 8, 8, 128),
            out.at[layer, pl.ds(t * (tile_rows // 8), tile_rows // 8)], sem_o.at[buf])

    def tile(t, _):
        buf = lax.rem(t, 2)

        @pl.when(t >= 2)
        def _():
            out_copy(t - 2, buf).wait()

        def clear(i, _):
            base = pl.multiple_of(i * 512, 512)
            acc[buf, pl.ds(base, 512), :] = jnp.zeros((512, 128), F32)
            return 0

        lax.fori_loop(0, tile_rows * 8 // 512, clear, 0)
        row0 = meta_ref[3 * n_src + 1] + t * tile_rows

        def run(k, _):
            first = bound_ref[k * (n_tiles + 1) + t]
            last = bound_ref[k * (n_tiles + 1) + t + 1]
            shift = meta_ref[2 * n_src + k] * CHUNK - meta_ref[k]

            def one(i, _):
                r = ids_ref[k * src_rows + i] - row0
                p = i + shift
                ra = lax.shift_right_logical(r, 3) * 64 + lax.bitwise_and(r, 7)
                pa = lax.shift_right_logical(p, 3) * 64 + lax.bitwise_and(p, 7)
                acc[buf, pl.ds(ra, 8, stride=8), :] += prod[pl.ds(pa, 8, stride=8), :]
                return 0

            return lax.fori_loop(first, last, one, 0)

        lax.fori_loop(0, n_src, run, 0)
        out_copy(t, buf).start()
        return 0

    lax.fori_loop(0, n_tiles, tile, 0)
    out_copy(n_tiles - 2, n_tiles % 2).wait()
    out_copy(n_tiles - 1, (n_tiles - 1) % 2).wait()


def owner_grad(layer, out_prev, out_shape, meta, bounds, ids, u_all, d_all, w_gate):
    smem = pl.BlockSpec(memory_space=pltpu.SMEM)
    hbm = pl.BlockSpec(memory_space=pl.ANY)
    width = w_gate.shape[0]
    max_rows = 17 * BLK
    args = [meta, bounds, ids, u_all, d_all, w_gate]
    specs = [smem, smem, smem, hbm, hbm, pl.BlockSpec(memory_space=pltpu.VMEM)]
    aliases = {}
    if out_prev is not None:
        args.append(out_prev)
        specs.append(hbm)
        aliases = {6: 0}
    return pl.pallas_call(
        functools.partial(owner_kernel, layer),
        out_shape=jax.ShapeDtypeStruct(out_shape, F32),
        in_specs=specs,
        out_specs=hbm,
        scratch_shapes=[
            pltpu.VMEM((max_rows, width), BF),
            pltpu.VMEM((max_rows, width), BF),
            pltpu.VMEM((max_rows * 8, 128), F32),
            pltpu.VMEM((2, TILE_ROWS * 8, 128), F32),
            pltpu.SemaphoreType.DMA,
            pltpu.SemaphoreType.DMA,
            pltpu.SemaphoreType.DMA((2,)),
        ],
        input_output_aliases=aliases,
        compiler_params=pltpu.CompilerParams(vmem_limit_bytes=58 << 20),
        cost_estimate=pl.CostEstimate(flops=40_000_000_000, bytes_accessed=100_000_000, transcendentals=0),
    )(*args)


def solution(mesh):
    n_emb = mesh.shape['emb']
    n_dev = n_emb * mesh.shape['dp']
    tok_spec = P(('dp', 'emb'))
    act_spec = P(('dp', 'emb'), None)
    table_spec = P(None, 'emb', None)
    full_spec = P(None, None, None)
    everyone = ('dp', 'emb')

    def device_body(tok_ids, resid_in, cot_out, tables, w_up, w_down, w_gate, w_proj):
        n_layers, range_rows, _ = tables.shape
        n_tok = tok_ids.shape[0]
        cap = min(2 * n_tok // n_emb, 3 * n_tok // 4)
        i_dp, i_emb = lax.axis_index('dp'), lax.axis_index('emb')

        pos = jnp.arange(n_tok, dtype=jnp.int32)
        before = (tok_ids[None, :] < tok_ids[:, None]) | ((tok_ids[None, :] == tok_ids[:, None]) & (pos[None, :] < pos[:, None]))
        rank = jnp.sum(before.astype(jnp.int32), axis=1)
        perm_mask = rank[None, :] == pos[:, None]
        perm = perm_mask.astype(BF)
        ids = jnp.sum(jnp.where(perm_mask, tok_ids[None, :], 0), axis=1)
        ids_all = lax.all_gather(ids, everyone, axis=0, tiled=True)
        ids_2d = ids_all.reshape(n_dev, n_tok)

        x = jnp.dot(perm, resid_in, preferred_element_type=F32).astype(BF)
        cot = jnp.dot(perm, cot_out, preferred_element_type=F32).astype(BF)

        n_tiles = range_rows // TILE_ROWS
        base = i_emb * range_rows
        edges = base + jnp.arange(n_tiles + 1, dtype=jnp.int32) * TILE_ROWS
        bounds = jnp.sum((ids_2d[:, None, :] < edges[None, :, None]).astype(jnp.int32), axis=2)
        lo = bounds[:, 0]
        hi = bounds[:, n_tiles]
        lo16 = (lo // CHUNK) * CHUNK
        n_ch = (hi - lo16 + CHUNK - 1) // CHUNK
        tri = jnp.arange(n_dev)[None, :] < jnp.arange(n_dev)[:, None]
        off = jnp.sum(jnp.where(tri, n_ch[None, :], 0), axis=1)
        meta = jnp.concatenate([lo16, n_ch, off, jnp.stack([jnp.sum(n_ch), base])]).astype(jnp.int32)

        mine = lax.dynamic_slice(ids_2d, (i_dp * n_emb, 0), (n_emb, n_tok))
        peer_lo = jnp.sum((mine < base).astype(jnp.int32), axis=1)
        peer_hi = jnp.sum((mine < base + range_rows).astype(jnp.int32), axis=1)
        served = serve_rows(tables, peer_hi - peer_lo, peer_lo + jnp.arange(n_emb, dtype=jnp.int32) * n_tok,
                            mine.reshape(-1) - base, cap)
        returned = lax.all_to_all(served, 'emb', 0, 0, tiled=True)
        returned = returned.reshape(n_emb, n_layers, cap, -1)
        owner = ids // range_rows
        first = jnp.sum((owner[None, :] < owner[:, None]).astype(jnp.int32), axis=1)
        slot = owner * cap + pos - first
        pick = (slot[:, None] == jnp.arange(n_emb * cap, dtype=jnp.int32)[None, :]).astype(BF)

        def gather(rows):
            return lax.all_gather(rows, everyone, axis=0, tiled=True)

        last = n_layers - 1
        u_all, saved = [], []
        d_all = [None] * n_layers
        normed = rms_norm(x.astype(F32)).astype(BF)
        u_all.append(gather(normed))
        d_mixed = mixed_cot(cot, w_proj[last])
        d_all[last] = gather(d_mixed)
        for l in range(n_layers):
            rows_l = returned[:, l].reshape(n_emb * cap, -1)
            fetched = jnp.dot(pick, rows_l, preferred_element_type=F32).astype(BF)
            x, kept = layer_forward(x, normed, fetched, w_up[l], w_down[l], w_gate[l], w_proj[l])
            saved.append(kept)
            if l < last:
                normed = rms_norm(x.astype(F32)).astype(BF)
                u_all.append(gather(normed))
        resid_out = lax.dot_general(perm, x, (((0,), (0,)), ((), ())), preferred_element_type=F32).astype(BF)
        for l in range(last, 0, -1):
            cot = layer_backward(cot, d_mixed, saved[l], w_up[l], w_down[l], w_gate[l])
            d_mixed = mixed_cot(cot, w_proj[l - 1])
            d_all[l - 1] = gather(d_mixed)

        width = tables.shape[2]
        grads = None
        out_shape = (n_layers, range_rows // 8, width // 128, 8, 128)
        for l in range(last, -1, -1):
            grads = owner_grad(l, grads, out_shape, meta, bounds.reshape(-1), ids_all, u_all[l], d_all[l], w_gate[l])
        d_tables = grads.transpose(0, 1, 3, 2, 4).reshape(n_layers, range_rows, width)
        return resid_out, d_tables

    return jax.shard_map(device_body, mesh=mesh, in_specs=(tok_spec, act_spec, act_spec, table_spec, full_spec, full_spec, full_spec, full_spec), out_specs=(act_spec, table_spec), check_vma=False)
```

time: 4140 us -> 721 us (0.17)
  waiting for transfers between devices: 2900 us -> 212 us
  other arithmetic: 604 us -> 7.73 us
  Pallas kernels: 0 us -> 291 us
  local copies, waits for them, and re-layouts: 280 us -> 21 us
  blocking collectives: 159 us -> 14.6 us
    psum x3 -> x0, waiting for transfers between devices: 2880 us -> none  [device_body(): grad_list[l_idx] = lax.psum(shard_grad, 'dp')]
    scatter-add x3 -> x0, other arithmetic: 457 us -> none  [device_body(): jax.ops.segment_sum(incoming, recv_ids, num_segments=range_rows)]
    pallas_call x0 -> x4, Pallas kernels: none -> 291 us  [the longest x3 219 us: owner_grad(): pl.pallas_call(functools.partial(owner_kernel, layer), out_shape=jax.Shap...]
    all_to_all x3 -> x0, blocking collectives: 159 us -> none  [device_body(): incoming = lax.all_to_all(outgoing, 'emb', 0, 0, tiled=True)]
    all_gather x0 -> x6, waiting for transfers between devices: none -> 147 us  [gather(): return lax.all_gather(rows, everyone, axis=0, tiled=True)]
    gather x10 -> x0, local copies, waits for them, and re-layouts: 142 us -> none  [the longest x3 101 us: device_body(): served = jnp.take(tables[l_idx], recv_ids, axis=0)]
    another operation x3 -> x0, other arithmetic: 131 us -> none  [the longest x1 130 us: device_body(): return (resid_cur, jnp.stack(grad_list))]
    another operation x3 -> x0, local copies, waits for them, and re-layouts: 64.1 us -> none
  transfers between devices with their start and end apart: 7 -> 7, of which waited for: 4 -> 4; matrix products, arithmetic and copies ran while one was open for 12% -> 23% of each run, Pallas kernels for 0% -> 31%
where the time goes in v1:
time: 721 us; the launch traced here: 714 us
  Pallas kernels  291 us (40%)
  waiting for transfers between devices  212 us (29%)
  matrix products  147 us (20%)
  local copies, waits for them, and re-layouts  21 us (3%)
  between operations  14.7 us (2%)
  blocking collectives  14.6 us (2%)
  other arithmetic  7.73 us (1%)
    pallas_call x3, Pallas kernels, owner_grad(): pl.pallas_call(functools.partial(owner_kernel, layer), out_shape=jax.Shap...  219 us
    all_gather x6, waiting for transfers between devices, gather(): return lax.all_gather(rows, everyone, axis=0, tiled=True)  147 us
    pallas_call x1, Pallas kernels, serve_rows(): pl.pallas_call(functools.partial(serve_kernel, n_layers, cap), out_shape=...  72.3 us
    all_to_all x1, waiting for transfers between devices, device_body(): returned = lax.all_to_all(served, 'emb', 0, 0, tiled=True)  64.1 us
    dot_general x2, matrix products, layer_backward(): jnp.einsum('tf,df->td', d_up_pre.astype(BF), w_up, preferred_element_type...  31.7 us
    dot_general x2, matrix products, layer_forward(): mlp_out = jnp.dot(hidden, w_down, preferred_element_type=F32)  28.8 us
    dot_general x2, matrix products, layer_forward(): up_pre = jnp.dot(normed, w_up, preferred_element_type=F32)  17.3 us
    all_gather x1, blocking collectives, device_body(): ids_all = lax.all_gather(ids, everyone, axis=0, tiled=True)  14.6 us
  transfers between devices with their start and end apart: 7, of which 4 were waited for; matrix products, arithmetic and copies ran while one was open for 23% of the time, Pallas kernels for 31%

profile of v1, /device:TPU:0, one launch (start us, length us, event | category | flops | bytes accessed | tf_op | source)
XLA Modules:
  0.0 713.8 jit_solution(7215437797869106786)
XLA Ops:
  7.2 1.1 convert_reduce_fusion.1
  8.3 1.9 convolution_convert_fusion.2
  10.3 1.0 copy-done.5
  11.3 3.9 fusion.169
  15.4 14.6 %all-gather = s32[16,1,512]{2,1,0:T(1,128)S(1)} all-gather(s32[1,1,512]{2,1,0:T(1,128)S(1)} %bitcast.154), channel_id=1, replica_groups=mesh['dp'=4,'emb'=4] {'dp','emb'}, dimensions={0}, use_global_device_ids=true | all-gather | bytes 34816 | tf_op jit(solution)/shard_map/all_gather | solution.py:267
  30.6 72.3 %serve_rows.1 = bf16[4,768,1024]{2,1,0:T(8,128)(2,1)S(1)} custom-call(s32[4]{0:T(128)S(1)} %get-tuple-element.15.cnt_ref, s32[4]{0:T(128)S(1)} %get-tuple-element.14.start_ref, s32[2048]{0:T(1024)S(1)} %bitcast.146, bf16[3,16384,1024]{2,1,0:T(8,128)(2,1)} %tables.1), custom_call_target="tpu_custom_call" | custom-call | flops 20000000000 | bytes 30000000 | tf_op jit(solution)/shard_map/serve_rows/pallas_call | solution.py:105
  102.9 2.7 copy-done.2
  105.6 5.3 all-to-all-start
  111.3 0.8 fusion.106
  112.2 1.0 copy-done.9
  113.2 4.3 fusion.288
  117.4 64.1 %all-to-all-done = bf16[4,768,1024]{2,1,0:T(8,128)(2,1)} async-done(((bf16[4,768,1024]{2,1,0:T(8,128)(2,1)}), bf16[4,768,1024]{2,1,0:T(8,128)(2,1)}, u32[]{:S(2)}, u32[]{:S(2)}) %all-to-all-start) | async-done | bytes 6291488 | tf_op jit(solution)/shard_map/all_to_all | solution.py:290
  181.5 5.8 fusion.296
  187.3 6.7 fusion.143
  194.0 16.9 %fusion.123 = (f32[512]{0:T(512)S(1)}, bf16[512,1024]{1,0:T(8,128)(2,1)}) fusion(f32[512,1024]{1,0:T(8,128)} %fusion.143, bf16[3,4096,1024]{2,1,0:T(8,128)(2,1)} %param.13, bf16[3,1024,4096]{2,1,0:T(8,128)(2,1)} %param.12, bf16[512,1024]{1,0:T(8,128)(2,1)S(1)} %copy-done.10, f32[512]{0:T(512)S(1)} %add_rsqrt_fusion), kind=kOutput, calls=%fused_computation.141 | convolution fusion | flops 8614051840 | bytes 22024192 | tf_op jit(solution)/shard_map/dot_general | solution.py:28
  210.9 1.5 fusion.124
  212.4 3.3 fusion.161
  215.7 3.2 fusion.289
  218.9 1.3 copy-done.17
  220.3 3.1 fusion.139
  223.4 7.0 fusion.42
  230.4 11.9 %fusion.128 = (f32[512]{0:T(512)S(1)}, bf16[512,1024]{1,0:T(8,128)(2,1)S(1)}) fusion(f32[512,1024]{1,0:T(8,128)S(1)} %fusion.139, bf16[3,4096,1024]{2,1,0:T(8,128)(2,1)} %param.13, f32[512,4096]{1,0:T(8,128)S(1)} %fusion.42, bf16[512,1024]{1,0:T(8,128)(2,1)S(1)} %copy-done.7), kind=kOutput, calls=%fused_computation.146 | convolution fusion | flops 4317511168 | bytes 20973568 | tf_op jit(solution)/shard_map/dot_general | solution.py:28
  242.3 1.2 fusion.129
  243.8 2.3 fusion.162
  246.1 4.2 fusion.290
  250.2 10.3 %fusion.34 = f32[512,4096]{1,0:T(8,128)} fusion(bf16[512,1024]{1,0:T(8,128)(2,1)S(1)} %copy-done.4, bf16[3,1024,4096]{2,1,0:T(8,128)(2,1)} %param.12), kind=kOutput, calls=%fused_computation.43 | convolution fusion | flops 4294967296 | bytes 17825792 | tf_op jit(solution)/shard_map/dot_general | solution.py:26
  260.6 15.7 %fusion.179 = bf16[512,1024]{1,0:T(8,128)(2,1)} fusion(bf16[3,1024,4096]{2,1,0:T(8,128)(2,1)} %param.12, f32[512,4096]{1,0:T(8,128)} %fusion.34, bf16[512,1024]{1,0:T(8,128)(2,1)S(1)} %copy-done.6, bf16[3,4096,1024]{2,1,0:T(8,128)(2,1)} %param.13), kind=kOutput, calls=%fused_computation.188 | convolution fusion | flops 8636596224 | bytes 27262976 | tf_op jit(solution)/shard_map/tf,df->td/dot_general | solution.py:47
  276.2 5.4 fusion.132
  281.6 0.7 fusion.120
  282.3 3.9 fusion.166
  286.2 0.5 all-gather.12.cloned.1.call-update
  286.8 0.9 copy-done.11
  287.7 1.2 fusion.107
  289.0 16.1 %fusion.172 = bf16[512,1024]{1,0:T(8,128)(2,1)} fusion(bf16[3,1024,4096]{2,1,0:T(8,128)(2,1)} %param.12, f32[512,4096]{1,0:T(8,128)} %copy-done.18, bf16[512,1024]{1,0:T(8,128)(2,1)S(1)} %fusion.120, bf16[3,4096,1024]{2,1,0:T(8,128)(2,1)} %param.13), kind=kOutput, calls=%fused_computation.187 | convolution fusion | flops 8636596224 | bytes 27262976 | tf_op jit(solution)/shard_map/tf,df->td/dot_general | solution.py:47
  305.1 5.7 fusion.127
  310.9 4.1 fusion.163
  315.5 0.7 reshape.166.bound_ref
  316.2 0.7 fusion.294
  317.1 1.3 concatenate.3.meta_ref
  318.4 5.8 slice_bitcast_fusion
  324.2 3.1 fusion.135
  327.3 13.1 %convolution_convert_fusion.3 = bf16[512,1024]{1,0:T(8,128)(2,1)} fusion(f32[512,1024]{1,0:T(8,128)S(1)} %fusion.135, bf16[512,1024]{1,0:T(8,128)(2,1)S(1)} %get-tuple-element.21, bf16[3,4096,1024]{2,1,0:T(8,128)(2,1)} %param.13, f32[512,4096]{1,0:T(8,128)} %fusion.34, s32[512]{0:T(512)S(1)} %convert_reduce_fusion.1), kind=kOutput, calls=%fused_computation.185 | convolution fusion | flops 4853596160 | bytes 20973568 | tf_op jit(solution)/shard_map/dot_general | solution.py:315
  340.4 73.1 %shard_map.95.rest_0_ = f32[3,2048,8,8,128]{4,3,2,1,0:T(8,128)} custom-call(s32[50]{0:T(128)} %concatenate.3.meta_ref, s32[272]{0:T(512)} %reshape.166.bound_ref, s32[8192]{0:T(1024)} %bitcast.150, bf16[8192,1024]{1,0:T(8,128)(2,1)} %all-gather.16.cloned.1.call-done.u_hbm, bf16[8192,1024]{1,0:T(8,128)(2,1)} %all-gather.18.cloned.1.call-done.d_hbm, ...), custom_call_target="tpu_custom_call" | custom-call | flops 40000000000 | bytes 100000000 | tf_op jit(solution)/shard_map/pallas_call | solution.py:226
  413.5 63.1 %all-gather.12.cloned.1.call-done.u_hbm = bf16[8192,1024]{1,0:T(8,128)(2,1)} async-done(((bf16[512,1024]{1,0:T(8,128)(2,1)}), bf16[8192,1024]{1,0:T(8,128)(2,1)}) %all-gather.12.cloned.1.call-update) | async-done | bytes 16777232 | tf_op jit(solution)/shard_map/all_gather | solution.py:298
  476.7 72.8 %shard_map.96.rest_0_ = f32[3,2048,8,8,128]{4,3,2,1,0:T(8,128)} custom-call(s32[50]{0:T(128)} %concatenate.3.meta_ref, s32[272]{0:T(512)} %reshape.166.bound_ref, s32[8192]{0:T(1024)} %bitcast.151, bf16[8192,1024]{1,0:T(8,128)(2,1)} %all-gather.12.cloned.1.call-done.u_hbm, ...), custom_call_target="tpu_custom_call", output_to_operand_aliasing={{}: (6, {})} | custom-call | flops 40000000000 | bytes 100000000 | tf_op jit(solution)/shard_map/pallas_call | solution.py:226
  549.5 5.7 all-gather.8.cloned.1.call-done.u_hbm
  555.2 78.6 %all-gather.10.cloned.1.call-done.d_hbm = bf16[8192,1024]{1,0:T(8,128)(2,1)} async-done(((bf16[512,1024]{1,0:T(8,128)(2,1)}), bf16[8192,1024]{1,0:T(8,128)(2,1)}) %all-gather.10.cloned.1.call-update) | async-done | bytes 16777232 | tf_op jit(solution)/shard_map/all_gather | solution.py:298
  633.8 72.9 %shard_map.97 = f32[3,2048,8,8,128]{4,3,2,1,0:T(8,128)} custom-call(s32[50]{0:T(128)} %concatenate.3.meta_ref, s32[272]{0:T(512)} %reshape.166.bound_ref, s32[8192]{0:T(1024)} %bitcast.152, bf16[8192,1024]{1,0:T(8,128)(2,1)} %all-gather.8.cloned.1.call-done.u_hbm, ...), custom_call_target="tpu_custom_call", output_to_operand_aliasing={{}: (6, {})} | custom-call | flops 40000000000 | bytes 100000000 | tf_op jit(solution)/shard_map/pallas_call | solution.py:226
  (67 shorter events, 2.5 us)
Async XLA Ops:
  7.2 104.2 %copy-start = (bf16[512,1024]{1,0:T(8,128)(2,1)S(1)}, bf16[512,1024]{1,0:T(8,128)(2,1)}, u32[]{:S(2)}) copy-start(bf16[512,1024]{1,0:T(8,128)(2,1)} %param.9) | copy-start | bytes 3145732
  7.2 333.2 %all-gather.18.cloned.1.call-start = ((), (), s32[]{:S(2)}) async-start(), calls=%async_computation.6 | async-start | bytes 17825792 | tf_op jit(solution)/shard_map/all_gather | solution.py:298
  10.3 1.0 copy-start.5
  11.3 3.9 copy-start.15
  30.0 0.6 copy-start.13
  102.9 2.7 copy-start.2
  105.6 75.9 %all-to-all-start = ((bf16[4,768,1024]{2,1,0:T(8,128)(2,1)}), bf16[4,768,1024]{2,1,0:T(8,128)(2,1)}, u32[]{:S(2)}, u32[]{:S(2)}) async-start(bf16[4,768,1024]{2,1,0:T(8,128)(2,1)} %copy-done.2), calls=%async_computation | async-start | bytes 12582912 | tf_op jit(solution)/shard_map/all_to_all | solution.py:290
  110.8 229.6 %all-gather.16.cloned.1.call-start = ((), (), s32[]{:S(2)}) async-start(), calls=%async_computation.5 | async-start | bytes 17825792 | tf_op jit(solution)/shard_map/all_gather | solution.py:298
  112.1 1.0 copy-start.9
  187.3 6.7 copy-start.10
  212.4 11.0 %copy-start.3 = (bf16[512,1024]{1,0:T(8,128)(2,1)}, bf16[512,1024]{1,0:T(8,128)(2,1)S(1)}, u32[]{:S(2)}) copy-start(bf16[512,1024]{1,0:T(8,128)(2,1)S(1)} %fusion.124) | copy-start | bytes 3145732
  215.7 3.2 copy-start.20
  218.9 1.3 copy-start.17
  223.4 7.0 copy-start.7
  230.4 11.9 %copy-start.18 = (f32[512,4096]{1,0:T(8,128)}, f32[512,4096]{1,0:T(8,128)S(1)}, u32[]{:S(2)}) copy-start(f32[512,4096]{1,0:T(8,128)S(1)} %fusion.42) | copy-start | bytes 25165828
  243.6 169.9 %all-gather.14.cloned.1.call-start = ((), (), s32[]{:S(2)}) async-start(), calls=%async_computation.4 | async-start | bytes 17825792 | tf_op jit(solution)/shard_map/all_gather | solution.py:298
  243.8 2.3 copy-start.4
  250.2 10.4 %copy-start.6 = (bf16[512,1024]{1,0:T(8,128)(2,1)S(1)}, bf16[512,1024]{1,0:T(8,128)(2,1)}, u32[]{:S(2)}) copy-start(bf16[512,1024]{1,0:T(8,128)(2,1)} %copy-done.5) | copy-start | bytes 3145732
  260.6 15.7 %copy-start.12 = (bf16[512,1024]{1,0:T(8,128)(2,1)S(1)}, bf16[512,1024]{1,0:T(8,128)(2,1)}, u32[]{:S(2)}) copy-start(bf16[512,1024]{1,0:T(8,128)(2,1)} %fusion.169) | copy-start | bytes 3145732
  286.2 1.5 copy-start.11
  286.2 190.5 %all-gather.12.cloned.1.call-start = ((), (), s32[]{:S(2)}) async-start(), calls=%async_computation.3 | async-start | bytes 17825792 | tf_op jit(solution)/shard_map/all_gather | solution.py:298
  286.8 268.5 %all-gather.8.cloned.1.call-start = ((), (), s32[]{:S(2)}) async-start(), calls=%async_computation.1 | async-start | bytes 17825792 | tf_op jit(solution)/shard_map/all_gather | solution.py:298
  289.0 16.1 %copy-start.8 = (bf16[512,1024]{1,0:T(8,128)(2,1)S(1)}, bf16[512,1024]{1,0:T(8,128)(2,1)}, u32[]{:S(2)}) copy-start(bf16[512,1024]{1,0:T(8,128)(2,1)} %get-tuple-element.19) | copy-start | bytes 3145732
  289.0 344.8 %all-gather.10.cloned.1.call-start = ((), (), s32[]{:S(2)}) async-start(), calls=%async_computation.2 | async-start | bytes 17825792 | tf_op jit(solution)/shard_map/all_gather | solution.py:298
  310.9 4.1 copy-start.14
  318.4 5.8 copy-start.16
  318.4 5.8 copy-start.19
  633.8 72.9 %copy-start.1 = (bf16[512,1024]{1,0:T(8,128)(2,1)S(1)}, bf16[512,1024]{1,0:T(8,128)(2,1)}, u32[]{:S(2)}) copy-start(bf16[512,1024]{1,0:T(8,128)(2,1)} %param.9) | copy-start | bytes 3145732
Sparse Core Ops, SparseCore 0:
  15.3 79.2 all-gather.17
  243.7 75.6 all-gather.15
  321.6 76.4 all-gather.13
  400.2 76.4 all-gather.11
  478.8 76.4 all-gather.7
  557.3 76.4 all-gather.9

commit v2 on v1

v2 whole, which is shorter than its diff:
```python
import functools

import jax
import jax.numpy as jnp
from jax import lax
from jax.experimental import pallas as pl
from jax.experimental.pallas import tpu as pltpu
from jax.sharding import PartitionSpec as P


NORM_EPS = 1e-6
BF = jnp.bfloat16
F32 = jnp.float32

CHUNK = 16
BLK = 256
TILE_ROWS = 1024


def rms_norm(x_f32):
    return x_f32 * lax.rsqrt(jnp.mean(x_f32 * x_f32, axis=-1, keepdims=True) + NORM_EPS)


def layer_forward(x, normed, fetched, w_up, w_down, w_gate, w_proj):
    x_f32 = x.astype(F32)
    up_pre = jnp.dot(normed, w_up, preferred_element_type=F32)
    hidden = jax.nn.gelu(up_pre).astype(BF)
    mlp_out = jnp.dot(hidden, w_down, preferred_element_type=F32)
    gate_pre = jnp.dot(normed, w_gate, preferred_element_type=F32)
    gate_act = jax.nn.gelu(gate_pre)
    mixed_in = (gate_act * fetched.astype(F32)).astype(BF)
    proj_out = jnp.dot(mixed_in, w_proj, preferred_element_type=F32)
    x_next = (x_f32 + mlp_out + proj_out).astype(BF)
    return x_next, (x, up_pre, gate_pre, fetched)


def mixed_cot(cot_next, w_proj):
    return jnp.einsum('td,ed->te', cot_next, w_proj, preferred_element_type=F32).astype(BF)


def layer_backward(cot_next, d_mixed, saved, w_up, w_down, w_gate):
    x, up_pre, gate_pre, fetched = saved
    d_gate_act = d_mixed.astype(F32) * fetched.astype(F32)
    d_gate_pre = jax.vjp(jax.nn.gelu, gate_pre)[1](d_gate_act)[0]
    d_hidden = jnp.einsum('td,fd->tf', cot_next, w_down, preferred_element_type=F32).astype(BF)
    d_up_pre = jax.vjp(jax.nn.gelu, up_pre)[1](d_hidden.astype(F32))[0]
    d_norm_mlp = jnp.einsum('tf,df->td', d_up_pre.astype(BF), w_up, preferred_element_type=F32).astype(BF)
    d_norm_gate = jnp.einsum('te,de->td', d_gate_pre.astype(BF), w_gate, preferred_element_type=F32).astype(BF)
    d_normed = (d_norm_mlp + d_norm_gate).astype(F32)
    d_x_norm = jax.vjp(rms_norm, x.astype(F32))[1](d_normed)[0]
    return (cot_next.astype(F32) + d_x_norm).astype(BF)


PICK = 32


def serve_kernel(n_layers, cap, cnt_ref, row_ref, pick_ref, tables, out_ref, blocks, sem):
    n_emb = out_ref.shape[0]

    def issue(e):
        def body(s, _):
            row = pl.multiple_of(row_ref[e * cap + s], 8)
            slot = pl.multiple_of(s * 8, 8)
            pltpu.make_async_copy(
                tables.at[:, pl.ds(row, 8), :], blocks.at[e % 2, :, pl.ds(slot, 8), :], sem.at[e % 2]).start()
            return 0

        lax.fori_loop(0, cnt_ref[e] * PICK, body, 0)

    issue(0)
    for e in range(n_emb):
        buf = e % 2
        if e + 1 < n_emb:
            issue(e + 1)

        def drain(s, _):
            pltpu.make_async_copy(
                tables.at[:, pl.ds(0, 8 * PICK), :], blocks.at[buf, :, pl.ds(0, 8 * PICK), :], sem.at[buf]).wait()
            return 0

        lax.fori_loop(0, cnt_ref[e], drain, 0)

        def take(b, _):
            r = pl.multiple_of(b * PICK, PICK)
            pick = pick_ref[pl.ds(pl.multiple_of(e * cap + r, PICK), PICK), :]
            for l in range(n_layers):
                rows = blocks[buf, l, pl.ds(pl.multiple_of(r * 8, 8 * PICK), 8 * PICK), :]
                out_ref[e, pl.ds(l * cap + r, PICK), :] = jnp.dot(pick, rows, preferred_element_type=F32).astype(BF)
            return 0

        lax.fori_loop(0, cnt_ref[e], take, 0)

        def rest(b, _):
            r = pl.multiple_of(b * PICK, PICK)
            for l in range(n_layers):
                out_ref[e, pl.ds(l * cap + r, PICK), :] = jnp.zeros((PICK, out_ref.shape[2]), BF)
            return 0

        lax.fori_loop(cnt_ref[e], cap // PICK, rest, 0)


def serve_rows(tables, counts, rows, pick, cap):
    n_layers, _, width = tables.shape
    n_emb = counts.shape[0]
    smem = pl.BlockSpec(memory_space=pltpu.SMEM)
    vmem = pl.BlockSpec(memory_space=pltpu.VMEM)
    return pl.pallas_call(
        functools.partial(serve_kernel, n_layers, cap),
        out_shape=jax.ShapeDtypeStruct((n_emb, n_layers * cap, width), BF),
        in_specs=[smem, smem, vmem, pl.BlockSpec(memory_space=pltpu.HBM)],
        out_specs=vmem,
        scratch_shapes=[
            pltpu.VMEM((2, n_layers, cap * 8, width), BF),
            pltpu.SemaphoreType.DMA((2,)),
        ],
        compiler_params=pltpu.CompilerParams(vmem_limit_bytes=48 << 20),
        cost_estimate=pl.CostEstimate(flops=20_000_000_000, bytes_accessed=30_000_000, transcendentals=0),
        name="serve_rows",
    )(counts, rows, pick, tables)


N_SRC = 16
MAX_ROWS = 17 * BLK


def pull_runs(meta_ref, src, col, dst, sem):
    src_rows = src.shape[0] // N_SRC
    width = dst.shape[1]

    def run(k, _):
        lo, off = meta_ref[k], meta_ref[2 * N_SRC + k]

        def chunk(c, _):
            a = pl.multiple_of(k * src_rows + lo + c * CHUNK, CHUNK)
            b = pl.multiple_of((off + c) * CHUNK, CHUNK)
            pltpu.make_async_copy(src.at[pl.ds(a, CHUNK), col:col + width], dst.at[pl.ds(b, CHUNK), :], sem).start()
            return 0

        return lax.fori_loop(0, meta_ref[N_SRC + k], chunk, 0)

    lax.fori_loop(0, N_SRC, run, 0)


def drain_runs(meta_ref, src, col, dst, sem):
    width = dst.shape[1]

    def one(c, _):
        pltpu.make_async_copy(src.at[pl.ds(0, CHUNK), col:col + width], dst.at[pl.ds(0, CHUNK), :], sem).wait()
        return 0

    lax.fori_loop(0, meta_ref[3 * N_SRC], one, 0)


def n_blocks(meta_ref):
    return lax.div(meta_ref[3 * N_SRC] * CHUNK + BLK - 1, BLK)


def gate_kernel(layer, col, meta_ref, u_hbm, w_ref, out, uc, stage, sem_u, sem_o):
    pull_runs(meta_ref, u_hbm, col, uc, sem_u)
    drain_runs(meta_ref, u_hbm, col, uc, sem_u)
    total = n_blocks(meta_ref)

    def out_copy(b):
        buf = lax.rem(b, 2)
        r = pl.multiple_of(b * BLK, BLK)
        return pltpu.make_async_copy(stage.at[buf], out.at[pl.ds(r, BLK), :], sem_o.at[buf])

    def block(b, _):
        @pl.when(b >= 2)
        def _():
            out_copy(b - 2).wait()

        u = uc[pl.ds(pl.multiple_of(b * BLK, BLK), BLK), :]
        for n in range(4):
            pre = jnp.dot(u, w_ref[layer, :, n * 256:(n + 1) * 256], preferred_element_type=F32)
            stage[lax.rem(b, 2), :, n * 256:(n + 1) * 256] = jax.nn.gelu(pre)
        out_copy(b).start()
        return 0

    lax.fori_loop(0, total, block, 0)
    lax.fori_loop(jnp.maximum(total - 2, 0), total, lambda b, c: (out_copy(b).wait(), c)[1], 0)


def owner_gate(layer, meta, u_all, col, w_gate):
    smem = pl.BlockSpec(memory_space=pltpu.SMEM)
    hbm = pl.BlockSpec(memory_space=pltpu.HBM)
    width = w_gate.shape[2]
    return pl.pallas_call(
        functools.partial(gate_kernel, layer, col),
        out_shape=pltpu.HBM((MAX_ROWS, width), F32),
        in_specs=[smem, hbm, pl.BlockSpec(memory_space=pltpu.VMEM)],
        out_specs=hbm,
        scratch_shapes=[
            pltpu.VMEM((MAX_ROWS, width), BF),
            pltpu.VMEM((2, BLK, width), F32),
            pltpu.SemaphoreType.DMA,
            pltpu.SemaphoreType.DMA((2,)),
        ],
        compiler_params=pltpu.CompilerParams(vmem_limit_bytes=28 << 20),
        cost_estimate=pl.CostEstimate(flops=10_000_000_000, bytes_accessed=30_000_000, transcendentals=0),
    )(meta, u_all, w_gate)


UNROLL = 8


def owner_kernel(layer, col, meta_ref, tile_ref, addr_ref, g_hbm, d_hbm, *rest):
    out, dc, gbuf, prod, acc, sem_d, sem_g, sem_o = rest[-8:]
    n_tiles = tile_ref.shape[0] - 1
    total = n_blocks(meta_ref)

    def g_copy(b):
        buf = lax.rem(b, 2)
        return pltpu.make_async_copy(g_hbm.at[pl.ds(pl.multiple_of(b * BLK, BLK), BLK), :], gbuf.at[buf], sem_g.at[buf])

    g_copy(0).start()
    pull_runs(meta_ref, d_hbm, col, dc, sem_d)
    drain_runs(meta_ref, d_hbm, col, dc, sem_d)

    def block(b, _):
        g_copy(b).wait()

        @pl.when(b + 1 < total)
        def _():
            g_copy(b + 1).start()

        buf = lax.rem(b, 2)
        for t in range(BLK // 16):
            d = dc[pl.ds(pl.multiple_of(b * BLK + t * 16, 16), 16), :].astype(F32)
            val = gbuf[buf, t * 16:(t + 1) * 16, :] * d
            for h in range(2):
                for j in range(8):
                    prod[pl.ds(pl.multiple_of(b * (BLK * 8) + (2 * t + h) * 64 + j * 8, 8), 8), :] = (
                        val[h * 8:(h + 1) * 8, j * 128:(j + 1) * 128])
        return 0

    lax.fori_loop(0, total, block, 0)

    def out_copy(t, buf):
        return pltpu.make_async_copy(
            acc.at[buf].reshape(TILE_ROWS // 8, 8, 8, 128),
            out.at[layer, pl.ds(t * (TILE_ROWS // 8), TILE_ROWS // 8)], sem_o.at[buf])

    def tile(t, _):
        buf = lax.rem(t, 2)

        @pl.when(t >= 2)
        def _():
            out_copy(t - 2, buf).wait()

        def clear(i, _):
            acc[buf, pl.ds(pl.multiple_of(i * 512, 512), 512), :] = jnp.zeros((512, 128), F32)
            return 0

        lax.fori_loop(0, TILE_ROWS * 8 // 512, clear, 0)
        first, last = tile_ref[t], tile_ref[t + 1]

        def one(i, run):
            word = addr_ref[i]
            pa = lax.bitwise_and(word, 0xFFFF)
            ra = lax.bitwise_and(lax.shift_right_logical(word, 16), 0x1FFF)
            fresh = word >= (1 << 29)
            run = jnp.where(fresh, 0.0, run) + prod[pl.ds(pa, 8, stride=8), :]
            acc[buf, pl.ds(ra, 8, stride=8), :] = run
            return run

        def many(i, run):
            for u in range(UNROLL):
                run = one(first + i * UNROLL + u, run)
            return run

        groups = lax.div(last - first, UNROLL)
        run = lax.fori_loop(0, groups, many, jnp.zeros((8, 128), F32))
        lax.fori_loop(first + groups * UNROLL, last, one, run)
        out_copy(t, buf).start()
        return 0

    lax.fori_loop(0, n_tiles, tile, 0)
    out_copy(n_tiles - 2, n_tiles % 2).wait()
    out_copy(n_tiles - 1, (n_tiles - 1) % 2).wait()


def owner_grad(layer, out_prev, out_shape, meta, tiles, addrs, g_rows, d_all, col):
    smem = pl.BlockSpec(memory_space=pltpu.SMEM)
    hbm = pl.BlockSpec(memory_space=pltpu.HBM)
    width = g_rows.shape[1]
    args = [meta, tiles, addrs, g_rows, d_all]
    specs = [smem, smem, smem, hbm, hbm]
    aliases = {}
    if out_prev is not None:
        args.append(out_prev)
        specs.append(hbm)
        aliases = {5: 0}
    return pl.pallas_call(
        functools.partial(owner_kernel, layer, col),
        out_shape=jax.ShapeDtypeStruct(out_shape, F32),
        in_specs=specs,
        out_specs=hbm,
        scratch_shapes=[
            pltpu.VMEM((MAX_ROWS, width), BF),
            pltpu.VMEM((2, BLK, width), F32),
            pltpu.VMEM((MAX_ROWS * 8, 128), F32),
            pltpu.VMEM((2, TILE_ROWS * 8, 128), F32),
            pltpu.SemaphoreType.DMA,
            pltpu.SemaphoreType.DMA((2,)),
            pltpu.SemaphoreType.DMA((2,)),
        ],
        input_output_aliases=aliases,
        compiler_params=pltpu.CompilerParams(vmem_limit_bytes=48 << 20),
        cost_estimate=pl.CostEstimate(flops=40_000_000_000, bytes_accessed=100_000_000, transcendentals=0),
    )(*args)


def solution(mesh):
    n_emb = mesh.shape['emb']
    n_dev = n_emb * mesh.shape['dp']
    tok_spec = P(('dp', 'emb'))
    act_spec = P(('dp', 'emb'), None)
    table_spec = P(None, 'emb', None)
    full_spec = P(None, None, None)
    everyone = ('dp', 'emb')

    def device_body(tok_ids, resid_in, cot_out, tables, w_up, w_down, w_gate, w_proj):
        n_layers, range_rows, width = tables.shape
        n_tok = tok_ids.shape[0]
        cap = min(2 * n_tok // n_emb, 3 * n_tok // 4)
        i_dp, i_emb = lax.axis_index('dp'), lax.axis_index('emb')
        last = n_layers - 1

        def gather(rows):
            return lax.all_gather(rows, everyone, axis=0, tiled=True)

        pos = jnp.arange(n_tok, dtype=jnp.int32)
        before = (tok_ids[None, :] < tok_ids[:, None]) | ((tok_ids[None, :] == tok_ids[:, None]) & (pos[None, :] < pos[:, None]))
        rank = jnp.sum(before.astype(jnp.int32), axis=1)
        perm_mask = rank[None, :] == pos[:, None]
        perm = perm_mask.astype(BF)
        x = jnp.dot(perm, resid_in, preferred_element_type=F32).astype(BF)
        cot = jnp.dot(perm, cot_out, preferred_element_type=F32).astype(BF)
        normed = rms_norm(x.astype(F32)).astype(BF)
        d_mixed = mixed_cot(cot, w_proj[last])
        first_set = jnp.concatenate([normed, d_mixed], axis=1)
        set_a = gather(first_set)

        ids = jnp.sum(jnp.where(perm_mask, tok_ids[None, :], 0), axis=1)
        ids, _ = lax.optimization_barrier((ids, first_set))
        ids_all = lax.all_gather(ids, everyone, axis=0, tiled=True)
        ids_2d = ids_all.reshape(n_dev, n_tok)
        base = i_emb * range_rows

        mine = lax.dynamic_slice(ids_2d, (i_dp * n_emb, 0), (n_emb, n_tok))
        peer_lo = jnp.sum((mine < base).astype(jnp.int32), axis=1)
        peer_hi = jnp.sum((mine < base + range_rows).astype(jnp.int32), axis=1)
        count = peer_hi - peer_lo
        padded = jnp.pad(mine - base, ((0, 0), (0, cap)))
        asked = jax.vmap(lambda r, s: lax.dynamic_slice(r, (s,), (cap,)))(padded, peer_lo)
        slot_pos = jnp.arange(cap, dtype=jnp.int32)
        valid = slot_pos[None, :] < count[:, None]
        asked = jnp.where(valid, asked, 0)
        pick_col = jnp.where(valid, (slot_pos[None, :] % PICK) * 8 + asked % 8, -1).reshape(-1, 1)
        pick8 = (pick_col == jnp.arange(8 * PICK, dtype=jnp.int32)[None, :]).astype(BF)
        served = serve_rows(tables, (count + PICK - 1) // PICK, (asked // 8 * 8).reshape(-1), pick8, cap)
        returned = lax.all_to_all(served, 'emb', 0, 0, tiled=True)
        returned = returned.reshape(n_emb, n_layers, cap, -1)
        owner = ids // range_rows
        first = jnp.sum((owner[None, :] < owner[:, None]).astype(jnp.int32), axis=1)
        slot = owner * cap + pos - first
        pick = (slot[:, None] == jnp.arange(n_emb * cap, dtype=jnp.int32)[None, :]).astype(BF)

        saved, us = [], [normed]
        for l in range(n_layers):
            rows_l = returned[:, l].reshape(n_emb * cap, -1)
            fetched = jnp.dot(pick, rows_l, preferred_element_type=F32).astype(BF)
            x, kept = layer_forward(x, normed, fetched, w_up[l], w_down[l], w_gate[l], w_proj[l])
            saved.append(kept)
            if l < last:
                normed = rms_norm(x.astype(F32)).astype(BF)
                us.append(normed)
        set_b = gather(jnp.concatenate(us[1:], axis=1))
        resid_out = lax.dot_general(perm, x, (((0,), (0,)), ((), ())), preferred_element_type=F32).astype(BF)
        d_sets = [None] * n_layers
        for l in range(last, 0, -1):
            cot = layer_backward(cot, d_mixed, saved[l], w_up[l], w_down[l], w_gate[l])
            d_mixed = mixed_cot(cot, w_proj[l - 1])
            d_sets[l - 1] = (gather(d_mixed), 0)

        n_tiles = range_rows // TILE_ROWS
        lo = jnp.sum((ids_2d < base).astype(jnp.int32), axis=1)
        hi = jnp.sum((ids_2d < base + range_rows).astype(jnp.int32), axis=1)
        lo16 = (lo // CHUNK) * CHUNK
        n_ch = (hi - lo16 + CHUNK - 1) // CHUNK
        tri = jnp.arange(n_dev)[None, :] < jnp.arange(n_dev)[:, None]
        off = jnp.sum(jnp.where(tri, n_ch[None, :], 0), axis=1)
        meta = jnp.concatenate([lo16, n_ch, off, jnp.sum(n_ch)[None]]).astype(jnp.int32)
        place = (off * CHUNK - lo16)[:, None] + pos[None, :]
        local = ids_2d - base
        owned = (local >= 0) & (local < range_rows)
        key = jnp.where(owned, local * (1 << 13) + place, jnp.iinfo(jnp.int32).max)
        key = lax.sort(key.reshape(-1), is_stable=False)[:n_emb * n_dev * cap // 4]
        p, r = key & ((1 << 13) - 1), key >> 13
        fresh = jnp.concatenate([jnp.ones((1,), jnp.bool_), r[1:] != r[:-1]])
        in_tile = r % TILE_ROWS
        addrs = ((p // 8) * 64 + p % 8) | (((in_tile // 8) * 64 + in_tile % 8) << 16) | (fresh.astype(jnp.int32) << 29)
        edges = jnp.arange(n_tiles + 1, dtype=jnp.int32) * TILE_ROWS
        tiles = jnp.sum((r[None, :] < edges[:, None]).astype(jnp.int32), axis=1)

        set_a, _ = lax.optimization_barrier((set_a, d_mixed))
        u_sets = [(set_a, 0)] + [(set_b, i * width) for i in range(n_layers - 1)]
        d_sets[last] = (set_a, width)
        grads = None
        out_shape = (n_layers, range_rows // 8, width // 128, 8, 128)
        gates = [owner_gate(l, meta, *u_sets[l], w_gate) for l in range(n_layers)]
        for l in range(last, -1, -1):
            grads = owner_grad(l, grads, out_shape, meta, tiles, addrs, gates[l], *d_sets[l])
        d_tables = grads.transpose(0, 1, 3, 2, 4).reshape(n_layers, range_rows, width)
        return resid_out, d_tables

    return jax.shard_map(device_body, mesh=mesh, in_specs=(tok_spec, act_spec, act_spec, table_spec, full_spec, full_spec, full_spec, full_spec), out_specs=(act_spec, table_spec), check_vma=False)
```

time: 721 us -> 611 us (0.85)
  Pallas kernels: 291 us -> 224 us
  waiting for transfers between devices: 212 us -> 157 us
  other arithmetic: 7.73 us -> 16.2 us
    all_gather x6 -> x4, waiting for transfers between devices: 147 us -> 33 us  [gather(): return lax.all_gather(rows, everyone, axis=0, tiled=True)]
    all_to_all x1, waiting for transfers between devices: 64.1 us -> 124 us  [device_body(): returned = lax.all_to_all(served, 'emb', 0, 0, tiled=True)]
    pallas_call x1, Pallas kernels: 72.3 us -> 23.8 us  [serve_rows(): pl.pallas_call(functools.partial(serve_kernel, n_layers, cap), out_shape=...]
    pallas_call x3 -> x6, Pallas kernels: 219 us -> 200 us  [the longest x3 148 us: owner_grad(): pl.pallas_call(functools.partial(owner_kernel, layer, col), out_shape=jax...]
    gather x0 -> x16, local copies, waits for them, and re-layouts: none -> 8.05 us
  transfers between devices with their start and end apart: 7 -> 5, of which waited for: 4 -> 3; matrix products, arithmetic and copies ran while one was open for 23% -> 28% of each run, Pallas kernels for 31% -> 29%
where the time goes in v2:
time: 611 us; the launch traced here: 603 us
  Pallas kernels  224 us (37%)
  waiting for transfers between devices  157 us (26%)
  matrix products  148 us (24%)
  local copies, waits for them, and re-layouts  23.2 us (4%)
  other arithmetic  16.2 us (3%)
  blocking collectives  14.5 us (2%)
  between operations  14.5 us (2%)
    pallas_call x3, Pallas kernels, owner_grad(): pl.pallas_call(functools.partial(owner_kernel, layer, col), out_shape=jax...  148 us
    all_to_all x1, waiting for transfers between devices, device_body(): returned = lax.all_to_all(served, 'emb', 0, 0, tiled=True)  124 us
    pallas_call x3, Pallas kernels, owner_gate(): pl.pallas_call(functools.partial(gate_kernel, layer, col), out_shape=pltp...  52.1 us
    all_gather x4, waiting for transfers between devices, gather(): return lax.all_gather(rows, everyone, axis=0, tiled=True)  33 us
    dot_general x2, matrix products, layer_backward(): jnp.einsum('tf,df->td', d_up_pre.astype(BF), w_up, preferred_element_type...  32.4 us
    dot_general x2, matrix products, layer_forward(): mlp_out = jnp.dot(hidden, w_down, preferred_element_type=F32)  28.3 us
    pallas_call x1, Pallas kernels, serve_rows(): pl.pallas_call(functools.partial(serve_kernel, n_layers, cap), out_shape=...  23.8 us
    dot_general x2, matrix products, layer_forward(): up_pre = jnp.dot(normed, w_up, preferred_element_type=F32)  17.6 us
  transfers between devices with their start and end apart: 5, of which 3 were waited for; matrix products, arithmetic and copies ran while one was open for 28% of the time, Pallas kernels for 29%

profile of v2, /device:TPU:0, one launch (start us, length us, event | category | flops | bytes accessed | tf_op | source)
XLA Modules:
  0.0 603.5 jit_solution(18243046808882650848)
XLA Ops:
  7.2 1.1 convert_reduce_fusion.1
  8.3 1.9 convolution_convert_fusion.1
  10.3 0.8 fusion.106
  11.1 3.3 fusion.178
  15.4 1.5 pad_maximum_fusion
  17.8 14.5 %all-gather = s32[16,1,512]{2,1,0:T(1,128)S(1)} all-gather(s32[1,1,512]{2,1,0:T(1,128)S(1)} %bitcast.161), channel_id=1, replica_groups=mesh['dp'=4,'emb'=4] {'dp','emb'}, dimensions={0}, use_global_device_ids=true | all-gather | bytes 34816 | tf_op jit(solution)/shard_map/all_gather | solution.py:347
  33.0 8.1 %while.1 = (s32[]{:T(128)}, s32[4,768]{1,0:T(4,128)S(1)}, s32[4,2]{0,1:T(2,128)S(1)}, s32[4,256]{1,0:T(4,128)S(1)}, s32[]{:T(128)}, /*index=5*/s32[]{:T(128)}) while((s32[]{:T(128)}, s32[4,768]{1,0:T(4,128)S(1)}, s32[4,2]{0,1:T(2,128)S(1)}, s32[4,256]{1,0:T(4,128)S(1)}, s32[]{:T(128)}, /*index=5*/s32[]{:T(128)}) %tuple.42), condition=%wide.while_cond, body=%wide.while_body.sunk | while | flops 2 | bytes 4217 | solution.py:356
  33.7 1.3 dynamic-slice.15
  35.7 1.3 dynamic-slice.15
  37.7 1.3 dynamic-slice.15
  39.8 1.3 dynamic-slice.15
  41.4 23.8 %serve_rows.1 = bf16[4,768,1024]{2,1,0:T(8,128)(2,1)} custom-call(s32[4]{0:T(128)S(1)} %get-tuple-element.29.cnt_ref, s32[1024]{0:T(1024)S(1)} %get-tuple-element.39.row_ref, bf16[1024,256]{1,0:T(8,128)(2,1)S(1)} %fusion.249.pick_ref, bf16[3,16384,1024]{2,1,0:T(8,128)(2,1)} %tables.1), custom_call_target="tpu_custom_call" | custom-call | flops 20000000000 | bytes 30000000 | tf_op jit(solution)/shard_map/serve_rows/pallas_call | solution.py:107
  65.1 5.2 all-to-all-start
  70.9 4.2 fusion.153
  75.1 124.2 %all-to-all-done = bf16[4,768,1024]{2,1,0:T(8,128)(2,1)} async-done(((bf16[4,768,1024]{2,1,0:T(8,128)(2,1)}), bf16[4,768,1024]{2,1,0:T(8,128)(2,1)}, u32[]{:S(2)}, u32[]{:S(2)}) %all-to-all-start) | async-done | bytes 6291488 | tf_op jit(solution)/shard_map/all_to_all | solution.py:363
  199.3 5.8 fusion.342
  205.1 6.7 %fusion.147 = f32[512,1024]{1,0:T(8,128)} fusion(bf16[3,1024,1024]{2,1,0:T(8,128)(2,1)} %param.15, f32[512,1024]{1,0:T(8,128)} %fusion.153, bf16[1024,1024]{1,0:T(8,128)(2,1)} %bitcast.158, s32[512]{0:T(512)S(1)} %add_subtract_fusion), kind=kOutput, calls=%fused_computation.168 | convolution fusion | flops 2154299392 | bytes 8390656 | tf_op jit(solution)/shard_map/dot_general | solution.py:32
  211.8 16.5 %fusion.123 = (f32[512]{0:T(512)S(1)}, bf16[512,1024]{1,0:T(8,128)(2,1)}) fusion(f32[512,1024]{1,0:T(8,128)} %fusion.147, bf16[3,4096,1024]{2,1,0:T(8,128)(2,1)} %param.13, bf16[3,1024,4096]{2,1,0:T(8,128)(2,1)} %param.12, bf16[512,1024]{1,0:T(8,128)(2,1)S(1)} %copy-done.7, f32[512]{0:T(512)S(1)} %add_rsqrt_fusion), kind=kOutput, calls=%fused_computation.142 | convolution fusion | flops 8614051840 | bytes 22024192 | tf_op jit(solution)/shard_map/dot_general | solution.py:28
  228.3 1.5 fusion.124
  229.8 1.5 fusion.176
  231.3 3.2 fusion.143
  234.6 1.4 copy-done.17
  235.9 3.1 fusion.139
  239.1 7.0 %fusion.42 = f32[512,4096]{1,0:T(8,128)S(1)} fusion(bf16[512,1024]{1,0:T(8,128)(2,1)S(1)} %fusion.124, bf16[3,1024,4096]{2,1,0:T(8,128)(2,1)} %param.12), kind=kOutput, calls=%fused_computation.52 | convolution fusion | flops 4294967296 | bytes 17825792 | tf_op jit(solution)/shard_map/dot_general | solution.py:26
  246.1 11.9 %fusion.128 = (f32[512]{0:T(512)S(1)}, bf16[512,1024]{1,0:T(8,128)(2,1)S(1)}) fusion(f32[512,1024]{1,0:T(8,128)S(1)} %fusion.139, bf16[3,4096,1024]{2,1,0:T(8,128)(2,1)} %param.13, f32[512,4096]{1,0:T(8,128)S(1)} %fusion.42, bf16[512,1024]{1,0:T(8,128)(2,1)S(1)} %copy-done.8), kind=kOutput, calls=%fused_computation.147 | convolution fusion | flops 4317511168 | bytes 20973568 | tf_op jit(solution)/shard_map/dot_general | solution.py:28
  258.2 1.5 pad_maximum_fusion.1
  260.3 3.9 fusion.177
  264.1 4.6 fusion.135
  268.7 10.6 %fusion.34 = f32[512,4096]{1,0:T(8,128)} fusion(bf16[512,1024]{1,0:T(8,128)(2,1)S(1)} %fusion.129, bf16[3,1024,4096]{2,1,0:T(8,128)(2,1)} %param.12), kind=kOutput, calls=%fused_computation.44 | convolution fusion | flops 4294967296 | bytes 17825792 | tf_op jit(solution)/shard_map/dot_general | solution.py:26
  279.3 16.6 %fusion.200 = bf16[512,1024]{1,0:T(8,128)(2,1)} fusion(bf16[3,1024,4096]{2,1,0:T(8,128)(2,1)} %param.12, f32[512,4096]{1,0:T(8,128)} %fusion.34, bf16[512,1024]{1,0:T(8,128)(2,1)S(1)} %copy-done.5, bf16[3,4096,1024]{2,1,0:T(8,128)(2,1)} %param.13), kind=kOutput, calls=%fused_computation.203 | convolution fusion | flops 8636596224 | bytes 27262976 | tf_op jit(solution)/shard_map/tf,df->td/dot_general | solution.py:47
  295.9 5.4 fusion.132
  302.0 3.9 fusion.187
  305.9 15.7 %fusion.193 = bf16[512,1024]{1,0:T(8,128)(2,1)} fusion(bf16[3,1024,4096]{2,1,0:T(8,128)(2,1)} %param.12, f32[512,4096]{1,0:T(8,128)} %copy-done.18, bf16[512,1024]{1,0:T(8,128)(2,1)S(1)} %fusion.120, bf16[3,4096,1024]{2,1,0:T(8,128)(2,1)} %param.13), kind=kOutput, calls=%fused_computation.202 | convolution fusion | flops 8636596224 | bytes 27262976 | tf_op jit(solution)/shard_map/tf,df->td/dot_general | solution.py:47
  321.6 5.8 fusion.127
  327.4 4.6 fusion.181
  333.8 5.6 sort.7
  340.5 4.1 fusion.149
  344.6 12.8 %convolution_convert_fusion = bf16[512,1024]{1,0:T(8,128)(2,1)} fusion(f32[512,1024]{1,0:T(8,128)S(1)} %fusion.149, bf16[512,1024]{1,0:T(8,128)(2,1)S(1)} %get-tuple-element.45, bf16[3,4096,1024]{2,1,0:T(8,128)(2,1)} %param.13, f32[512,4096]{1,0:T(8,128)} %fusion.34, s32[512]{0:T(512)S(1)} %copy-done.16), kind=kOutput, calls=%fused_computation.199 | convolution fusion | flops 4853596160 | bytes 20973568 | tf_op jit(solution)/shard_map/dot_general | solution.py:380
  357.4 3.4 copy-done.2
  360.8 17.4 %shard_map.95.g_hbm = f32[4352,1024]{1,0:T(8,128)} custom-call(s32[49]{0:T(128)S(1)} %pad_add_fusion.1.meta_ref, bf16[8192,2048]{1,0:T(8,128)(2,1)} %all-gather.6.cloned.1.call-done.u_hbm.d_hbm, bf16[3,1024,1024]{2,1,0:T(8,128)(2,1)S(1)} %copy-done.2), custom_call_target="tpu_custom_call" | custom-call | flops 10000000000 | bytes 30000000 | tf_op jit(solution)/shard_map/pallas_call | solution.py:188
  378.2 13.1 %all-gather.10.cloned.1.call-done.u_hbm = bf16[8192,2048]{1,0:T(8,128)(2,1)} async-done(((bf16[512,2048]{1,0:T(8,128)(2,1)}), bf16[8192,2048]{1,0:T(8,128)(2,1)}) %all-gather.10.cloned.1.call-update) | async-done | bytes 33554448 | tf_op jit(solution)/shard_map/all_gather | solution.py:331
  391.2 2.8 copy-done.3
  394.0 17.3 %shard_map.97.g_hbm = f32[4352,1024]{1,0:T(8,128)} custom-call(s32[49]{0:T(128)S(1)} %pad_add_fusion.1.meta_ref, bf16[8192,2048]{1,0:T(8,128)(2,1)} %all-gather.10.cloned.1.call-done.u_hbm, bf16[3,1024,1024]{2,1,0:T(8,128)(2,1)S(1)} %copy-done.3), custom_call_target="tpu_custom_call" | custom-call | flops 10000000000 | bytes 30000000 | tf_op jit(solution)/shard_map/pallas_call | solution.py:188
  411.3 17.5 %shard_map.96.g_hbm = f32[4352,1024]{1,0:T(8,128)} custom-call(s32[49]{0:T(128)S(1)} %pad_add_fusion.1.meta_ref, bf16[8192,2048]{1,0:T(8,128)(2,1)} %all-gather.10.cloned.1.call-done.u_hbm, bf16[3,1024,1024]{2,1,0:T(8,128)(2,1)S(1)} %copy-done.3), custom_call_target="tpu_custom_call" | custom-call | flops 10000000000 | bytes 30000000 | tf_op jit(solution)/shard_map/pallas_call | solution.py:188
  428.8 49.1 %shard_map.98.rest_0_ = f32[3,2048,8,8,128]{4,3,2,1,0:T(8,128)} custom-call(s32[49]{0:T(128)S(1)} %pad_add_fusion.1.meta_ref, s32[17]{0:T(128)S(1)} %convert_reduce_fusion.2.tile_ref, s32[4096]{0:T(1024)S(1)} %fusion.258.addr_ref, f32[4352,1024]{1,0:T(8,128)} %shard_map.97.g_hbm, bf16[8192,2048]{1,0:T(8,128)(2,1)} %all-gather.6.cloned.1.call-done.u_hbm.d_hbm), custom_call_target="tpu_custom_call" | custom-call | flops 40000000000 | bytes 100000000 | tf_op jit(solution)/shard_map/pallas_call | solution.py:294
  477.9 50.9 %shard_map.99.rest_0_ = f32[3,2048,8,8,128]{4,3,2,1,0:T(8,128)} custom-call(s32[49]{0:T(128)S(1)} %pad_add_fusion.1.meta_ref, s32[17]{0:T(128)S(1)} %convert_reduce_fusion.2.tile_ref, s32[4096]{0:T(1024)S(1)} %fusion.258.addr_ref, f32[4352,1024]{1,0:T(8,128)} %shard_map.96.g_hbm, ...), custom_call_target="tpu_custom_call", output_to_operand_aliasing={{}: (5, {})} | custom-call | flops 40000000000 | bytes 100000000 | tf_op jit(solution)/shard_map/pallas_call | solution.py:294
  528.8 19.9 %all-gather.8.cloned.1.call-done.d_hbm = bf16[8192,1024]{1,0:T(8,128)(2,1)} async-done(((bf16[512,1024]{1,0:T(8,128)(2,1)}), bf16[8192,1024]{1,0:T(8,128)(2,1)}) %all-gather.8.cloned.1.call-update) | async-done | bytes 16777232 | tf_op jit(solution)/shard_map/all_gather | solution.py:331
  548.7 48.0 %shard_map.100 = f32[3,2048,8,8,128]{4,3,2,1,0:T(8,128)} custom-call(s32[49]{0:T(128)S(1)} %pad_add_fusion.1.meta_ref, s32[17]{0:T(128)S(1)} %convert_reduce_fusion.2.tile_ref, s32[4096]{0:T(1024)S(1)} %fusion.258.addr_ref, f32[4352,1024]{1,0:T(8,128)} %shard_map.95.g_hbm, ...), custom_call_target="tpu_custom_call", output_to_operand_aliasing={{}: (5, {})} | custom-call | flops 40000000000 | bytes 100000000 | tf_op jit(solution)/shard_map/pallas_call | solution.py:294
  (102 shorter events, 10.4 us)
Async XLA Ops:
  7.2 3.1 copy-start
  7.2 350.2 %all-gather.6.cloned.1.call-start = ((), (), s32[]{:S(2)}) async-start(), calls=%async_computation.1 | async-start | bytes 35651584 | tf_op jit(solution)/shard_map/all_gather | solution.py:331
  8.3 8.7 %copy-start.15 = (s32[512]{0:T(512)}, s32[512]{0:T(512)S(1)}, u32[]{:S(2)}) copy-start(s32[512]{0:T(512)S(1)} %convert_reduce_fusion.1) | copy-start | bytes 6148
  10.3 4.1 copy-start.4
  11.1 59.8 %copy-start.6 = (bf16[512,1024]{1,0:T(8,128)(2,1)}, bf16[512,1024]{1,0:T(8,128)(2,1)S(1)}, u32[]{:S(2)}) copy-start(bf16[512,1024]{1,0:T(8,128)(2,1)S(1)} %get-tuple-element.41) | copy-start | bytes 3145732
  14.4 1.0 copy-start.10
  16.9 0.7 copy-start.14
  32.3 0.6 copy-start.12
  65.1 134.2 %all-to-all-start = ((bf16[4,768,1024]{2,1,0:T(8,128)(2,1)}), bf16[4,768,1024]{2,1,0:T(8,128)(2,1)}, u32[]{:S(2)}, u32[]{:S(2)}) async-start(bf16[4,768,1024]{2,1,0:T(8,128)(2,1)} %serve_rows.1), calls=%async_computation | async-start | bytes 12582912 | tf_op jit(solution)/shard_map/all_to_all | solution.py:363
  70.4 320.8 %all-gather.10.cloned.1.call-start = ((), (), s32[]{:S(2)}) async-start(), calls=%async_computation.3 | async-start | bytes 35651584 | tf_op jit(solution)/shard_map/all_gather | solution.py:331
  205.1 6.7 %copy-start.7 = (bf16[512,1024]{1,0:T(8,128)(2,1)S(1)}, bf16[512,1024]{1,0:T(8,128)(2,1)}, u32[]{:S(2)}) copy-start(bf16[512,1024]{1,0:T(8,128)(2,1)} %copy-done.6) | copy-start | bytes 3145732
  231.3 3.2 copy-start.19
  234.5 1.4 copy-start.17
  239.1 7.0 %copy-start.8 = (bf16[512,1024]{1,0:T(8,128)(2,1)S(1)}, bf16[512,1024]{1,0:T(8,128)(2,1)}, u32[]{:S(2)}) copy-start(bf16[512,1024]{1,0:T(8,128)(2,1)} %get-tuple-element.43) | copy-start | bytes 3145732
  246.1 11.9 %copy-start.18 = (f32[512,4096]{1,0:T(8,128)}, f32[512,4096]{1,0:T(8,128)S(1)}, u32[]{:S(2)}) copy-start(f32[512,4096]{1,0:T(8,128)S(1)} %fusion.42) | copy-start | bytes 25165828
  259.8 218.1 %all-gather.12.cloned.1.call-start = ((), (), s32[]{:S(2)}) async-start(), calls=%async_computation.4 | async-start | bytes 17825792 | tf_op jit(solution)/shard_map/all_gather | solution.py:331
  268.7 10.6 %copy-start.5 = (bf16[512,1024]{1,0:T(8,128)(2,1)S(1)}, bf16[512,1024]{1,0:T(8,128)(2,1)}, u32[]{:S(2)}) copy-start(bf16[512,1024]{1,0:T(8,128)(2,1)} %copy-done.4) | copy-start | bytes 3145732
  279.3 16.6 %copy-start.11 = (bf16[512,1024]{1,0:T(8,128)(2,1)S(1)}, bf16[512,1024]{1,0:T(8,128)(2,1)}, u32[]{:S(2)}) copy-start(bf16[512,1024]{1,0:T(8,128)(2,1)} %copy-done.10) | copy-start | bytes 3145732
  305.9 15.8 %copy-start.9 = (bf16[512,1024]{1,0:T(8,128)(2,1)S(1)}, bf16[512,1024]{1,0:T(8,128)(2,1)}, u32[]{:S(2)}) copy-start(bf16[512,1024]{1,0:T(8,128)(2,1)} %get-tuple-element.43) | copy-start | bytes 3145732
  305.9 242.8 %all-gather.8.cloned.1.call-start = ((), (), s32[]{:S(2)}) async-start(), calls=%async_computation.2 | async-start | bytes 17825792 | tf_op jit(solution)/shard_map/all_gather | solution.py:331
  327.4 4.7 copy-start.13
  340.5 4.1 copy-start.16
  357.4 3.4 copy-start.2
  391.2 2.8 copy-start.3
  548.7 48.1 %copy-start.1 = (bf16[512,1024]{1,0:T(8,128)(2,1)S(1)}, bf16[512,1024]{1,0:T(8,128)(2,1)}, u32[]{:S(2)}) copy-start(bf16[512,1024]{1,0:T(8,128)(2,1)} %param.9) | copy-start | bytes 3145732
Sparse Core Ops, SparseCore 0:
  17.1 194.7 all-gather.5
  259.9 131.2 all-gather.9
  393.5 76.5 all-gather.11
  472.2 76.4 all-gather.7

commit v3 on v2

--- a/solution.py
+++ b/solution.py
@@ -21,45 +21,276 @@
     return x_f32 * lax.rsqrt(jnp.mean(x_f32 * x_f32, axis=-1, keepdims=True) + NORM_EPS)
 
 
-def layer_forward(x, normed, fetched, w_up, w_down, w_gate, w_proj):
-    x_f32 = x.astype(F32)
-    up_pre = jnp.dot(normed, w_up, preferred_element_type=F32)
-    hidden = jax.nn.gelu(up_pre).astype(BF)
-    mlp_out = jnp.dot(hidden, w_down, preferred_element_type=F32)
-    gate_pre = jnp.dot(normed, w_gate, preferred_element_type=F32)
-    gate_act = jax.nn.gelu(gate_pre)
-    mixed_in = (gate_act * fetched.astype(F32)).astype(BF)
-    proj_out = jnp.dot(mixed_in, w_proj, preferred_element_type=F32)
-    x_next = (x_f32 + mlp_out + proj_out).astype(BF)
-    return x_next, (x, up_pre, gate_pre, fetched)
-
-
-def mixed_cot(cot_next, w_proj):
-    return jnp.einsum('td,ed->te', cot_next, w_proj, preferred_element_type=F32).astype(BF)
-
-
-def layer_backward(cot_next, d_mixed, saved, w_up, w_down, w_gate):
-    x, up_pre, gate_pre, fetched = saved
-    d_gate_act = d_mixed.astype(F32) * fetched.astype(F32)
-    d_gate_pre = jax.vjp(jax.nn.gelu, gate_pre)[1](d_gate_act)[0]
-    d_hidden = jnp.einsum('td,fd->tf', cot_next, w_down, preferred_element_type=F32).astype(BF)
-    d_up_pre = jax.vjp(jax.nn.gelu, up_pre)[1](d_hidden.astype(F32))[0]
-    d_norm_mlp = jnp.einsum('tf,df->td', d_up_pre.astype(BF), w_up, preferred_element_type=F32).astype(BF)
-    d_norm_gate = jnp.einsum('te,de->td', d_gate_pre.astype(BF), w_gate, preferred_element_type=F32).astype(BF)
-    d_normed = (d_norm_mlp + d_norm_gate).astype(F32)
-    d_x_norm = jax.vjp(rms_norm, x.astype(F32))[1](d_normed)[0]
-    return (cot_next.astype(F32) + d_x_norm).astype(BF)
+def share_kernel(n_dp, n_emb, ids_ref, out_ref, local_sem, send_sem, recv_sem):
+    n = n_dp * n_emb
+    me = lax.axis_index('dp') * n_emb + lax.axis_index('emb')
+
+    def place(o):
+        to = lax.rem(me + o, n)
+        return (to // n_emb, lax.rem(to, n_emb))
+
+    barrier = pltpu.get_barrier_semaphore()
+    for o in range(1, n):
+        pl.semaphore_signal(barrier, inc=1, device_id=place(o), device_id_type=pl.DeviceIdType.MESH)
+    pl.semaphore_wait(barrier, n - 1)
+    sends = [
+        pltpu.make_async_remote_copy(
+            src_ref=ids_ref, dst_ref=out_ref.at[me], send_sem=send_sem.at[o], recv_sem=recv_sem.at[o],
+            device_id=place(o), device_id_type=pl.DeviceIdType.MESH)
+        for o in range(1, n)
+    ]
+    for cp in sends:
+        cp.start()
+    out_ref[me] = ids_ref[...]
+    for cp in sends:
+        cp.wait()
+
+
+def share_ids(ids, n_dp, n_emb):
+    n = n_dp * n_emb
+    rows = ids.shape[0] // 128
+    vmem = pl.BlockSpec(memory_space=pltpu.VMEM)
+    out = pl.pallas_call(
+        functools.partial(share_kernel, n_dp, n_emb),
+        out_shape=jax.ShapeDtypeStruct((n, rows, 128), jnp.int32),
+        in_specs=[vmem], out_specs=vmem,
+        scratch_shapes=[pltpu.SemaphoreType.DMA, pltpu.SemaphoreType.DMA((n,)), pltpu.SemaphoreType.DMA((n,))],
+        compiler_params=pltpu.CompilerParams(collective_id=0, has_side_effects=True),
+        name="share_ids",
+    )(ids.reshape(rows, 128))
+    return out.reshape(-1)
+
+
+FCH = 512
+N_BUF = 3
+GELU_C = 0.7978845608028654
+GELU_A = 0.044715
+
+
+def gelu_grad(v):
+    t = jnp.tanh(GELU_C * (v + GELU_A * (v * v * v)))
+    return 0.5 * (1.0 + t) + (0.5 * GELU_C) * v * (1.0 - t * t) * (1.0 + (3 * GELU_A) * (v * v))
+
+
+def dot_nt(a, b):
+    return lax.dot_general(a, b, (((1,), (1,)), ((), ())), preferred_element_type=F32)
+
+
+def dot_nn(a, b):
+    return jnp.dot(a, b, preferred_element_type=F32)
+
+
+def stream(layer, w_up, w_down, up_buf, down_buf, sem):
+    def copies(c):
+        buf = lax.rem(c, N_BUF)
+        f = pl.multiple_of(c * FCH, FCH)
+        return (pltpu.make_async_copy(w_up.at[layer, :, pl.ds(f, FCH)], up_buf.at[buf], sem.at[0, buf]),
+                pltpu.make_async_copy(w_down.at[layer, pl.ds(f, FCH), :], down_buf.at[buf], sem.at[1, buf]))
+
+    return copies
+
+
+def forward_kernel(layer, keep, x_ref, u_ref, rows_ref, pick_ref, w_up, w_down, w_gate, w_proj, *rest):
+    if keep:
+        x_out, u_out, up_hbm, gate_hbm, got_out = rest[:5]
+        up_buf, down_buf, gate_w, proj_w, acc, up_stage, gate_stage, sem, sem_gp, sem_o = rest[5:]
+    else:
+        x_out, u_out = rest[:2]
+        up_buf, down_buf, gate_w, proj_w, acc, sem, sem_gp = rest[2:]
+    n_ch = w_up.shape[2] // FCH
+    copies = stream(layer, w_up, w_down, up_buf, down_buf, sem)
+    for c in range(N_BUF - 1):
+        for cp in copies(c):
+            cp.start()
+    gate_cp = pltpu.make_async_copy(w_gate.at[layer], gate_w, sem_gp.at[0])
+    proj_cp = pltpu.make_async_copy(w_proj.at[layer], proj_w, sem_gp.at[1])
+    gate_cp.start()
+    proj_cp.start()
+
+    def stage_copy(c):
+        buf = lax.rem(c, 2)
+        return pltpu.make_async_copy(
+            up_stage.at[buf], up_hbm.at[:, pl.ds(pl.multiple_of(c * FCH, FCH), FCH)], sem_o.at[buf])
+
+    acc[...] = x_ref[...].astype(F32)
+
+    def chunk(c, _):
+        @pl.when(c + N_BUF - 1 < n_ch)
+        def _():
+            for cp in copies(c + N_BUF - 1):
+                cp.start()
+
+        for cp in copies(c):
+            cp.wait()
+        if keep:
+            @pl.when(c >= 2)
+            def _():
+                stage_copy(c - 2).wait()
+
+        buf = lax.rem(c, N_BUF)
+        hidden = []
+        for n in range(FCH // 256):
+            pre = dot_nn(u_ref[...], up_buf[buf, :, n * 256:(n + 1) * 256])
+            if keep:
+                up_stage[lax.rem(c, 2), :, n * 256:(n + 1) * 256] = pre
+            hidden.append(jax.nn.gelu(pre).astype(BF))
+        hidden = jnp.concatenate(hidden, axis=1)
+        for n in range(4):
+            acc[:, n * 256:(n + 1) * 256] += dot_nn(hidden, down_buf[buf, :, n * 256:(n + 1) * 256])
+        if keep:
+            stage_copy(c).start()
+        return 0
+
+    lax.fori_loop(0, n_ch, chunk, 0)
+    gate_cp.wait()
+    proj_cp.wait()
+    mixed = []
+    for n in range(4):
+        cols = slice(n * 256, (n + 1) * 256)
+        pre = dot_nn(u_ref[...], gate_w[:, cols])
+        got = dot_nn(pick_ref[...], rows_ref[:, cols]).astype(BF)
+        if keep:
+            gate_stage[:, cols] = pre
+            got_out[:, cols] = got
+        mixed.append((jax.nn.gelu(pre) * got.astype(F32)).astype(BF))
+    mixed = jnp.concatenate(mixed, axis=1)
+    if keep:
+        gate_out = pltpu.make_async_copy(gate_stage, gate_hbm, sem_o.at[2])
+        gate_out.start()
+    for n in range(4):
+        cols = slice(n * 256, (n + 1) * 256)
+        x_out[:, cols] = (acc[:, cols] + dot_nn(mixed, proj_w[:, cols])).astype(BF)
+    x_next = x_out[...].astype(F32)
+    scale = lax.rsqrt(jnp.mean(x_next * x_next, axis=-1, keepdims=True) + NORM_EPS)
+    u_out[...] = (x_next * scale).astype(BF)
+    if keep:
+        gate_out.wait()
+        stage_copy(n_ch - 2).wait()
+        stage_copy(n_ch - 1).wait()
+
+
+def layer_fwd(layer, keep, x, u, rows, pick, w_up, w_down, w_gate, w_proj):
+    t, d = x.shape
+    f = w_up.shape[2]
+    hbm = pl.BlockSpec(memory_space=pltpu.HBM)
+    vmem = pl.BlockSpec(memory_space=pltpu.VMEM)
+    act = jax.ShapeDtypeStruct((t, d), BF)
+    out_shape = [act, act]
+    out_specs = [vmem, vmem]
+    scratch = [
+        pltpu.VMEM((N_BUF, d, FCH), BF), pltpu.VMEM((N_BUF, FCH, d), BF),
+        pltpu.VMEM((d, d), BF), pltpu.VMEM((d, d), BF), pltpu.VMEM((t, d), F32),
+    ]
+    sems = [pltpu.SemaphoreType.DMA((2, N_BUF)), pltpu.SemaphoreType.DMA((2,))]
+    if keep:
+        out_shape += [pltpu.HBM((t, f), F32), pltpu.HBM((t, d), F32), act]
+        out_specs += [hbm, hbm, vmem]
+        scratch += [pltpu.VMEM((2, t, FCH), F32), pltpu.VMEM((t, d), F32)]
+        sems += [pltpu.SemaphoreType.DMA((3,))]
+    return pl.pallas_call(
+        functools.partial(forward_kernel, layer, keep),
+        out_shape=out_shape, in_specs=[vmem] * 4 + [hbm] * 4, out_specs=out_specs,
+        scratch_shapes=scratch + sems,
+        compiler_params=pltpu.CompilerParams(vmem_limit_bytes=40 << 20),
+        cost_estimate=pl.CostEstimate(flops=11_000_000_000, bytes_accessed=30_000_000, transcendentals=0),
+    )(x, u, rows, pick, w_up, w_down, w_gate, w_proj)
+
+
+def backward_kernel(layer, cot_ref, dm_ref, x_ref, got_ref, up_hbm, gate_hbm, w_up, w_down, w_gate, w_proj,
+                    cot_out, dm_out, up_buf, down_buf, pre_buf, gate_w, proj_w, gate_pre, acc, sem, sem_gp):
+    n_ch = w_up.shape[2] // FCH
+    copies = stream(layer, w_up, w_down, up_buf, down_buf, sem)
+
+    def all_copies(c):
+        buf = lax.rem(c, N_BUF)
+        pre = pltpu.make_async_copy(
+            up_hbm.at[:, pl.ds(pl.multiple_of(c * FCH, FCH), FCH)], pre_buf.at[buf], sem.at[2, buf])
+        return copies(c) + (pre,)
+
+    for c in range(N_BUF - 1):
+        for cp in all_copies(c):
+            cp.start()
+    gate_cp = pltpu.make_async_copy(w_gate.at[layer], gate_w, sem_gp.at[0])
+    pre_cp = pltpu.make_async_copy(gate_hbm, gate_pre, sem_gp.at[1])
+    proj_cp = pltpu.make_async_copy(w_proj.at[layer - 1], proj_w, sem_gp.at[2])
+    for cp in (gate_cp, pre_cp, proj_cp):
+        cp.start()
+
+    def chunk(c, _):
+        @pl.when(c + N_BUF - 1 < n_ch)
+        def _():
+            for cp in all_copies(c + N_BUF - 1):
+                cp.start()
+
+        for cp in all_copies(c):
+            cp.wait()
+        buf = lax.rem(c, N_BUF)
+        d_pre = []
+        for n in range(FCH // 256):
+            cols = slice(n * 256, (n + 1) * 256)
+            d_hidden = dot_nt(cot_ref[...], down_buf[buf, cols, :]).astype(BF).astype(F32)
+            d_pre.append((d_hidden * gelu_grad(pre_buf[buf, :, cols])).astype(BF))
+        d_pre = jnp.concatenate(d_pre, axis=1)
+        for n in range(4):
+            cols = slice(n * 256, (n + 1) * 256)
+            part = dot_nt(d_pre, up_buf[buf, cols, :])
+            acc[:, cols] = part + jnp.where(c == 0, 0.0, acc[:, cols])
+        return 0
+
+    lax.fori_loop(0, n_ch, chunk, 0)
+    for cp in (gate_cp, pre_cp, proj_cp):
+        cp.wait()
+    d_pre = []
+    for n in range(4):
+        cols = slice(n * 256, (n + 1) * 256)
+        d_act = dm_ref[:, cols].astype(F32) * got_ref[:, cols].astype(F32)
+        d_pre.append((d_act * gelu_grad(gate_pre[:, cols])).astype(BF))
+    d_pre = jnp.concatenate(d_pre, axis=1)
+    for n in range(4):
+        cols = slice(n * 256, (n + 1) * 256)
+        both = acc[:, cols].astype(BF) + dot_nt(d_pre, gate_w[cols, :]).astype(BF)
+        acc[:, cols] = both.astype(F32)
+    x = x_ref[...].astype(F32)
+    dy = acc[...]
+    r = lax.rsqrt(jnp.mean(x * x, axis=-1, keepdims=True) + NORM_EPS)
+    proj = jnp.mean(x * dy, axis=-1, keepdims=True)
+    cot = (cot_ref[...].astype(F32) + (dy * r - x * (r * r * r * proj))).astype(BF)
+    cot_out[...] = cot
+    for n in range(4):
+        cols = slice(n * 256, (n + 1) * 256)
+        dm_out[:, cols] = dot_nt(cot, proj_w[cols, :]).astype(BF)
+
+
+def layer_bwd(layer, cot, d_mixed, x, got, up_pre, gate_pre, w_up, w_down, w_gate, w_proj):
+    t, d = x.shape
+    hbm = pl.BlockSpec(memory_space=pltpu.HBM)
+    vmem = pl.BlockSpec(memory_space=pltpu.VMEM)
+    act = jax.ShapeDtypeStruct((t, d), BF)
+    return pl.pallas_call(
+        functools.partial(backward_kernel, layer),
+        out_shape=[act, act], in_specs=[vmem] * 4 + [hbm] * 6, out_specs=[vmem, vmem],
+        scratch_shapes=[
+            pltpu.VMEM((N_BUF, d, FCH), BF), pltpu.VMEM((N_BUF, FCH, d), BF), pltpu.VMEM((N_BUF, t, FCH), F32),
+            pltpu.VMEM((d, d), BF), pltpu.VMEM((d, d), BF), pltpu.VMEM((t, d), F32), pltpu.VMEM((t, d), F32),
+            pltpu.SemaphoreType.DMA((3, N_BUF)), pltpu.SemaphoreType.DMA((3,)),
+        ],
+        compiler_params=pltpu.CompilerParams(vmem_limit_bytes=40 << 20),
+        cost_estimate=pl.CostEstimate(flops=11_000_000_000, bytes_accessed=40_000_000, transcendentals=0),
+    )(cot, d_mixed, x, got, up_pre, gate_pre, w_up, w_down, w_gate, w_proj)
 
 
 PICK = 32
 
 
-def serve_kernel(n_layers, cap, cnt_ref, row_ref, pick_ref, tables, out_ref, blocks, sem):
-    n_emb = out_ref.shape[0]
+def serve_kernel(n_layers, cap, cnt_ref, start_ref, ids_ref, pick_ref, tables, *rest):
+    outs, (blocks, sem) = rest[:n_layers], rest[n_layers:]
+    n_emb = outs[0].shape[0]
+    range_rows = tables.shape[1]
 
     def issue(e):
         def body(s, _):
-            row = pl.multiple_of(row_ref[e * cap + s], 8)
+            row = lax.rem(ids_ref[start_ref[e] + s], range_rows)
+            row = pl.multiple_of(lax.div(row, 8) * 8, 8)
             slot = pl.multiple_of(s * 8, 8)
             pltpu.make_async_copy(
                 tables.at[:, pl.ds(row, 8), :], blocks.at[e % 2, :, pl.ds(slot, 8), :], sem.at[e % 2]).start()
@@ -85,7 +316,7 @@
             pick = pick_ref[pl.ds(pl.multiple_of(e * cap + r, PICK), PICK), :]
             for l in range(n_layers):
                 rows = blocks[buf, l, pl.ds(pl.multiple_of(r * 8, 8 * PICK), 8 * PICK), :]
-                out_ref[e, pl.ds(l * cap + r, PICK), :] = jnp.dot(pick, rows, preferred_element_type=F32).astype(BF)
+                outs[l][e, pl.ds(r, PICK), :] = jnp.dot(pick, rows, preferred_element_type=F32).astype(BF)
             return 0
 
         lax.fori_loop(0, cnt_ref[e], take, 0)
@@ -93,22 +324,22 @@
         def rest(b, _):
             r = pl.multiple_of(b * PICK, PICK)
             for l in range(n_layers):
-                out_ref[e, pl.ds(l * cap + r, PICK), :] = jnp.zeros((PICK, out_ref.shape[2]), BF)
+                outs[l][e, pl.ds(r, PICK), :] = jnp.zeros((PICK, outs[l].shape[2]), BF)
             return 0
 
         lax.fori_loop(cnt_ref[e], cap // PICK, rest, 0)
 
 
-def serve_rows(tables, counts, rows, pick, cap):
+def serve_rows(tables, counts, starts, ids, pick, cap):
     n_layers, _, width = tables.shape
     n_emb = counts.shape[0]
     smem = pl.BlockSpec(memory_space=pltpu.SMEM)
     vmem = pl.BlockSpec(memory_space=pltpu.VMEM)
     return pl.pallas_call(
         functools.partial(serve_kernel, n_layers, cap),
-        out_shape=jax.ShapeDtypeStruct((n_emb, n_layers * cap, width), BF),
-        in_specs=[smem, smem, vmem, pl.BlockSpec(memory_space=pltpu.HBM)],
-        out_specs=vmem,
+        out_shape=[jax.ShapeDtypeStruct((n_emb, cap, width), BF)] * n_layers,
+        in_specs=[smem, smem, smem, vmem, pl.BlockSpec(memory_space=pltpu.HBM)],
+        out_specs=[vmem] * n_layers,
         scratch_shapes=[
             pltpu.VMEM((2, n_layers, cap * 8, width), BF),
             pltpu.SemaphoreType.DMA((2,)),
@@ -116,7 +347,7 @@
         compiler_params=pltpu.CompilerParams(vmem_limit_bytes=48 << 20),
         cost_estimate=pl.CostEstimate(flops=20_000_000_000, bytes_accessed=30_000_000, transcendentals=0),
         name="serve_rows",
-    )(counts, rows, pick, tables)
+    )(counts, starts, ids, pick, tables)
 
 
 N_SRC = 16
@@ -162,8 +393,7 @@
 
     def out_copy(b):
         buf = lax.rem(b, 2)
-        r = pl.multiple_of(b * BLK, BLK)
-        return pltpu.make_async_copy(stage.at[buf], out.at[pl.ds(r, BLK), :], sem_o.at[buf])
+        return pltpu.make_async_copy(stage.at[buf], out.at[pl.ds(b * (BLK // 8), BLK // 8)], sem_o.at[buf])
 
     def block(b, _):
         @pl.when(b >= 2)
@@ -173,7 +403,9 @@
         u = uc[pl.ds(pl.multiple_of(b * BLK, BLK), BLK), :]
         for n in range(4):
             pre = jnp.dot(u, w_ref[layer, :, n * 256:(n + 1) * 256], preferred_element_type=F32)
-            stage[lax.rem(b, 2), :, n * 256:(n + 1) * 256] = jax.nn.gelu(pre)
+            act = jax.nn.gelu(pre)
+            for j in range(2):
+                stage[lax.rem(b, 2), :, n * 2 + j] = act[:, j * 128:(j + 1) * 128].reshape(BLK // 8, 8, 128)
         out_copy(b).start()
         return 0
 
@@ -187,12 +419,12 @@
     width = w_gate.shape[2]
     return pl.pallas_call(
         functools.partial(gate_kernel, layer, col),
-        out_shape=pltpu.HBM((MAX_ROWS, width), F32),
+        out_shape=pltpu.HBM((MAX_ROWS // 8, width // 128, 8, 128), F32),
         in_specs=[smem, hbm, pl.BlockSpec(memory_space=pltpu.VMEM)],
         out_specs=hbm,
         scratch_shapes=[
             pltpu.VMEM((MAX_ROWS, width), BF),
-            pltpu.VMEM((2, BLK, width), F32),
+            pltpu.VMEM((2, BLK // 8, width // 128, 8, 128), F32),
             pltpu.SemaphoreType.DMA,
             pltpu.SemaphoreType.DMA((2,)),
         ],
@@ -205,33 +437,37 @@
 
 
 def owner_kernel(layer, col, meta_ref, tile_ref, addr_ref, g_hbm, d_hbm, *rest):
-    out, dc, gbuf, prod, acc, sem_d, sem_g, sem_o = rest[-8:]
+    out, dc, prod, acc, sem_d, sem_g, sem_o = rest[-7:]
     n_tiles = tile_ref.shape[0] - 1
     total = n_blocks(meta_ref)
 
     def g_copy(b):
-        buf = lax.rem(b, 2)
-        return pltpu.make_async_copy(g_hbm.at[pl.ds(pl.multiple_of(b * BLK, BLK), BLK), :], gbuf.at[buf], sem_g.at[buf])
-
-    g_copy(0).start()
+        n = BLK // 8
+        return pltpu.make_async_copy(
+            g_hbm.at[pl.ds(b * n, n)], prod.reshape(MAX_ROWS // 8, 8, 8, 128).at[pl.ds(b * n, n)], sem_g.at[b])
+
     pull_runs(meta_ref, d_hbm, col, dc, sem_d)
+    lax.fori_loop(0, total, lambda b, c: (g_copy(b).start(), c)[1], 0)
+
+    def clear(buf):
+        def some(i, _):
+            acc[buf, pl.ds(pl.multiple_of(i * 512, 512), 512), :] = jnp.zeros((512, 128), F32)
+            return 0
+
+        lax.fori_loop(0, TILE_ROWS * 8 // 512, some, 0)
+
+    clear(0)
+    clear(1)
     drain_runs(meta_ref, d_hbm, col, dc, sem_d)
 
     def block(b, _):
         g_copy(b).wait()
-
-        @pl.when(b + 1 < total)
-        def _():
-            g_copy(b + 1).start()
-
-        buf = lax.rem(b, 2)
         for t in range(BLK // 16):
             d = dc[pl.ds(pl.multiple_of(b * BLK + t * 16, 16), 16), :].astype(F32)
-            val = gbuf[buf, t * 16:(t + 1) * 16, :] * d
             for h in range(2):
                 for j in range(8):
-                    prod[pl.ds(pl.multiple_of(b * (BLK * 8) + (2 * t + h) * 64 + j * 8, 8), 8), :] = (
-                        val[h * 8:(h + 1) * 8, j * 128:(j + 1) * 128])
+                    at = pl.ds(pl.multiple_of(b * (BLK * 8) + (2 * t + h) * 64 + j * 8, 8), 8)
+                    prod[at, :] = prod[at, :] * d[h * 8:(h + 1) * 8, j * 128:(j + 1) * 128]
         return 0
 
     lax.fori_loop(0, total, block, 0)
@@ -247,12 +483,8 @@
         @pl.when(t >= 2)
         def _():
             out_copy(t - 2, buf).wait()
-
-        def clear(i, _):
-            acc[buf, pl.ds(pl.multiple_of(i * 512, 512), 512), :] = jnp.zeros((512, 128), F32)
-            return 0
-
-        lax.fori_loop(0, TILE_ROWS * 8 // 512, clear, 0)
+            clear(buf)
+
         first, last = tile_ref[t], tile_ref[t + 1]
 
         def one(i, run):
@@ -283,7 +515,7 @@
 def owner_grad(layer, out_prev, out_shape, meta, tiles, addrs, g_rows, d_all, col):
     smem = pl.BlockSpec(memory_space=pltpu.SMEM)
     hbm = pl.BlockSpec(memory_space=pltpu.HBM)
-    width = g_rows.shape[1]
+    width = g_rows.shape[1] * 128
     args = [meta, tiles, addrs, g_rows, d_all]
     specs = [smem, smem, smem, hbm, hbm]
     aliases = {}
@@ -298,11 +530,10 @@
         out_specs=hbm,
         scratch_shapes=[
             pltpu.VMEM((MAX_ROWS, width), BF),
-            pltpu.VMEM((2, BLK, width), F32),
             pltpu.VMEM((MAX_ROWS * 8, 128), F32),
             pltpu.VMEM((2, TILE_ROWS * 8, 128), F32),
             pltpu.SemaphoreType.DMA,
-            pltpu.SemaphoreType.DMA((2,)),
+            pltpu.SemaphoreType.DMA((MAX_ROWS // BLK,)),
             pltpu.SemaphoreType.DMA((2,)),
         ],
         input_output_aliases=aliases,
@@ -322,6 +553,7 @@
 
     def device_body(tok_ids, resid_in, cot_out, tables, w_up, w_down, w_gate, w_proj):
         n_layers, range_rows, width = tables.shape
+        n_dp = n_dev // n_emb
         n_tok = tok_ids.shape[0]
         cap = min(2 * n_tok // n_emb, 3 * n_tok // 4)
         i_dp, i_emb = lax.axis_index('dp'), lax.axis_index('emb')
@@ -338,50 +570,45 @@
         x = jnp.dot(perm, resid_in, preferred_element_type=F32).astype(BF)
         cot = jnp.dot(perm, cot_out, preferred_element_type=F32).astype(BF)
         normed = rms_norm(x.astype(F32)).astype(BF)
-        d_mixed = mixed_cot(cot, w_proj[last])
+        d_mixed = lax.dot_general(cot, w_proj[last], (((1,), (1,)), ((), ())), preferred_element_type=F32).astype(BF)
         first_set = jnp.concatenate([normed, d_mixed], axis=1)
         set_a = gather(first_set)
 
         ids = jnp.sum(jnp.where(perm_mask, tok_ids[None, :], 0), axis=1)
         ids, _ = lax.optimization_barrier((ids, first_set))
-        ids_all = lax.all_gather(ids, everyone, axis=0, tiled=True)
+        ids_all = share_ids(ids, n_dp, n_emb)
         ids_2d = ids_all.reshape(n_dev, n_tok)
         base = i_emb * range_rows
 
         mine = lax.dynamic_slice(ids_2d, (i_dp * n_emb, 0), (n_emb, n_tok))
         peer_lo = jnp.sum((mine < base).astype(jnp.int32), axis=1)
-        peer_hi = jnp.sum((mine < base + range_rows).astype(jnp.int32), axis=1)
-        count = peer_hi - peer_lo
-        padded = jnp.pad(mine - base, ((0, 0), (0, cap)))
-        asked = jax.vmap(lambda r, s: lax.dynamic_slice(r, (s,), (cap,)))(padded, peer_lo)
+        count = jnp.sum((mine < base + range_rows).astype(jnp.int32), axis=1) - peer_lo
         slot_pos = jnp.arange(cap, dtype=jnp.int32)
-        valid = slot_pos[None, :] < count[:, None]
-        asked = jnp.where(valid, asked, 0)
-        pick_col = jnp.where(valid, (slot_pos[None, :] % PICK) * 8 + asked % 8, -1).reshape(-1, 1)
-        pick8 = (pick_col == jnp.arange(8 * PICK, dtype=jnp.int32)[None, :]).astype(BF)
-        served = serve_rows(tables, (count + PICK - 1) // PICK, (asked // 8 * 8).reshape(-1), pick8, cap)
-        returned = lax.all_to_all(served, 'emb', 0, 0, tiled=True)
-        returned = returned.reshape(n_emb, n_layers, cap, -1)
+        at = pos[None, None, :] == (peer_lo[:, None] + slot_pos[None, :])[:, :, None]
+        low = jnp.sum(jnp.where(at, mine[:, None, :] % 8, 0), axis=2)
+        pick_col = jnp.where(slot_pos[None, :] < count[:, None], (slot_pos[None, :] % PICK) * 8 + low, -1)
+        pick8 = (pick_col.reshape(-1, 1) == jnp.arange(8 * PICK, dtype=jnp.int32)[None, :]).astype(BF)
+        starts = peer_lo + (i_dp * n_emb + jnp.arange(n_emb, dtype=jnp.int32)) * n_tok
+        served = serve_rows(tables, (count + PICK - 1) // PICK, starts, jnp.pad(ids_all, (0, PICK)), pick8, cap)
+        returned = [lax.all_to_all(rows, 'emb', 0, 0, tiled=True).reshape(n_emb * cap, width) for rows in served]
         owner = ids // range_rows
         first = jnp.sum((owner[None, :] < owner[:, None]).astype(jnp.int32), axis=1)
         slot = owner * cap + pos - first
         pick = (slot[:, None] == jnp.arange(n_emb * cap, dtype=jnp.int32)[None, :]).astype(BF)
 
+        weights = (w_up, w_down, w_gate, w_proj)
         saved, us = [], [normed]
         for l in range(n_layers):
-            rows_l = returned[:, l].reshape(n_emb * cap, -1)
-            fetched = jnp.dot(pick, rows_l, preferred_element_type=F32).astype(BF)
-            x, kept = layer_forward(x, normed, fetched, w_up[l], w_down[l], w_gate[l], w_proj[l])
-            saved.append(kept)
-            if l < last:
-                normed = rms_norm(x.astype(F32)).astype(BF)
-                us.append(normed)
-        set_b = gather(jnp.concatenate(us[1:], axis=1))
+            x_in = x
+            x, u_next, *kept = layer_fwd(l, l > 0, x, us[-1], returned[l], pick, *weights)
+            saved.append((x_in, *kept))
+            us.append(u_next)
+        set_b = gather(jnp.concatenate(us[1:n_layers], axis=1))
         resid_out = lax.dot_general(perm, x, (((0,), (0,)), ((), ())), preferred_element_type=F32).astype(BF)
         d_sets = [None] * n_layers
         for l in range(last, 0, -1):
-            cot = layer_backward(cot, d_mixed, saved[l], w_up[l], w_down[l], w_gate[l])
-            d_mixed = mixed_cot(cot, w_proj[l - 1])
+            x_in, up_pre, gate_pre, got = saved[l]
+            cot, d_mixed = layer_bwd(l, cot, d_mixed, x_in, got, up_pre, gate_pre, *weights)
             d_sets[l - 1] = (gather(d_mixed), 0)
 
         n_tiles = range_rows // TILE_ROWS

time: 611 us -> 536 us (0.88)
  matrix products: 148 us -> 8.96 us
  Pallas kernels: 224 us -> 298 us
  waiting for transfers between devices: 157 us -> 127 us
  blocking collectives: 14.5 us -> 36 us
    dot_general x19 -> x1, matrix products: 132 us -> 3.25 us  [device_body(): lax.dot_general(cot, w_proj[last], (((1,), (1,)), ((), ())), preferred_el...]
    pallas_call x0 -> x6, Pallas kernels: none -> 106 us  [the longest x3 55.5 us: layer_fwd(): pl.pallas_call(functools.partial(forward_kernel, layer, keep), out_shape=...]
    all_to_all x1 -> x2, waiting for transfers between devices: 124 us -> 66.2 us  [device_body(): lax.all_to_all(rows, 'emb', 0, 0, tiled=True).reshape(n_emb * cap, width)]
    all_to_all x0 -> x1, blocking collectives: none -> 36 us  [device_body(): lax.all_to_all(rows, 'emb', 0, 0, tiled=True).reshape(n_emb * cap, width)]
    pallas_call x3, Pallas kernels: 148 us -> 113 us  [owner_grad(): pl.pallas_call(functools.partial(owner_kernel, layer, col), out_shape=jax...]
    all_gather x4, waiting for transfers between devices: 33 us -> 60.9 us  [gather(): return lax.all_gather(rows, everyone, axis=0, tiled=True)]
    unnamed x47 -> x55, local copies, waits for them, and re-layouts: 9.31 us -> 23.9 us
    all_gather x1 -> x0, blocking collectives: 14.5 us -> none  [device_body(): ids_all = lax.all_gather(ids, everyone, axis=0, tiled=True)]
  transfers between devices with their start and end apart: 5 -> 6, of which waited for: 3 -> 5; matrix products, arithmetic and copies ran while one was open for 28% -> 3% of each run, Pallas kernels for 29% -> 49%
where the time goes in v3:
time: 536 us; the launch traced here: 534 us
  Pallas kernels  298 us (56%)
  waiting for transfers between devices  127 us (24%)
  blocking collectives  36 us (7%)
  local copies, waits for them, and re-layouts  24.7 us (5%)
  other arithmetic  14.9 us (3%)
  between operations  14.2 us (3%)
  starting transfers between devices  9.7 us (2%)
  matrix products  8.96 us (2%)
    pallas_call x3, Pallas kernels, owner_grad(): pl.pallas_call(functools.partial(owner_kernel, layer, col), out_shape=jax...  113 us
    all_to_all x2, waiting for transfers between devices, device_body(): lax.all_to_all(rows, 'emb', 0, 0, tiled=True).reshape(n_emb * cap, width)  66.2 us
    all_gather x4, waiting for transfers between devices, gather(): return lax.all_gather(rows, everyone, axis=0, tiled=True)  60.9 us
    pallas_call x3, Pallas kernels, layer_fwd(): pl.pallas_call(functools.partial(forward_kernel, layer, keep), out_shape=...  55.5 us
    pallas_call x3, Pallas kernels, owner_gate(): pl.pallas_call(functools.partial(gate_kernel, layer, col), out_shape=pltp...  52.3 us
    pallas_call x2, Pallas kernels, layer_bwd(): pl.pallas_call(functools.partial(backward_kernel, layer), out_shape=[act,...  41.8 us
    all_to_all x1, blocking collectives, device_body(): lax.all_to_all(rows, 'emb', 0, 0, tiled=True).reshape(n_emb * cap, width)  36 us
    pallas_call x1, Pallas kernels, serve_rows(): pl.pallas_call(functools.partial(serve_kernel, n_layers, cap), out_shape=...  27.1 us
  transfers between devices with their start and end apart: 6, of which 5 were waited for; matrix products, arithmetic and copies ran while one was open for 3% of the time, Pallas kernels for 49%

profile of v3, /device:TPU:0, one launch (start us, length us, event | category | flops | bytes accessed | tf_op | source)
XLA Modules:
  0.0 534.1 jit_solution(12168630583975076048)
XLA Ops:
  7.2 1.1 convert_reduce_fusion.1
  8.3 1.9 convolution_convert_fusion.1.cot_ref
  10.3 0.8 fusion
  11.1 3.3 fusion.6.dm_ref
  14.6 0.7 copy-done.7
  15.4 1.5 pad_maximum_fusion
  17.6 0.7 select_reduce_fusion.1
  18.3 9.0 %share_ids.1 = s32[16,4,128]{2,1,0:T(4,128)} custom-call(s32[4,128]{1,0:T(4,128)} %bitcast.34), custom_call_target="tpu_custom_call" | custom-call | tf_op jit(solution)/shard_map/share_ids/pallas_call | solution.py:53
  27.2 0.8 copy.16
  28.8 0.8 pad.4.ids_ref
  29.8 27.1 %serve_rows.1 = (bf16[4,256,1024]{2,1,0:T(8,128)(2,1)}, bf16[4,256,1024]{2,1,0:T(8,128)(2,1)}, bf16[4,256,1024]{2,1,0:T(8,128)(2,1)}) custom-call(s32[4]{0:T(128)S(1)} %get-tuple-element.47.cnt_ref, s32[4]{0:T(128)S(1)} %get-tuple-element.50.start_ref, s32[8224]{0:T(1024)S(1)} %pad.4.ids_ref, bf16[1024,256]{1,0:T(8,128)(2,1)S(1)} %fusion.11.pick_ref, ...), custom_call_target="tpu_custom_call" | custom-call | flops 20000000000 | bytes 30000000 | tf_op jit(solution)/shard_map/serve_rows/pallas_call | solution.py:338
  57.0 4.5 all-to-all-start
  61.5 42.6 %all-to-all-done = bf16[4,256,1024]{2,1,0:T(8,128)(2,1)} async-done(((bf16[4,256,1024]{2,1,0:T(8,128)(2,1)}), bf16[4,256,1024]{2,1,0:T(8,128)(2,1)}, u32[]{:S(2)}, u32[]{:S(2)}) %all-to-all-start) | async-done | bytes 2097184 | tf_op jit(solution)/shard_map/all_to_all | solution.py:593
  104.1 4.6 all-to-all-start.1
  109.4 4.0 copy-done.2
  113.5 1.2 copy-done.6
  114.7 18.0 %shard_map.95 = (bf16[512,1024]{1,0:T(8,128)(2,1)S(1)}, bf16[512,1024]{1,0:T(8,128)(2,1)S(1)}) custom-call(bf16[512,1024]{1,0:T(8,128)(2,1)S(1)} %copy-done.6, bf16[512,1024]{1,0:T(8,128)(2,1)S(1)} %fusion.1.u_ref, bf16[1024,1024]{1,0:T(8,128)(2,1)} %bitcast.3.rows_ref, bf16[512,1024]{1,0:T(8,128)(2,1)S(1)} %fusion.5.pick_ref, bf16[3,1024,4096]{2,1,0:T(8,128)(2,1)} %w_up.9, ...), custom_call_target="tpu_custom_call" | custom-call | flops 11000000512 | bytes 30000000 | tf_op jit(solution)/shard_map/pallas_call | solution.py:190
  132.7 1.0 copy-done.11
  133.7 23.6 %all-to-all-done.1 = bf16[4,256,1024]{2,1,0:T(8,128)(2,1)} async-done(((bf16[4,256,1024]{2,1,0:T(8,128)(2,1)}), bf16[4,256,1024]{2,1,0:T(8,128)(2,1)}, u32[]{:S(2)}, u32[]{:S(2)}) %all-to-all-start.1) | async-done | bytes 2097184 | tf_op jit(solution)/shard_map/all_to_all | solution.py:593
  157.3 1.2 copy-done.12
  158.5 18.6 %shard_map.96 = (bf16[512,1024]{1,0:T(8,128)(2,1)S(1)}, bf16[512,1024]{1,0:T(8,128)(2,1)S(1)}, f32[512,4096]{1,0:T(8,128)}, f32[512,1024]{1,0:T(8,128)}, bf16[512,1024]{1,0:T(8,128)(2,1)S(1)}) custom-call(bf16[512,1024]{1,0:T(8,128)(2,1)S(1)} %get-tuple-element.23.x_ref, bf16[512,1024]{1,0:T(8,128)(2,1)S(1)} %copy-done.12, ...), custom_call_target="tpu_custom_call" | custom-call | flops 11000000512 | bytes 30000000 | tf_op jit(solution)/shard_map/pallas_call | solution.py:190
  177.1 1.0 copy-done.17
  178.1 1.6 pad_maximum_fusion.1
  179.6 1.0 copy-done.9
  180.7 36.0 %all_to_all.15 = bf16[4,256,1024]{2,1,0:T(8,128)(2,1)S(1)} all-to-all(bf16[4,256,1024]{2,1,0:T(8,128)(2,1)} %get-tuple-element.28), channel_id=1, replica_groups=mesh['dp'=4,'emb'=4] {'emb'}, dimensions={0} | all-to-all | bytes 4194304 | tf_op jit(solution)/shard_map/all_to_all | solution.py:593
  216.7 18.9 %shard_map.97 = (bf16[512,1024]{1,0:T(8,128)(2,1)S(1)}, bf16[512,1024]{1,0:T(8,128)(2,1)}, f32[512,4096]{1,0:T(8,128)}, f32[512,1024]{1,0:T(8,128)}, bf16[512,1024]{1,0:T(8,128)(2,1)S(1)}) custom-call(bf16[512,1024]{1,0:T(8,128)(2,1)S(1)} %get-tuple-element.26.x_ref, bf16[512,1024]{1,0:T(8,128)(2,1)S(1)} %copy-done.10, bf16[1024,1024]{1,0:T(8,128)(2,1)S(1)} %bitcast.28, ...), custom_call_target="tpu_custom_call" | custom-call | flops 11000000512 | bytes 30000000 | tf_op jit(solution)/shard_map/pallas_call | solution.py:190
  235.7 2.0 copy-done.14
  237.7 20.0 %shard_map.98 = (bf16[512,1024]{1,0:T(8,128)(2,1)S(1)}, bf16[512,1024]{1,0:T(8,128)(2,1)}) custom-call(bf16[512,1024]{1,0:T(8,128)(2,1)S(1)} %copy-done.16, bf16[512,1024]{1,0:T(8,128)(2,1)S(1)} %copy-done.8, bf16[512,1024]{1,0:T(8,128)(2,1)S(1)} %get-tuple-element.26.x_ref, bf16[512,1024]{1,0:T(8,128)(2,1)S(1)} %get-tuple-element.30.got_ref, ...), custom_call_target="tpu_custom_call" | custom-call | flops 11000000512 | bytes 40000000 | tf_op jit(solution)/shard_map/pallas_call | solution.py:269
  257.7 1.0 copy-done.19
  259.0 1.6 copy-done.13
  260.6 1.2 copy-done.20
  261.8 21.8 %shard_map.99 = (bf16[512,1024]{1,0:T(8,128)(2,1)}, bf16[512,1024]{1,0:T(8,128)(2,1)S(1)}) custom-call(bf16[512,1024]{1,0:T(8,128)(2,1)S(1)} %copy-done.20, bf16[512,1024]{1,0:T(8,128)(2,1)} %get-tuple-element.34.dm_ref, bf16[512,1024]{1,0:T(8,128)(2,1)S(1)} %get-tuple-element.23.x_ref, bf16[512,1024]{1,0:T(8,128)(2,1)S(1)} %copy-done.18, ...), custom_call_target="tpu_custom_call" | custom-call | flops 11000000512 | bytes 40000000 | tf_op jit(solution)/shard_map/pallas_call | solution.py:269
  283.6 1.0 copy-done.21
  284.6 0.7 convert_reduce_fusion.4
  286.2 5.6 %sort.7 = s32[8192]{0:T(1024)S(1)} sort(s32[8192]{0:T(1024)S(1)} %add_select_fusion), dimensions={0}, to_apply=%region_11.12 | sort | flops 106496 | bytes 65536 | tf_op jit(solution)/shard_map/sort | solution.py:626
  291.8 0.7 pad_add_fusion.meta_ref
  292.9 3.0 convolution_convert_fusion
  295.9 2.8 copy-done.3
  298.7 17.5 %shard_map.100.g_hbm = f32[544,8,8,128]{3,2,1,0:T(8,128)} custom-call(s32[49]{0:T(128)S(1)} %pad_add_fusion.meta_ref, bf16[8192,2048]{1,0:T(8,128)(2,1)} %all-gather.5.cloned.1.call-done.u_hbm.d_hbm, bf16[3,1024,1024]{2,1,0:T(8,128)(2,1)S(1)} %copy-done.3), custom_call_target="tpu_custom_call" | custom-call | flops 10000000000 | bytes 30000000 | tf_op jit(solution)/shard_map/pallas_call | solution.py:420
  316.2 16.9 %all-gather.9.cloned.1.call-done.u_hbm = bf16[8192,2048]{1,0:T(8,128)(2,1)} async-done(((bf16[512,2048]{1,0:T(8,128)(2,1)}), bf16[8192,2048]{1,0:T(8,128)(2,1)}) %all-gather.9.cloned.1.call-update) | async-done | bytes 33554448 | tf_op jit(solution)/shard_map/all_gather | solution.py:563
  333.1 2.8 copy-done.4
  335.9 17.2 %shard_map.102.g_hbm = f32[544,8,8,128]{3,2,1,0:T(8,128)} custom-call(s32[49]{0:T(128)S(1)} %pad_add_fusion.meta_ref, bf16[8192,2048]{1,0:T(8,128)(2,1)} %all-gather.9.cloned.1.call-done.u_hbm, bf16[3,1024,1024]{2,1,0:T(8,128)(2,1)S(1)} %copy-done.4), custom_call_target="tpu_custom_call" | custom-call | flops 10000000000 | bytes 30000000 | tf_op jit(solution)/shard_map/pallas_call | solution.py:420
  353.1 17.5 %shard_map.101.g_hbm = f32[544,8,8,128]{3,2,1,0:T(8,128)} custom-call(s32[49]{0:T(128)S(1)} %pad_add_fusion.meta_ref, bf16[8192,2048]{1,0:T(8,128)(2,1)} %all-gather.9.cloned.1.call-done.u_hbm, bf16[3,1024,1024]{2,1,0:T(8,128)(2,1)S(1)} %copy-done.4), custom_call_target="tpu_custom_call" | custom-call | flops 10000000000 | bytes 30000000 | tf_op jit(solution)/shard_map/pallas_call | solution.py:420
  370.7 38.6 %shard_map.103.rest_0_ = f32[3,2048,8,8,128]{4,3,2,1,0:T(8,128)} custom-call(s32[49]{0:T(128)S(1)} %pad_add_fusion.meta_ref, s32[17]{0:T(128)S(1)} %convert_reduce_fusion.2.tile_ref, s32[4096]{0:T(1024)S(1)} %fusion.18.addr_ref, f32[544,8,8,128]{3,2,1,0:T(8,128)} %shard_map.102.g_hbm, bf16[8192,2048]{1,0:T(8,128)(2,1)} %all-gather.5.cloned.1.call-done.u_hbm.d_hbm), custom_call_target="tpu_custom_call" | custom-call | flops 40000000000 | bytes 100000000 | tf_op jit(solution)/shard_map/pallas_call | solution.py:526
  409.3 2.7 all-gather.11.cloned.1.call-done.d_hbm
  411.9 37.2 %shard_map.104.rest_0_ = f32[3,2048,8,8,128]{4,3,2,1,0:T(8,128)} custom-call(s32[49]{0:T(128)S(1)} %pad_add_fusion.meta_ref, s32[17]{0:T(128)S(1)} %convert_reduce_fusion.2.tile_ref, s32[4096]{0:T(1024)S(1)} %fusion.18.addr_ref, f32[544,8,8,128]{3,2,1,0:T(8,128)} %shard_map.101.g_hbm, ...), custom_call_target="tpu_custom_call", output_to_operand_aliasing={{}: (5, {})} | custom-call | flops 40000000000 | bytes 100000000 | tf_op jit(solution)/shard_map/pallas_call | solution.py:526
  449.2 41.4 %all-gather.7.cloned.1.call-done.d_hbm = bf16[8192,1024]{1,0:T(8,128)(2,1)} async-done(((bf16[512,1024]{1,0:T(8,128)(2,1)}), bf16[8192,1024]{1,0:T(8,128)(2,1)}) %all-gather.7.cloned.1.call-update) | async-done | bytes 16777232 | tf_op jit(solution)/shard_map/all_gather | solution.py:563
  490.5 37.0 %shard_map.105 = f32[3,2048,8,8,128]{4,3,2,1,0:T(8,128)} custom-call(s32[49]{0:T(128)S(1)} %pad_add_fusion.meta_ref, s32[17]{0:T(128)S(1)} %convert_reduce_fusion.2.tile_ref, s32[4096]{0:T(1024)S(1)} %fusion.18.addr_ref, f32[544,8,8,128]{3,2,1,0:T(8,128)} %shard_map.100.g_hbm, ...), custom_call_target="tpu_custom_call", output_to_operand_aliasing={{}: (5, {})} | custom-call | flops 40000000000 | bytes 100000000 | tf_op jit(solution)/shard_map/pallas_call | solution.py:526
  (72 shorter events, 4.4 us)
Async XLA Ops:
  7.2 3.1 copy-start
  7.2 288.7 %all-gather.5.cloned.1.call-start = ((), (), s32[]{:S(2)}) async-start(), calls=%async_computation.3 | async-start | bytes 35651584 | tf_op jit(solution)/shard_map/all_gather | solution.py:563
  10.3 4.1 copy-start.15
  11.1 3.3 copy-start.5
  14.4 1.0 copy-start.7
  16.9 0.7 copy-start.25
  57.0 4.5 copy-start.24
  57.0 47.1 %all-to-all-start = ((bf16[4,256,1024]{2,1,0:T(8,128)(2,1)}), bf16[4,256,1024]{2,1,0:T(8,128)(2,1)}, u32[]{:S(2)}, u32[]{:S(2)}) async-start(bf16[4,256,1024]{2,1,0:T(8,128)(2,1)} %get-tuple-element.22), calls=%async_computation | async-start | bytes 4194304 | tf_op jit(solution)/shard_map/all_to_all | solution.py:593
  104.1 53.2 %all-to-all-start.1 = ((bf16[4,256,1024]{2,1,0:T(8,128)(2,1)}), bf16[4,256,1024]{2,1,0:T(8,128)(2,1)}, u32[]{:S(2)}, u32[]{:S(2)}) async-start(bf16[4,256,1024]{2,1,0:T(8,128)(2,1)} %get-tuple-element.25), calls=%async_computation.1 | async-start | bytes 4194304 | tf_op jit(solution)/shard_map/all_to_all | solution.py:593
  108.7 224.4 %all-gather.9.cloned.1.call-start = ((), (), s32[]{:S(2)}) async-start(), calls=%async_computation.5 | async-start | bytes 35651584 | tf_op jit(solution)/shard_map/all_gather | solution.py:563
  109.4 4.1 copy-start.2
  113.5 1.2 copy-start.6
  132.7 1.0 copy-start.11
  157.3 1.2 copy-start.12
  177.1 1.0 copy-start.17
  179.6 1.0 copy-start.9
  180.6 231.3 %all-gather.11.cloned.1.call-start = ((), (), s32[]{:S(2)}) async-start(), calls=%async_computation.6 | async-start | bytes 17825792 | tf_op jit(solution)/shard_map/all_gather | solution.py:563
  180.7 36.1 %copy-start.10 = (bf16[512,1024]{1,0:T(8,128)(2,1)S(1)}, bf16[512,1024]{1,0:T(8,128)(2,1)}, u32[]{:S(2)}) copy-start(bf16[512,1024]{1,0:T(8,128)(2,1)} %copy-done.9) | copy-start | bytes 3145732
  216.7 19.0 %copy-start.8 = (bf16[512,1024]{1,0:T(8,128)(2,1)S(1)}, bf16[512,1024]{1,0:T(8,128)(2,1)}, u32[]{:S(2)}) copy-start(bf16[512,1024]{1,0:T(8,128)(2,1)} %copy-done.7) | copy-start | bytes 3145732
  216.7 19.0 %copy-start.16 = (bf16[512,1024]{1,0:T(8,128)(2,1)S(1)}, bf16[512,1024]{1,0:T(8,128)(2,1)}, u32[]{:S(2)}) copy-start(bf16[512,1024]{1,0:T(8,128)(2,1)} %copy-done.15) | copy-start | bytes 3145732
  235.7 22.0 %copy-start.22 = (bf16[512,1024]{1,0:T(8,128)(2,1)}, bf16[512,1024]{1,0:T(8,128)(2,1)S(1)}, u32[]{:S(2)}) copy-start(bf16[512,1024]{1,0:T(8,128)(2,1)S(1)} %get-tuple-element.29) | copy-start | bytes 3145732
  235.7 2.0 copy-start.14
  237.7 21.3 %copy-start.18 = (bf16[512,1024]{1,0:T(8,128)(2,1)S(1)}, bf16[512,1024]{1,0:T(8,128)(2,1)}, u32[]{:S(2)}) copy-start(bf16[512,1024]{1,0:T(8,128)(2,1)} %copy-done.17) | copy-start | bytes 3145732
  257.7 1.0 copy-start.19
  258.7 231.9 %all-gather.7.cloned.1.call-start = ((), (), s32[]{:S(2)}) async-start(), calls=%async_computation.4 | async-start | bytes 17825792 | tf_op jit(solution)/shard_map/all_gather | solution.py:563
  259.0 1.6 copy-start.13
  260.6 1.2 copy-start.20
  261.8 22.8 %copy-start.23 = (s32[16,4,128]{2,1,0:T(4,128)S(1)}, s32[16,4,128]{2,1,0:T(4,128)}, u32[]{:S(2)}) copy-start(s32[16,4,128]{2,1,0:T(4,128)} %share_ids.1) | copy-start | bytes 98308
  283.6 1.0 copy-start.21
  295.9 2.8 copy-start.3
  333.1 2.8 copy-start.4
  490.5 37.0 %copy-start.1 = (bf16[512,1024]{1,0:T(8,128)(2,1)S(1)}, bf16[512,1024]{1,0:T(8,128)(2,1)}, u32[]{:S(2)}) copy-start(bf16[512,1024]{1,0:T(8,128)(2,1)} %param.9) | copy-start | bytes 3145732
Sparse Core Ops, SparseCore 0:
  17.0 178.6 all-gather.4
  198.0 135.0 all-gather.8
  335.3 76.5 all-gather.10
  414.0 76.4 all-gather.6

commit v4 on v3

--- a/solution.py
+++ b/solution.py
@@ -15,6 +15,10 @@
 CHUNK = 16
 BLK = 256
 TILE_ROWS = 1024
+
+
+def in_hbm(*arrays):
+    return [pltpu.with_memory_space_constraint(a, pltpu.HBM) for a in arrays]
 
 
 def rms_norm(x_f32):
@@ -90,7 +94,7 @@
     return copies
 
 
-def forward_kernel(layer, keep, x_ref, u_ref, rows_ref, pick_ref, w_up, w_down, w_gate, w_proj, *rest):
+def forward_kernel(layer, keep, x_ref, u_ref, r0_ref, r1_ref, r2_ref, r3_ref, pick_ref, w_up, w_down, w_gate, w_proj, *rest):
     if keep:
         x_out, u_out, up_hbm, gate_hbm, got_out = rest[:5]
         up_buf, down_buf, gate_w, proj_w, acc, up_stage, gate_stage, sem, sem_gp, sem_o = rest[5:]
@@ -148,7 +152,9 @@
     for n in range(4):
         cols = slice(n * 256, (n + 1) * 256)
         pre = dot_nn(u_ref[...], gate_w[:, cols])
-        got = dot_nn(pick_ref[...], rows_ref[:, cols]).astype(BF)
+        cap = r0_ref.shape[0]
+        got = sum(dot_nn(pick_ref[:, f * cap:(f + 1) * cap], r[:, cols])
+                  for f, r in enumerate((r0_ref, r1_ref, r2_ref, r3_ref))).astype(BF)
         if keep:
             gate_stage[:, cols] = pre
             got_out[:, cols] = got
@@ -189,11 +195,11 @@
         sems += [pltpu.SemaphoreType.DMA((3,))]
     return pl.pallas_call(
         functools.partial(forward_kernel, layer, keep),
-        out_shape=out_shape, in_specs=[vmem] * 4 + [hbm] * 4, out_specs=out_specs,
+        out_shape=out_shape, in_specs=[vmem] * 7 + [hbm] * 4, out_specs=out_specs,
         scratch_shapes=scratch + sems,
         compiler_params=pltpu.CompilerParams(vmem_limit_bytes=40 << 20),
         cost_estimate=pl.CostEstimate(flops=11_000_000_000, bytes_accessed=30_000_000, transcendentals=0),
-    )(x, u, rows, pick, w_up, w_down, w_gate, w_proj)
+    )(x, u, *rows, pick, *in_hbm(w_up, w_down, w_gate, w_proj))
 
 
 def backward_kernel(layer, cot_ref, dm_ref, x_ref, got_ref, up_hbm, gate_hbm, w_up, w_down, w_gate, w_proj,
@@ -276,15 +282,15 @@
         ],
         compiler_params=pltpu.CompilerParams(vmem_limit_bytes=40 << 20),
         cost_estimate=pl.CostEstimate(flops=11_000_000_000, bytes_accessed=40_000_000, transcendentals=0),
-    )(cot, d_mixed, x, got, up_pre, gate_pre, w_up, w_down, w_gate, w_proj)
+    )(cot, d_mixed, x, got, *in_hbm(up_pre, gate_pre, w_up, w_down, w_gate, w_proj))
 
 
 PICK = 32
 
 
 def serve_kernel(n_layers, cap, cnt_ref, start_ref, ids_ref, pick_ref, tables, *rest):
-    outs, (blocks, sem) = rest[:n_layers], rest[n_layers:]
-    n_emb = outs[0].shape[0]
+    blocks, sem = rest[-2:]
+    n_emb = len(rest[:-2]) // n_layers
     range_rows = tables.shape[1]
 
     def issue(e):
@@ -316,18 +322,18 @@
             pick = pick_ref[pl.ds(pl.multiple_of(e * cap + r, PICK), PICK), :]
             for l in range(n_layers):
                 rows = blocks[buf, l, pl.ds(pl.multiple_of(r * 8, 8 * PICK), 8 * PICK), :]
-                outs[l][e, pl.ds(r, PICK), :] = jnp.dot(pick, rows, preferred_element_type=F32).astype(BF)
+                rest[l * n_emb + e][pl.ds(r, PICK), :] = jnp.dot(pick, rows, preferred_element_type=F32).astype(BF)
             return 0
 
         lax.fori_loop(0, cnt_ref[e], take, 0)
 
-        def rest(b, _):
+        def blank(b, _):
             r = pl.multiple_of(b * PICK, PICK)
             for l in range(n_layers):
-                outs[l][e, pl.ds(r, PICK), :] = jnp.zeros((PICK, outs[l].shape[2]), BF)
+                rest[l * n_emb + e][pl.ds(r, PICK), :] = jnp.zeros((PICK, tables.shape[2]), BF)
             return 0
 
-        lax.fori_loop(cnt_ref[e], cap // PICK, rest, 0)
+        lax.fori_loop(cnt_ref[e], cap // PICK, blank, 0)
 
 
 def serve_rows(tables, counts, starts, ids, pick, cap):
@@ -337,9 +343,9 @@
     vmem = pl.BlockSpec(memory_space=pltpu.VMEM)
     return pl.pallas_call(
         functools.partial(serve_kernel, n_layers, cap),
-        out_shape=[jax.ShapeDtypeStruct((n_emb, cap, width), BF)] * n_layers,
+        out_shape=[jax.ShapeDtypeStruct((cap, width), BF)] * (n_layers * n_emb),
         in_specs=[smem, smem, smem, vmem, pl.BlockSpec(memory_space=pltpu.HBM)],
-        out_specs=[vmem] * n_layers,
+        out_specs=[vmem] * (n_layers * n_emb),
         scratch_shapes=[
             pltpu.VMEM((2, n_layers, cap * 8, width), BF),
             pltpu.SemaphoreType.DMA((2,)),
@@ -347,36 +353,40 @@
         compiler_params=pltpu.CompilerParams(vmem_limit_bytes=48 << 20),
         cost_estimate=pl.CostEstimate(flops=20_000_000_000, bytes_accessed=30_000_000, transcendentals=0),
         name="serve_rows",
-    )(counts, starts, ids, pick, tables)
+    )(counts, starts, ids, pick, *in_hbm(tables))
 
 
 N_SRC = 16
 MAX_ROWS = 17 * BLK
 
 
-def pull_runs(meta_ref, src, col, dst, sem):
-    src_rows = src.shape[0] // N_SRC
+def pull_runs(meta_ref, srcs, col, dst, sem):
     width = dst.shape[1]
 
-    def run(k, _):
+    def run(src, k, base):
         lo, off = meta_ref[k], meta_ref[2 * N_SRC + k]
 
         def chunk(c, _):
-            a = pl.multiple_of(k * src_rows + lo + c * CHUNK, CHUNK)
+            a = pl.multiple_of(base + lo + c * CHUNK, CHUNK)
             b = pl.multiple_of((off + c) * CHUNK, CHUNK)
             pltpu.make_async_copy(src.at[pl.ds(a, CHUNK), col:col + width], dst.at[pl.ds(b, CHUNK), :], sem).start()
             return 0
 
-        return lax.fori_loop(0, meta_ref[N_SRC + k], chunk, 0)
-
-    lax.fori_loop(0, N_SRC, run, 0)
-
-
-def drain_runs(meta_ref, src, col, dst, sem):
+        lax.fori_loop(0, meta_ref[N_SRC + k], chunk, 0)
+
+    if len(srcs) == 1:
+        src_rows = srcs[0].shape[0] // N_SRC
+        lax.fori_loop(0, N_SRC, lambda k, c: (run(srcs[0], k, k * src_rows), c)[1], 0)
+    else:
+        for j, src in enumerate(srcs):
+            run(src, meta_ref[3 * N_SRC + 1 + j], 0)
+
+
+def drain_runs(meta_ref, srcs, col, dst, sem):
     width = dst.shape[1]
 
     def one(c, _):
-        pltpu.make_async_copy(src.at[pl.ds(0, CHUNK), col:col + width], dst.at[pl.ds(0, CHUNK), :], sem).wait()
+        pltpu.make_async_copy(srcs[0].at[pl.ds(0, CHUNK), col:col + width], dst.at[pl.ds(0, CHUNK), :], sem).wait()
         return 0
 
     lax.fori_loop(0, meta_ref[3 * N_SRC], one, 0)
@@ -387,8 +397,8 @@
 
 
 def gate_kernel(layer, col, meta_ref, u_hbm, w_ref, out, uc, stage, sem_u, sem_o):
-    pull_runs(meta_ref, u_hbm, col, uc, sem_u)
-    drain_runs(meta_ref, u_hbm, col, uc, sem_u)
+    pull_runs(meta_ref, [u_hbm], col, uc, sem_u)
+    drain_runs(meta_ref, [u_hbm], col, uc, sem_u)
     total = n_blocks(meta_ref)
 
     def out_copy(b):
@@ -430,13 +440,14 @@
         ],
         compiler_params=pltpu.CompilerParams(vmem_limit_bytes=28 << 20),
         cost_estimate=pl.CostEstimate(flops=10_000_000_000, bytes_accessed=30_000_000, transcendentals=0),
-    )(meta, u_all, w_gate)
+    )(meta, *in_hbm(u_all), w_gate)
 
 
 UNROLL = 8
 
 
-def owner_kernel(layer, col, meta_ref, tile_ref, addr_ref, g_hbm, d_hbm, *rest):
+def owner_kernel(layer, col, n_src, meta_ref, tile_ref, addr_ref, g_hbm, *rest):
+    d_hbm = rest[:n_src]
     out, dc, prod, acc, sem_d, sem_g, sem_o = rest[-7:]
     n_tiles = tile_ref.shape[0] - 1
     total = n_blocks(meta_ref)
@@ -516,15 +527,15 @@
     smem = pl.BlockSpec(memory_space=pltpu.SMEM)
     hbm = pl.BlockSpec(memory_space=pltpu.HBM)
     width = g_rows.shape[1] * 128
-    args = [meta, tiles, addrs, g_rows, d_all]
-    specs = [smem, smem, smem, hbm, hbm]
+    args = [meta, tiles, addrs, *in_hbm(g_rows, *d_all)]
+    specs = [smem, smem, smem, hbm] + [hbm] * len(d_all)
     aliases = {}
     if out_prev is not None:
         args.append(out_prev)
         specs.append(hbm)
-        aliases = {5: 0}
+        aliases = {len(args) - 1: 0}
     return pl.pallas_call(
-        functools.partial(owner_kernel, layer, col),
+        functools.partial(owner_kernel, layer, col, len(d_all)),
         out_shape=jax.ShapeDtypeStruct(out_shape, F32),
         in_specs=specs,
         out_specs=hbm,
@@ -571,16 +582,38 @@
         cot = jnp.dot(perm, cot_out, preferred_element_type=F32).astype(BF)
         normed = rms_norm(x.astype(F32)).astype(BF)
         d_mixed = lax.dot_general(cot, w_proj[last], (((1,), (1,)), ((), ())), preferred_element_type=F32).astype(BF)
-        first_set = jnp.concatenate([normed, d_mixed], axis=1)
-        set_a = gather(first_set)
+        set_a = gather(normed)
+
+        def flip(block, axis, bit):
+            n = mesh.shape[axis]
+            return lax.ppermute(block, axis, [(i, i ^ bit) for i in range(n)])
+
+        def spread(block):
+            at = {(0, 0, 0): block}
+            at[1, 0, 0] = flip(block, 'emb', 2)
+            at[0, 1, 0] = flip(block, 'dp', 1)
+            at[0, 0, 1] = flip(block, 'dp', 2)
+            at[0, 1, 1] = flip(at[0, 1, 0], 'dp', 2)
+            at[1, 0, 1] = flip(at[1, 0, 0], 'dp', 2)
+            at[1, 1, 0] = flip(at[1, 0, 0], 'dp', 1)
+            at[1, 1, 1] = flip(at[1, 0, 1], 'dp', 1)
+            offsets = sorted(at, key=lambda o: (sum(o), o))
+            blocks = [at[o] for o in offsets] + [flip(at[o], 'emb', 1) for o in offsets]
+            places = [((o[2] * 2 + o[1]), (o[0] * 2 + c)) for c in range(2) for o in offsets]
+            return blocks, places
+
+        d2_blocks, places = spread(d_mixed)
+        sources = jnp.stack([(i_dp ^ d) * n_emb + (i_emb ^ e) for d, e in places]).astype(jnp.int32)
 
         ids = jnp.sum(jnp.where(perm_mask, tok_ids[None, :], 0), axis=1)
-        ids, _ = lax.optimization_barrier((ids, first_set))
+        ids, _ = lax.optimization_barrier((ids, d_mixed))
         ids_all = share_ids(ids, n_dp, n_emb)
         ids_2d = ids_all.reshape(n_dev, n_tok)
         base = i_emb * range_rows
 
-        mine = lax.dynamic_slice(ids_2d, (i_dp * n_emb, 0), (n_emb, n_tok))
+        peers = i_dp * n_emb + (i_emb ^ jnp.arange(n_emb, dtype=jnp.int32))
+        is_peer = peers[:, None] == jnp.arange(n_dev, dtype=jnp.int32)[None, :]
+        mine = jnp.sum(jnp.where(is_peer[:, :, None], ids_2d[None], 0), axis=1)
         peer_lo = jnp.sum((mine < base).astype(jnp.int32), axis=1)
         count = jnp.sum((mine < base + range_rows).astype(jnp.int32), axis=1) - peer_lo
         slot_pos = jnp.arange(cap, dtype=jnp.int32)
@@ -588,12 +621,13 @@
         low = jnp.sum(jnp.where(at, mine[:, None, :] % 8, 0), axis=2)
         pick_col = jnp.where(slot_pos[None, :] < count[:, None], (slot_pos[None, :] % PICK) * 8 + low, -1)
         pick8 = (pick_col.reshape(-1, 1) == jnp.arange(8 * PICK, dtype=jnp.int32)[None, :]).astype(BF)
-        starts = peer_lo + (i_dp * n_emb + jnp.arange(n_emb, dtype=jnp.int32)) * n_tok
-        served = serve_rows(tables, (count + PICK - 1) // PICK, starts, jnp.pad(ids_all, (0, PICK)), pick8, cap)
-        returned = [lax.all_to_all(rows, 'emb', 0, 0, tiled=True).reshape(n_emb * cap, width) for rows in served]
+        served = serve_rows(tables, (count + PICK - 1) // PICK, peer_lo + peers * n_tok,
+                            jnp.pad(ids_all, (0, PICK)), pick8, cap)
+        returned = [[served[l * n_emb]] + [flip(served[l * n_emb + f], 'emb', f) for f in range(1, n_emb)]
+                    for l in range(n_layers)]
         owner = ids // range_rows
         first = jnp.sum((owner[None, :] < owner[:, None]).astype(jnp.int32), axis=1)
-        slot = owner * cap + pos - first
+        slot = (owner ^ i_emb) * cap + pos - first
         pick = (slot[:, None] == jnp.arange(n_emb * cap, dtype=jnp.int32)[None, :]).astype(BF)
 
         weights = (w_up, w_down, w_gate, w_proj)
@@ -609,7 +643,7 @@
         for l in range(last, 0, -1):
             x_in, up_pre, gate_pre, got = saved[l]
             cot, d_mixed = layer_bwd(l, cot, d_mixed, x_in, got, up_pre, gate_pre, *weights)
-            d_sets[l - 1] = (gather(d_mixed), 0)
+            d_sets[l - 1] = spread(d_mixed)[0] if l == last else [gather(d_mixed)]
 
         n_tiles = range_rows // TILE_ROWS
         lo = jnp.sum((ids_2d < base).astype(jnp.int32), axis=1)
@@ -618,7 +652,7 @@
         n_ch = (hi - lo16 + CHUNK - 1) // CHUNK
         tri = jnp.arange(n_dev)[None, :] < jnp.arange(n_dev)[:, None]
         off = jnp.sum(jnp.where(tri, n_ch[None, :], 0), axis=1)
-        meta = jnp.concatenate([lo16, n_ch, off, jnp.sum(n_ch)[None]]).astype(jnp.int32)
+        meta = jnp.concatenate([lo16, n_ch, off, jnp.sum(n_ch)[None], sources]).astype(jnp.int32)
         place = (off * CHUNK - lo16)[:, None] + pos[None, :]
         local = ids_2d - base
         owned = (local >= 0) & (local < range_rows)
@@ -633,12 +667,14 @@
 
         set_a, _ = lax.optimization_barrier((set_a, d_mixed))
         u_sets = [(set_a, 0)] + [(set_b, i * width) for i in range(n_layers - 1)]
-        d_sets[last] = (set_a, width)
+        d_sets[last] = d2_blocks
         grads = None
         out_shape = (n_layers, range_rows // 8, width // 128, 8, 128)
-        gates = [owner_gate(l, meta, *u_sets[l], w_gate) for l in range(n_layers)]
+        gates = []
+        for l in range(n_layers):
+            gates.append(owner_gate(l, meta, *u_sets[l], w_gate))
         for l in range(last, -1, -1):
-            grads = owner_grad(l, grads, out_shape, meta, tiles, addrs, gates[l], *d_sets[l])
+            grads = owner_grad(l, grads, out_shape, meta, tiles, addrs, gates[l], d_sets[l], 0)
         d_tables = grads.transpose(0, 1, 3, 2, 4).reshape(n_layers, range_rows, width)
         return resid_out, d_tables
 

time: 536 us -> 669 us (1.25)
  waiting for transfers between devices: 127 us -> 290 us
  blocking collectives: 36 us -> 0 us
  starting transfers between devices: 9.7 us -> 26 us
  local copies, waits for them, and re-layouts: 24.7 us -> 17.3 us
    ppermute x0 -> x39, waiting for transfers between devices: none -> 290 us  [flip(): return lax.ppermute(block, axis, [(i, i ^ bit) for i in range(n)])]
    all_to_all x2 -> x0, waiting for transfers between devices: 66.2 us -> none  [device_body(): lax.all_to_all(rows, 'emb', 0, 0, tiled=True).reshape(n_emb * cap, width)]
    all_gather x4 -> x3, waiting for transfers between devices: 60.9 us -> 0.04 us  [gather(): return lax.all_gather(rows, everyone, axis=0, tiled=True)]
    all_to_all x1 -> x0, blocking collectives: 36 us -> none  [device_body(): lax.all_to_all(rows, 'emb', 0, 0, tiled=True).reshape(n_emb * cap, width)]
    ppermute x0 -> x39, starting transfers between devices: none -> 25.7 us  [flip(): return lax.ppermute(block, axis, [(i, i ^ bit) for i in range(n)])]
    all_to_all x2 -> x0, starting transfers between devices: 9.09 us -> none  [device_body(): lax.all_to_all(rows, 'emb', 0, 0, tiled=True).reshape(n_emb * cap, width)]
    unnamed x55 -> x87, local copies, waits for them, and re-layouts: 23.9 us -> 15.8 us
  transfers between devices with their start and end apart: 6 -> 42, of which waited for: 5 -> 16; matrix products, arithmetic and copies ran while one was open for 3% -> 3% of each run, Pallas kernels for 49% -> 39%
where the time goes in v4:
time: 669 us; the launch traced here: 663 us
  Pallas kernels  294 us (44%)
  waiting for transfers between devices  290 us (43%)
  starting transfers between devices  26 us (4%)
  local copies, waits for them, and re-layouts  17.3 us (3%)
  other arithmetic  14.7 us (2%)
  between operations  14.7 us (2%)
    ppermute x39, waiting for transfers between devices, flip(): return lax.ppermute(block, axis, [(i, i ^ bit) for i in range(n)])  290 us
    pallas_call x3, Pallas kernels, owner_grad(): pl.pallas_call(functools.partial(owner_kernel, layer, col, len(d_all)), o...  111 us
    pallas_call x3, Pallas kernels, layer_fwd(): pl.pallas_call(functools.partial(forward_kernel, layer, keep), out_shape=...  52.6 us
    pallas_call x3, Pallas kernels, owner_gate(): pl.pallas_call(functools.partial(gate_kernel, layer, col), out_shape=pltp...  51.2 us
    pallas_call x2, Pallas kernels, layer_bwd(): pl.pallas_call(functools.partial(backward_kernel, layer), out_shape=[act,...  44.2 us
    pallas_call x1, Pallas kernels, serve_rows(): pl.pallas_call(functools.partial(serve_kernel, n_layers, cap), out_shape=...  25.7 us
    ppermute x39, starting transfers between devices, flip(): return lax.ppermute(block, axis, [(i, i ^ bit) for i in range(n)])  25.7 us
    unnamed x87, local copies, waits for them, and re-layouts  15.8 us
  transfers between devices with their start and end apart: 42, of which 16 were waited for; matrix products, arithmetic and copies ran while one was open for 3% of the time, Pallas kernels for 39%

profile of v4, /device:TPU:0, one launch (start us, length us, event | category | flops | bytes accessed | tf_op | source)
XLA Modules:
  0.0 663.2 jit_solution(9552079652852191392)
XLA Ops:
  7.2 1.1 convert_reduce_fusion.1
  9.3 1.2 fusion.1.u_ref
  13.1 3.3 fusion.6.dm_ref.rest_0_
  16.3 9.1 %share_ids.1 = s32[16,4,128]{2,1,0:T(4,128)} custom-call(s32[4,128]{1,0:T(4,128)} %bitcast.48), custom_call_target="tpu_custom_call" | custom-call | tf_op jit(solution)/shard_map/share_ids/pallas_call | solution.py:57
  29.0 25.7 %serve_rows.1 = (bf16[256,1024]{1,0:T(8,128)(2,1)S(1)}, bf16[256,1024]{1,0:T(8,128)(2,1)S(1)}, bf16[256,1024]{1,0:T(8,128)(2,1)S(1)}, bf16[256,1024]{1,0:T(8,128...) custom-call(s32[4]{0:T(128)S(1)} %get-tuple-element.65.cnt_ref, ...), custom_call_target="tpu_custom_call" | custom-call | flops 20000000000 | bytes 30000000 | tf_op jit(solution)/shard_map/serve_rows/pallas_call | solution.py:344
  54.8 1.8 collective-permute-start.2
  57.6 1.5 collective-permute-start.5
  59.1 21.7 %collective-permute-done.1.r2_ref = bf16[256,1024]{1,0:T(8,128)(2,1)S(1)} collective-permute-done((bf16[256,1024]{1,0:T(8,128)(2,1)S(1)}, bf16[256,1024]{1,0:T(8,128)(2,1)S(1)}, u32[]{:S(2)}, u32[]{:S(2)}) %collective-permute-start.1) | collective-permute-done | bytes 524320 | tf_op jit(solution)/shard_map/ppermute | solution.py:589
  80.7 20.4 %collective-permute-done.2.r3_ref = bf16[256,1024]{1,0:T(8,128)(2,1)S(1)} collective-permute-done((bf16[256,1024]{1,0:T(8,128)(2,1)S(1)}, bf16[256,1024]{1,0:T(8,128)(2,1)S(1)}, u32[]{:S(2)}, u32[]{:S(2)}) %collective-permute-start.2) | collective-permute-done | bytes 524320 | tf_op jit(solution)/shard_map/ppermute | solution.py:589
  101.2 16.4 %shard_map.95 = (bf16[512,1024]{1,0:T(8,128)(2,1)S(1)}, bf16[512,1024]{1,0:T(8,128)(2,1)S(1)}) custom-call(bf16[512,1024]{1,0:T(8,128)(2,1)S(1)} %copy-done.10, bf16[512,1024]{1,0:T(8,128)(2,1)S(1)} %copy-done.4, bf16[256,1024]{1,0:T(8,128)(2,1)S(1)} %get-tuple-element.31.r0_ref, bf16[256,1024]{1,0:T(8,128)(2,1)S(1)} %collective-permute-done.r1_ref, ...), custom_call_target="tpu_custom_call" | custom-call | flops 11000000512 | bytes 30000000 | tf_op jit(solution)/shard_map/pallas_call | solution.py:196
  117.6 4.4 collective-permute-done.4.r2_ref
  122.0 10.2 %collective-permute-done.5.r3_ref = bf16[256,1024]{1,0:T(8,128)(2,1)S(1)} collective-permute-done((bf16[256,1024]{1,0:T(8,128)(2,1)S(1)}, bf16[256,1024]{1,0:T(8,128)(2,1)S(1)}, u32[]{:S(2)}, u32[]{:S(2)}) %collective-permute-start.5) | collective-permute-done | bytes 524320 | tf_op jit(solution)/shard_map/ppermute | solution.py:589
  132.2 16.4 %shard_map.96 = (bf16[512,1024]{1,0:T(8,128)(2,1)S(1)}, bf16[512,1024]{1,0:T(8,128)(2,1)S(1)}, f32[512,4096]{1,0:T(8,128)}, f32[512,1024]{1,0:T(8,128)}, bf16[512,1024]{1,0:T(8,128)(2,1)S(1)}) custom-call(bf16[512,1024]{1,0:T(8,128)(2,1)S(1)} %get-tuple-element.35.x_ref, bf16[512,1024]{1,0:T(8,128)(2,1)S(1)} %get-tuple-element.36.u_ref, ...), custom_call_target="tpu_custom_call" | custom-call | flops 11000000512 | bytes 30000000 | tf_op jit(solution)/shard_map/pallas_call | solution.py:196
  149.6 1.6 pad_maximum_fusion
  153.1 1.2 collective-permute-start.8
  154.5 17.9 %collective-permute-done.7.r2_ref = bf16[256,1024]{1,0:T(8,128)(2,1)S(1)} collective-permute-done((bf16[256,1024]{1,0:T(8,128)(2,1)}, bf16[256,1024]{1,0:T(8,128)(2,1)S(1)}, u32[]{:S(2)}, u32[]{:S(2)}) %collective-permute-start.7) | collective-permute-done | bytes 524320 | tf_op jit(solution)/shard_map/ppermute | solution.py:589
  172.4 19.3 %collective-permute-done.8.r3_ref = bf16[256,1024]{1,0:T(8,128)(2,1)S(1)} collective-permute-done((bf16[256,1024]{1,0:T(8,128)(2,1)}, bf16[256,1024]{1,0:T(8,128)(2,1)S(1)}, u32[]{:S(2)}, u32[]{:S(2)}) %collective-permute-start.8) | collective-permute-done | bytes 524320 | tf_op jit(solution)/shard_map/ppermute | solution.py:589
  191.7 1.2 copy-done.12
  193.0 1.0 copy-done.18
  194.0 19.8 %shard_map.97 = (bf16[512,1024]{1,0:T(8,128)(2,1)S(1)}, bf16[512,1024]{1,0:T(8,128)(2,1)}, f32[512,4096]{1,0:T(8,128)}, f32[512,1024]{1,0:T(8,128)}, bf16[512,1024]{1,0:T(8,128)(2,1)S(1)}) custom-call(bf16[512,1024]{1,0:T(8,128)(2,1)S(1)} %get-tuple-element.41.x_ref, bf16[512,1024]{1,0:T(8,128)(2,1)S(1)} %copy-done.12, bf16[256,1024]{1,0:T(8,128)(2,1)S(1)} %copy-done.18, ...), custom_call_target="tpu_custom_call" | custom-call | flops 11000000512 | bytes 30000000 | tf_op jit(solution)/shard_map/pallas_call | solution.py:196
  213.9 19.7 %shard_map.98 = (bf16[512,1024]{1,0:T(8,128)(2,1)S(1)}, bf16[512,1024]{1,0:T(8,128)(2,1)S(1)}) custom-call(bf16[512,1024]{1,0:T(8,128)(2,1)S(1)} %copy-done.14, bf16[512,1024]{1,0:T(8,128)(2,1)S(1)} %fusion.6.dm_ref.rest_0_, bf16[512,1024]{1,0:T(8,128)(2,1)S(1)} %get-tuple-element.41.x_ref, bf16[512,1024]{1,0:T(8,128)(2,1)S(1)} %get-tuple-element.48.got_ref, ...), custom_call_target="tpu_custom_call" | custom-call | flops 11000000512 | bytes 40000000 | tf_op jit(solution)/shard_map/pallas_call | solution.py:275
  233.7 24.5 %shard_map.99 = (bf16[512,1024]{1,0:T(8,128)(2,1)}, bf16[512,1024]{1,0:T(8,128)(2,1)}) custom-call(bf16[512,1024]{1,0:T(8,128)(2,1)S(1)} %get-tuple-element.51.cot_ref, bf16[512,1024]{1,0:T(8,128)(2,1)S(1)} %get-tuple-element.52.dm_ref.rest_0_, bf16[512,1024]{1,0:T(8,128)(2,1)S(1)} %copy-done.8, bf16[512,1024]{1,0:T(8,128)(2,1)S(1)} %copy-done.16, ...), custom_call_target="tpu_custom_call" | custom-call | flops 11000000512 | bytes 40000000 | tf_op jit(solution)/shard_map/pallas_call | solution.py:275
  258.2 1.7 collective-permute-start.26
  260.0 3.0 collective-permute-start.24
  263.7 43.2 %collective-permute-done.26.rest_3_ = bf16[512,1024]{1,0:T(8,128)(2,1)} collective-permute-done((bf16[512,1024]{1,0:T(8,128)(2,1)S(1)}, bf16[512,1024]{1,0:T(8,128)(2,1)}, u32[]{:S(2)}, u32[]{:S(2)}) %collective-permute-start.26) | collective-permute-done | bytes 1048608 | tf_op jit(solution)/shard_map/ppermute | solution.py:589
  306.9 1.3 collective-permute-done.25.rest_2_
  308.2 2.0 collective-permute-start.9
  311.2 28.3 %collective-permute-done.11.rest_3_ = bf16[512,1024]{1,0:T(8,128)(2,1)S(1)} collective-permute-done((bf16[512,1024]{1,0:T(8,128)(2,1)S(1)}, bf16[512,1024]{1,0:T(8,128)(2,1)S(1)}, u32[]{:S(2)}, u32[]{:S(2)}) %collective-permute-start.11) | collective-permute-done | bytes 1048608 | tf_op jit(solution)/shard_map/ppermute | solution.py:589
  342.6 1.6 collective-permute-start.27
  344.4 25.6 %collective-permute-done.28.rest_5_ = bf16[512,1024]{1,0:T(8,128)(2,1)} collective-permute-done((bf16[512,1024]{1,0:T(8,128)(2,1)}, bf16[512,1024]{1,0:T(8,128)(2,1)}, u32[]{:S(2)}, u32[]{:S(2)}) %collective-permute-start.28) | collective-permute-done | bytes 1048608 | tf_op jit(solution)/shard_map/ppermute | solution.py:589
  370.0 3.4 collective-permute-done.29.rest_6_
  373.4 1.4 collective-permute-start.13
  375.7 5.6 sort.7
  382.0 25.4 %collective-permute-done.27.rest_4_ = bf16[512,1024]{1,0:T(8,128)(2,1)} collective-permute-done((bf16[512,1024]{1,0:T(8,128)(2,1)}, bf16[512,1024]{1,0:T(8,128)(2,1)}, u32[]{:S(2)}, u32[]{:S(2)}) %collective-permute-start.27) | collective-permute-done | bytes 1048608 | tf_op jit(solution)/shard_map/ppermute | solution.py:589
  407.4 1.4 collective-permute-start.14
  410.0 39.8 %collective-permute-done.13.rest_5_ = bf16[512,1024]{1,0:T(8,128)(2,1)} collective-permute-done((bf16[512,1024]{1,0:T(8,128)(2,1)}, bf16[512,1024]{1,0:T(8,128)(2,1)}, u32[]{:S(2)}, u32[]{:S(2)}) %collective-permute-start.13) | collective-permute-done | bytes 1048608 | tf_op jit(solution)/shard_map/ppermute | solution.py:589
  449.7 1.3 collective-permute-start.30
  451.4 1.7 convolution_convert_fusion
  453.2 28.7 %collective-permute-done.12.rest_4_ = bf16[512,1024]{1,0:T(8,128)(2,1)} collective-permute-done((bf16[512,1024]{1,0:T(8,128)(2,1)}, bf16[512,1024]{1,0:T(8,128)(2,1)}, u32[]{:S(2)}, u32[]{:S(2)}) %collective-permute-start.12) | collective-permute-done | bytes 1048608 | tf_op jit(solution)/shard_map/ppermute | solution.py:589
  482.4 1.5 collective-permute-start.15
  484.3 2.8 copy-done.2
  487.1 16.9 %shard_map.100.g_hbm = f32[544,8,8,128]{3,2,1,0:T(8,128)} custom-call(s32[65]{0:T(128)S(1)} %concatenate.9.meta_ref, bf16[8192,1024]{1,0:T(8,128)(2,1)} %all-gather.4.cloned.1.call-done.u_hbm, bf16[3,1024,1024]{2,1,0:T(8,128)(2,1)S(1)} %copy-done.2), custom_call_target="tpu_custom_call" | custom-call | flops 10000000000 | bytes 30000000 | tf_op jit(solution)/shard_map/pallas_call | solution.py:430
  504.0 2.8 copy-done.3
  506.8 17.2 %shard_map.102.g_hbm = f32[544,8,8,128]{3,2,1,0:T(8,128)} custom-call(s32[65]{0:T(128)S(1)} %concatenate.9.meta_ref, bf16[8192,2048]{1,0:T(8,128)(2,1)} %all-gather.8.cloned.1.call-done.u_hbm, bf16[3,1024,1024]{2,1,0:T(8,128)(2,1)S(1)} %copy-done.3), custom_call_target="tpu_custom_call" | custom-call | flops 10000000000 | bytes 30000000 | tf_op jit(solution)/shard_map/pallas_call | solution.py:430
  525.2 37.0 %shard_map.103.rest_16_ = f32[3,2048,8,8,128]{4,3,2,1,0:T(8,128)} custom-call(s32[65]{0:T(128)S(1)} %concatenate.9.meta_ref, s32[17]{0:T(128)S(1)} %convert_reduce_fusion.2.tile_ref, s32[4096]{0:T(1024)S(1)} %fusion.18.addr_ref, f32[544,8,8,128]{3,2,1,0:T(8,128)} %shard_map.102.g_hbm, bf16[512,1024]{1,0:T(8,128)(2,1)} %copy-done.5, ...), custom_call_target="tpu_custom_call" | custom-call | flops 40000000000 | bytes 100000000 | tf_op jit(solution)/shard_map/pallas_call | solution.py:537
  562.2 17.1 %shard_map.101.g_hbm = f32[544,8,8,128]{3,2,1,0:T(8,128)} custom-call(s32[65]{0:T(128)S(1)} %concatenate.9.meta_ref, bf16[8192,2048]{1,0:T(8,128)(2,1)} %all-gather.8.cloned.1.call-done.u_hbm, bf16[3,1024,1024]{2,1,0:T(8,128)(2,1)S(1)} %bitcast.42), custom_call_target="tpu_custom_call" | custom-call | flops 10000000000 | bytes 30000000 | tf_op jit(solution)/shard_map/pallas_call | solution.py:430
  582.4 37.0 %shard_map.104.rest_1_ = f32[3,2048,8,8,128]{4,3,2,1,0:T(8,128)} custom-call(s32[65]{0:T(128)S(1)} %concatenate.9.meta_ref, s32[17]{0:T(128)S(1)} %convert_reduce_fusion.2.tile_ref, s32[4096]{0:T(1024)S(1)} %fusion.18.addr_ref, f32[544,8,8,128]{3,2,1,0:T(8,128)} %shard_map.101.g_hbm, bf16[512,1024]{1,0:T(8,128)(2,1)} %copy-done.6, ...), custom_call_target="tpu_custom_call", output_to_operand_aliasing={{}: (20, {})} | custom-call | flops 40000000000 | bytes 100000000 | tf_op jit(solution)/shard_map/pallas_call | solution.py:537
  619.4 37.0 %shard_map.105 = f32[3,2048,8,8,128]{4,3,2,1,0:T(8,128)} custom-call(s32[65]{0:T(128)S(1)} %concatenate.9.meta_ref, s32[17]{0:T(128)S(1)} %convert_reduce_fusion.2.tile_ref, s32[4096]{0:T(1024)S(1)} %fusion.18.addr_ref, f32[544,8,8,128]{3,2,1,0:T(8,128)} %shard_map.100.g_hbm, ...), custom_call_target="tpu_custom_call", output_to_operand_aliasing={{}: (5, {})} | custom-call | flops 40000000000 | bytes 100000000 | tf_op jit(solution)/shard_map/pallas_call | solution.py:537
  (177 shorter events, 24.5 us)
Async XLA Ops:
  7.2 446.0 %all-gather.4.cloned.1.call-start = ((), (), s32[]{:S(2)}) async-start(), calls=%async_computation | async-start | bytes 17825792 | tf_op jit(solution)/shard_map/all_gather | solution.py:574
  11.5 492.5 %all-gather.8.cloned.1.call-start = ((), (), s32[]{:S(2)}) async-start(), calls=%async_computation.2 | async-start | bytes 35651584 | tf_op jit(solution)/shard_map/all_gather | solution.py:574
  16.3 246.7 %copy-start.5 = (bf16[512,1024]{1,0:T(8,128)(2,1)}, bf16[512,1024]{1,0:T(8,128)(2,1)S(1)}, u32[]{:S(2)}) copy-start(bf16[512,1024]{1,0:T(8,128)(2,1)S(1)} %fusion.6.dm_ref.rest_0_) | copy-start | bytes 3145732
  28.9 72.2 %copy-start.10 = (bf16[512,1024]{1,0:T(8,128)(2,1)S(1)}, bf16[512,1024]{1,0:T(8,128)(2,1)}, u32[]{:S(2)}) copy-start(bf16[512,1024]{1,0:T(8,128)(2,1)} %copy-done.9) | copy-start | bytes 3145732
  54.7 2.8 collective-permute-start
  54.8 26.0 %collective-permute-start.1 = (bf16[256,1024]{1,0:T(8,128)(2,1)S(1)}, bf16[256,1024]{1,0:T(8,128)(2,1)S(1)}, u32[]{:S(2)}, u32[]{:S(2)}) collective-permute-start(bf16[256,1024]{1,0:T(8,128)(2,1)S(1)} %get-tuple-element.33), channel_id=1, source_target_pairs={{0,2},{1,3},{2,0},{3,1},{4,6},{5,7},{6,4},{7,5},{8,10},{9,11},{10,... | collective-permute-start | bytes 1572872 | tf_op jit(solution)/shard_map/ppermute | solution.py:589
  54.8 46.4 %collective-permute-start.2 = (bf16[256,1024]{1,0:T(8,128)(2,1)S(1)}, bf16[256,1024]{1,0:T(8,128)(2,1)S(1)}, u32[]{:S(2)}, u32[]{:S(2)}) collective-permute-start(bf16[256,1024]{1,0:T(8,128)(2,1)S(1)} %get-tuple-element.34), channel_id=1, source_target_pairs={{0,3},{1,2},{2,1},{3,0},{4,7},{5,6},{6,5},{7,4},{8,11},{9,10},{10,... | collective-permute-start | bytes 1572872 | tf_op jit(solution)/shard_map/ppermute | solution.py:589
  56.6 61.0 %collective-permute-start.3 = (bf16[256,1024]{1,0:T(8,128)(2,1)S(1)}, bf16[256,1024]{1,0:T(8,128)(2,1)S(1)}, u32[]{:S(2)}, u32[]{:S(2)}) collective-permute-start(bf16[256,1024]{1,0:T(8,128)(2,1)S(1)} %get-tuple-element.38), channel_id=1, source_target_pairs={{0,1},{1,0},{2,3},{3,2},{4,5},{5,4},{6,7},{7,6},{8,9},{9,8},{10,11... | collective-permute-start | bytes 1572872 | tf_op jit(solution)/shard_map/ppermute | solution.py:589
  56.9 65.1 %collective-permute-start.4 = (bf16[256,1024]{1,0:T(8,128)(2,1)S(1)}, bf16[256,1024]{1,0:T(8,128)(2,1)S(1)}, u32[]{:S(2)}, u32[]{:S(2)}) collective-permute-start(bf16[256,1024]{1,0:T(8,128)(2,1)S(1)} %get-tuple-element.39), channel_id=1, source_target_pairs={{0,2},{1,3},{2,0},{3,1},{4,6},{5,7},{6,4},{7,5},{8,10},{9,11},{10,... | collective-permute-start | bytes 1572872 | tf_op jit(solution)/shard_map/ppermute | solution.py:589
  57.6 74.7 %collective-permute-start.5 = (bf16[256,1024]{1,0:T(8,128)(2,1)S(1)}, bf16[256,1024]{1,0:T(8,128)(2,1)S(1)}, u32[]{:S(2)}, u32[]{:S(2)}) collective-permute-start(bf16[256,1024]{1,0:T(8,128)(2,1)S(1)} %get-tuple-element.40), channel_id=1, source_target_pairs={{0,3},{1,2},{2,1},{3,0},{4,7},{5,6},{6,5},{7,4},{8,11},{9,10},{10,... | collective-permute-start | bytes 1572872 | tf_op jit(solution)/shard_map/ppermute | solution.py:589
  152.2 467.2 %all-gather.6.cloned.1.call-start = ((), (), s32[]{:S(2)}) async-start(), calls=%async_computation.1 | async-start | bytes 17825792 | tf_op jit(solution)/shard_map/all_gather | solution.py:574
  152.4 2.2 collective-permute-start.6
  152.7 19.7 %collective-permute-start.7 = (bf16[256,1024]{1,0:T(8,128)(2,1)}, bf16[256,1024]{1,0:T(8,128)(2,1)S(1)}, u32[]{:S(2)}, u32[]{:S(2)}) collective-permute-start(bf16[256,1024]{1,0:T(8,128)(2,1)} %copy-done.21), channel_id=1, source_target_pairs={{0,2},{1,3},{2,0},{3,1},{4,6},{5,7},{6,4},{7,5},{8,10},{9,11},{10,... | collective-permute-start | bytes 1572872 | tf_op jit(solution)/shard_map/ppermute | solution.py:589
  153.1 38.7 %collective-permute-start.8 = (bf16[256,1024]{1,0:T(8,128)(2,1)}, bf16[256,1024]{1,0:T(8,128)(2,1)S(1)}, u32[]{:S(2)}, u32[]{:S(2)}) collective-permute-start(bf16[256,1024]{1,0:T(8,128)(2,1)} %get-tuple-element.46), channel_id=1, source_target_pairs={{0,3},{1,2},{2,1},{3,0},{4,7},{5,6},{6,5},{7,4},{8,11},{9,10},{10,... | collective-permute-start | bytes 1572872 | tf_op jit(solution)/shard_map/ppermute | solution.py:589
  233.6 76.6 %copy-start.6 = (bf16[512,1024]{1,0:T(8,128)(2,1)}, bf16[512,1024]{1,0:T(8,128)(2,1)S(1)}, u32[]{:S(2)}) copy-start(bf16[512,1024]{1,0:T(8,128)(2,1)S(1)} %get-tuple-element.52.dm_ref.rest_0_) | copy-start | bytes 3145732
  233.6 107.5 %copy-start.36 = (s32[16,4,128]{2,1,0:T(4,128)S(1)}, s32[16,4,128]{2,1,0:T(4,128)}, u32[]{:S(2)}) copy-start(s32[16,4,128]{2,1,0:T(4,128)} %share_ids.1) | copy-start | bytes 98308
  233.6 217.8 %copy-start.20 = (bf16[512,1024]{1,0:T(8,128)(2,1)S(1)}, bf16[512,1024]{1,0:T(8,128)(2,1)}, u32[]{:S(2)}) copy-start(bf16[512,1024]{1,0:T(8,128)(2,1)} %copy-done.19) | copy-start | bytes 3145732
  258.2 48.6 %collective-permute-start.26 = (bf16[512,1024]{1,0:T(8,128)(2,1)S(1)}, bf16[512,1024]{1,0:T(8,128)(2,1)}, u32[]{:S(2)}, u32[]{:S(2)}) collective-permute-start(bf16[512,1024]{1,0:T(8,128)(2,1)S(1)} %fusion.6.dm_ref.rest_0_), channel_id=1, source_target_pairs={{0,2},{1,3},{2,0},{3,1},{4,6},{5,7},{6,4},{7,5},{8,10},{9,11},{10,... | collective-permute-start | bytes 3145736 | tf_op jit(solution)/shard_map/ppermute | solution.py:589
  260.0 48.2 %collective-permute-start.25 = (bf16[512,1024]{1,0:T(8,128)(2,1)S(1)}, bf16[512,1024]{1,0:T(8,128)(2,1)S(1)}, u32[]{:S(2)}, u32[]{:S(2)}) collective-permute-start(bf16[512,1024]{1,0:T(8,128)(2,1)S(1)} %fusion.6.dm_ref.rest_0_), channel_id=1, source_target_pairs={{0,4},{4,0},{8,12},{12,8},{1,5},{5,1},{9,13},{13,9},{2,6},{6,2},{1... | collective-permute-start | bytes 3145736 | tf_op jit(solution)/shard_map/ppermute | solution.py:589
  260.0 50.3 %collective-permute-start.24 = (bf16[512,1024]{1,0:T(8,128)(2,1)S(1)}, bf16[512,1024]{1,0:T(8,128)(2,1)S(1)}, u32[]{:S(2)}, u32[]{:S(2)}) collective-permute-start(bf16[512,1024]{1,0:T(8,128)(2,1)S(1)} %fusion.6.dm_ref.rest_0_), channel_id=1, source_target_pairs={{0,8},{4,12},{8,0},{12,4},{1,9},{5,13},{9,1},{13,5},{2,10},{6,14},... | collective-permute-start | bytes 3145736 | tf_op jit(solution)/shard_map/ppermute | solution.py:589
  263.0 47.3 %collective-permute-start.31 = (bf16[512,1024]{1,0:T(8,128)(2,1)S(1)}, bf16[512,1024]{1,0:T(8,128)(2,1)S(1)}, u32[]{:S(2)}, u32[]{:S(2)}) collective-permute-start(bf16[512,1024]{1,0:T(8,128)(2,1)S(1)} %fusion.6.dm_ref.rest_0_), channel_id=1, source_target_pairs={{0,1},{1,0},{2,3},{3,2},{4,5},{5,4},{6,7},{7,6},{8,9},{9,8},{10,11... | collective-permute-start | bytes 3145736 | tf_op jit(solution)/shard_map/ppermute | solution.py:589
  263.0 76.4 %collective-permute-start.11 = (bf16[512,1024]{1,0:T(8,128)(2,1)S(1)}, bf16[512,1024]{1,0:T(8,128)(2,1)S(1)}, u32[]{:S(2)}, u32[]{:S(2)}) collective-permute-start(bf16[512,1024]{1,0:T(8,128)(2,1)S(1)} %get-tuple-element.52.dm_ref.rest_0_), channel_id=1, source_target_pairs={{0,2},{1,3},{2,0},{3,1},{4,6},{5,7},{6,4},{7,5},{8,10},{9,11},{10,... | collective-permute-start | bytes 3145736 | tf_op jit(solution)/shard_map/ppermute | solution.py:589
  306.9 34.9 %collective-permute-start.10 = (bf16[512,1024]{1,0:T(8,128)(2,1)S(1)}, bf16[512,1024]{1,0:T(8,128)(2,1)}, u32[]{:S(2)}, u32[]{:S(2)}) collective-permute-start(bf16[512,1024]{1,0:T(8,128)(2,1)S(1)} %get-tuple-element.52.dm_ref.rest_0_), channel_id=1, source_target_pairs={{0,4},{4,0},{8,12},{12,8},{1,5},{5,1},{9,13},{13,9},{2,6},{6,2},{1... | collective-permute-start | bytes 3145736 | tf_op jit(solution)/shard_map/ppermute | solution.py:589
  308.2 34.4 %collective-permute-start.9 = (bf16[512,1024]{1,0:T(8,128)(2,1)S(1)}, bf16[512,1024]{1,0:T(8,128)(2,1)}, u32[]{:S(2)}, u32[]{:S(2)}) collective-permute-start(bf16[512,1024]{1,0:T(8,128)(2,1)S(1)} %get-tuple-element.52.dm_ref.rest_0_), channel_id=1, source_target_pairs={{0,8},{4,12},{8,0},{12,4},{1,9},{5,13},{9,1},{13,5},{2,10},{6,14},... | collective-permute-start | bytes 3145736 | tf_op jit(solution)/shard_map/ppermute | solution.py:589
  310.2 33.9 %collective-permute-start.16 = (bf16[512,1024]{1,0:T(8,128)(2,1)S(1)}, bf16[512,1024]{1,0:T(8,128)(2,1)}, u32[]{:S(2)}, u32[]{:S(2)}) collective-permute-start(bf16[512,1024]{1,0:T(8,128)(2,1)S(1)} %get-tuple-element.52.dm_ref.rest_0_), channel_id=1, source_target_pairs={{0,1},{1,0},{2,3},{3,2},{4,5},{5,4},{6,7},{7,6},{8,9},{9,8},{10,11... | collective-permute-start | bytes 3145736 | tf_op jit(solution)/shard_map/ppermute | solution.py:589
  310.3 59.7 %collective-permute-start.28 = (bf16[512,1024]{1,0:T(8,128)(2,1)}, bf16[512,1024]{1,0:T(8,128)(2,1)}, u32[]{:S(2)}, u32[]{:S(2)}) collective-permute-start(bf16[512,1024]{1,0:T(8,128)(2,1)} %collective-permute-done.26.rest_3_), channel_id=1, source_target_pairs={{0,8},{4,12},{8,0},{12,4},{1,9},{5,13},{9,1},{13,5},{2,10},{6,14},... | collective-permute-start | bytes 3145736 | tf_op jit(solution)/shard_map/ppermute | solution.py:589
  340.5 32.9 %collective-permute-start.29 = (bf16[512,1024]{1,0:T(8,128)(2,1)}, bf16[512,1024]{1,0:T(8,128)(2,1)}, u32[]{:S(2)}, u32[]{:S(2)}) collective-permute-start(bf16[512,1024]{1,0:T(8,128)(2,1)} %collective-permute-done.26.rest_3_), channel_id=1, source_target_pairs={{0,4},{4,0},{8,12},{12,8},{1,5},{5,1},{9,13},{13,9},{2,6},{6,2},{1... | collective-permute-start | bytes 3145736 | tf_op jit(solution)/shard_map/ppermute | solution.py:589
  341.8 67.0 %collective-permute-start.34 = (bf16[512,1024]{1,0:T(8,128)(2,1)}, bf16[512,1024]{1,0:T(8,128)(2,1)S(1)}, u32[]{:S(2)}, u32[]{:S(2)}) collective-permute-start(bf16[512,1024]{1,0:T(8,128)(2,1)} %collective-permute-done.26.rest_3_), channel_id=1, source_target_pairs={{0,1},{1,0},{2,3},{3,2},{4,5},{5,4},{6,7},{7,6},{8,9},{9,8},{10,11... | collective-permute-start | bytes 3145736 | tf_op jit(solution)/shard_map/ppermute | solution.py:589
  342.6 64.8 %collective-permute-start.27 = (bf16[512,1024]{1,0:T(8,128)(2,1)}, bf16[512,1024]{1,0:T(8,128)(2,1)}, u32[]{:S(2)}, u32[]{:S(2)}) collective-permute-start(bf16[512,1024]{1,0:T(8,128)(2,1)} %copy-done.25), channel_id=1, source_target_pairs={{0,8},{4,12},{8,0},{12,4},{1,9},{5,13},{9,1},{13,5},{2,10},{6,14},... | collective-permute-start | bytes 3145736 | tf_op jit(solution)/shard_map/ppermute | solution.py:589
  344.2 65.3 %collective-permute-start.33 = (bf16[512,1024]{1,0:T(8,128)(2,1)}, bf16[512,1024]{1,0:T(8,128)(2,1)}, u32[]{:S(2)}, u32[]{:S(2)}) collective-permute-start(bf16[512,1024]{1,0:T(8,128)(2,1)} %copy-done.25), channel_id=1, source_target_pairs={{0,1},{1,0},{2,3},{3,2},{4,5},{5,4},{6,7},{7,6},{8,9},{9,8},{10,11... | collective-permute-start | bytes 3145736 | tf_op jit(solution)/shard_map/ppermute | solution.py:589
  370.0 39.5 %collective-permute-start.32 = (bf16[512,1024]{1,0:T(8,128)(2,1)}, bf16[512,1024]{1,0:T(8,128)(2,1)}, u32[]{:S(2)}, u32[]{:S(2)}) collective-permute-start(bf16[512,1024]{1,0:T(8,128)(2,1)} %copy-done.26), channel_id=1, source_target_pairs={{0,1},{1,0},{2,3},{3,2},{4,5},{5,4},{6,7},{7,6},{8,9},{9,8},{10,11... | collective-permute-start | bytes 3145736 | tf_op jit(solution)/shard_map/ppermute | solution.py:589
  373.4 76.3 %collective-permute-start.13 = (bf16[512,1024]{1,0:T(8,128)(2,1)}, bf16[512,1024]{1,0:T(8,128)(2,1)}, u32[]{:S(2)}, u32[]{:S(2)}) collective-permute-start(bf16[512,1024]{1,0:T(8,128)(2,1)} %copy-done.23), channel_id=1, source_target_pairs={{0,8},{4,12},{8,0},{12,4},{1,9},{5,13},{9,1},{13,5},{2,10},{6,14},... | collective-permute-start | bytes 3145736 | tf_op jit(solution)/shard_map/ppermute | solution.py:589
  407.4 74.5 %collective-permute-start.14 = (bf16[512,1024]{1,0:T(8,128)(2,1)}, bf16[512,1024]{1,0:T(8,128)(2,1)}, u32[]{:S(2)}, u32[]{:S(2)}) collective-permute-start(bf16[512,1024]{1,0:T(8,128)(2,1)} %copy-done.23), channel_id=1, source_target_pairs={{0,4},{4,0},{8,12},{12,8},{1,5},{5,1},{9,13},{13,9},{2,6},{6,2},{1... | collective-permute-start | bytes 3145736 | tf_op jit(solution)/shard_map/ppermute | solution.py:589
  408.8 95.2 %copy-start.28 = (bf16[512,1024]{1,0:T(8,128)(2,1)}, bf16[512,1024]{1,0:T(8,128)(2,1)S(1)}, u32[]{:S(2)}) copy-start(bf16[512,1024]{1,0:T(8,128)(2,1)S(1)} %collective-permute-done.34.rest_11_) | copy-start | bytes 3145732
  408.8 73.1 %collective-permute-start.12 = (bf16[512,1024]{1,0:T(8,128)(2,1)}, bf16[512,1024]{1,0:T(8,128)(2,1)}, u32[]{:S(2)}, u32[]{:S(2)}) collective-permute-start(bf16[512,1024]{1,0:T(8,128)(2,1)} %collective-permute-done.10.rest_2_), channel_id=1, source_target_pairs={{0,8},{4,12},{8,0},{12,4},{1,9},{5,13},{9,1},{13,5},{2,10},{6,14},... | collective-permute-start | bytes 3145736 | tf_op jit(solution)/shard_map/ppermute | solution.py:589
  409.5 73.0 %collective-permute-start.18 = (bf16[512,1024]{1,0:T(8,128)(2,1)}, bf16[512,1024]{1,0:T(8,128)(2,1)}, u32[]{:S(2)}, u32[]{:S(2)}) collective-permute-start(bf16[512,1024]{1,0:T(8,128)(2,1)} %collective-permute-done.10.rest_2_), channel_id=1, source_target_pairs={{0,1},{1,0},{2,3},{3,2},{4,5},{5,4},{6,7},{7,6},{8,9},{9,8},{10,11... | collective-permute-start | bytes 3145736 | tf_op jit(solution)/shard_map/ppermute | solution.py:589
  409.5 72.9 %collective-permute-start.17 = (bf16[512,1024]{1,0:T(8,128)(2,1)}, bf16[512,1024]{1,0:T(8,128)(2,1)}, u32[]{:S(2)}, u32[]{:S(2)}) collective-permute-start(bf16[512,1024]{1,0:T(8,128)(2,1)} %collective-permute-done.9.rest_1_), channel_id=1, source_target_pairs={{0,1},{1,0},{2,3},{3,2},{4,5},{5,4},{6,7},{7,6},{8,9},{9,8},{10,11... | collective-permute-start | bytes 3145736 | tf_op jit(solution)/shard_map/ppermute | solution.py:589
  449.7 34.6 %collective-permute-start.30 = (bf16[512,1024]{1,0:T(8,128)(2,1)}, bf16[512,1024]{1,0:T(8,128)(2,1)}, u32[]{:S(2)}, u32[]{:S(2)}) collective-permute-start(bf16[512,1024]{1,0:T(8,128)(2,1)} %collective-permute-done.28.rest_5_), channel_id=1, source_target_pairs={{0,4},{4,0},{8,12},{12,8},{1,5},{5,1},{9,13},{13,9},{2,6},{6,2},{1... | collective-permute-start | bytes 3145736 | tf_op jit(solution)/shard_map/ppermute | solution.py:589
  481.9 42.2 %collective-permute-start.36 = (bf16[512,1024]{1,0:T(8,128)(2,1)}, bf16[512,1024]{1,0:T(8,128)(2,1)S(1)}, u32[]{:S(2)}, u32[]{:S(2)}) collective-permute-start(bf16[512,1024]{1,0:T(8,128)(2,1)} %collective-permute-done.28.rest_5_), channel_id=1, source_target_pairs={{0,1},{1,0},{2,3},{3,2},{4,5},{5,4},{6,7},{7,6},{8,9},{9,8},{10,11... | collective-permute-start | bytes 3145736 | tf_op jit(solution)/shard_map/ppermute | solution.py:589
  481.9 42.2 %collective-permute-start.37 = (bf16[512,1024]{1,0:T(8,128)(2,1)}, bf16[512,1024]{1,0:T(8,128)(2,1)}, u32[]{:S(2)}, u32[]{:S(2)}) collective-permute-start(bf16[512,1024]{1,0:T(8,128)(2,1)} %collective-permute-done.29.rest_6_), channel_id=1, source_target_pairs={{0,1},{1,0},{2,3},{3,2},{4,5},{5,4},{6,7},{7,6},{8,9},{9,8},{10,11... | collective-permute-start | bytes 3145736 | tf_op jit(solution)/shard_map/ppermute | solution.py:589
  482.4 42.2 %collective-permute-start.35 = (bf16[512,1024]{1,0:T(8,128)(2,1)}, bf16[512,1024]{1,0:T(8,128)(2,1)}, u32[]{:S(2)}, u32[]{:S(2)}) collective-permute-start(bf16[512,1024]{1,0:T(8,128)(2,1)} %collective-permute-done.27.rest_4_), channel_id=1, source_target_pairs={{0,1},{1,0},{2,3},{3,2},{4,5},{5,4},{6,7},{7,6},{8,9},{9,8},{10,11... | collective-permute-start | bytes 3145736 | tf_op jit(solution)/shard_map/ppermute | solution.py:589
  482.4 42.2 %collective-permute-start.15 = (bf16[512,1024]{1,0:T(8,128)(2,1)}, bf16[512,1024]{1,0:T(8,128)(2,1)S(1)}, u32[]{:S(2)}, u32[]{:S(2)}) collective-permute-start(bf16[512,1024]{1,0:T(8,128)(2,1)} %collective-permute-done.13.rest_5_), channel_id=1, source_target_pairs={{0,4},{4,0},{8,12},{12,8},{1,5},{5,1},{9,13},{13,9},{2,6},{6,2},{1... | collective-permute-start | bytes 3145736 | tf_op jit(solution)/shard_map/ppermute | solution.py:589
  484.3 40.8 %collective-permute-start.38 = (bf16[512,1024]{1,0:T(8,128)(2,1)}, bf16[512,1024]{1,0:T(8,128)(2,1)}, u32[]{:S(2)}, u32[]{:S(2)}) collective-permute-start(bf16[512,1024]{1,0:T(8,128)(2,1)} %collective-permute-done.30.rest_7_), channel_id=1, source_target_pairs={{0,1},{1,0},{2,3},{3,2},{4,5},{5,4},{6,7},{7,6},{8,9},{9,8},{10,11... | collective-permute-start | bytes 3145736 | tf_op jit(solution)/shard_map/ppermute | solution.py:589
  524.1 55.2 %collective-permute-start.19 = (bf16[512,1024]{1,0:T(8,128)(2,1)S(1)}, bf16[512,1024]{1,0:T(8,128)(2,1)S(1)}, u32[]{:S(2)}, u32[]{:S(2)}) collective-permute-start(bf16[512,1024]{1,0:T(8,128)(2,1)S(1)} %copy-done.24), channel_id=1, source_target_pairs={{0,1},{1,0},{2,3},{3,2},{4,5},{5,4},{6,7},{7,6},{8,9},{9,8},{10,11... | collective-permute-start | bytes 3145736 | tf_op jit(solution)/shard_map/ppermute | solution.py:589
  524.1 55.2 %collective-permute-start.21 = (bf16[512,1024]{1,0:T(8,128)(2,1)}, bf16[512,1024]{1,0:T(8,128)(2,1)S(1)}, u32[]{:S(2)}, u32[]{:S(2)}) collective-permute-start(bf16[512,1024]{1,0:T(8,128)(2,1)} %collective-permute-done.13.rest_5_), channel_id=1, source_target_pairs={{0,1},{1,0},{2,3},{3,2},{4,5},{5,4},{6,7},{7,6},{8,9},{9,8},{10,11... | collective-permute-start | bytes 3145736 | tf_op jit(solution)/shard_map/ppermute | solution.py:589
  524.6 54.7 %collective-permute-start.20 = (bf16[512,1024]{1,0:T(8,128)(2,1)}, bf16[512,1024]{1,0:T(8,128)(2,1)S(1)}, u32[]{:S(2)}, u32[]{:S(2)}) collective-permute-start(bf16[512,1024]{1,0:T(8,128)(2,1)} %collective-permute-done.12.rest_4_), channel_id=1, source_target_pairs={{0,1},{1,0},{2,3},{3,2},{4,5},{5,4},{6,7},{7,6},{8,9},{9,8},{10,11... | collective-permute-start | bytes 3145736 | tf_op jit(solution)/shard_map/ppermute | solution.py:589
  524.7 54.7 %collective-permute-start.22 = (bf16[512,1024]{1,0:T(8,128)(2,1)}, bf16[512,1024]{1,0:T(8,128)(2,1)S(1)}, u32[]{:S(2)}, u32[]{:S(2)}) collective-permute-start(bf16[512,1024]{1,0:T(8,128)(2,1)} %collective-permute-done.14.rest_6_), channel_id=1, source_target_pairs={{0,1},{1,0},{2,3},{3,2},{4,5},{5,4},{6,7},{7,6},{8,9},{9,8},{10,11... | collective-permute-start | bytes 3145736 | tf_op jit(solution)/shard_map/ppermute | solution.py:589
  525.1 54.3 %collective-permute-start.23 = (bf16[512,1024]{1,0:T(8,128)(2,1)S(1)}, bf16[512,1024]{1,0:T(8,128)(2,1)S(1)}, u32[]{:S(2)}, u32[]{:S(2)}) collective-permute-start(bf16[512,1024]{1,0:T(8,128)(2,1)S(1)} %collective-permute-done.15.rest_7_), channel_id=1, source_target_pairs={{0,1},{1,0},{2,3},{3,2},{4,5},{5,4},{6,7},{7,6},{8,9},{9,8},{10,11... | collective-permute-start | bytes 3145736 | tf_op jit(solution)/shard_map/ppermute | solution.py:589
  (36 other events, 703.8 us)
Sparse Core Ops, SparseCore 0:
  11.6 108.8 all-gather.3
  152.3 178.4 all-gather.7
  333.0 139.6 all-gather.5

commit v5 on v4

--- a/solution.py
+++ b/solution.py
@@ -579,34 +579,33 @@
         perm_mask = rank[None, :] == pos[:, None]
         perm = perm_mask.astype(BF)
         x = jnp.dot(perm, resid_in, preferred_element_type=F32).astype(BF)
-        cot = jnp.dot(perm, cot_out, preferred_element_type=F32).astype(BF)
         normed = rms_norm(x.astype(F32)).astype(BF)
-        d_mixed = lax.dot_general(cot, w_proj[last], (((1,), (1,)), ((), ())), preferred_element_type=F32).astype(BF)
-        set_a = gather(normed)
+        u_sets = [gather(normed)]
 
         def flip(block, axis, bit):
             n = mesh.shape[axis]
             return lax.ppermute(block, axis, [(i, i ^ bit) for i in range(n)])
 
-        def spread(block):
+        def spread(block, x_heavy):
             at = {(0, 0, 0): block}
             at[1, 0, 0] = flip(block, 'emb', 2)
             at[0, 1, 0] = flip(block, 'dp', 1)
             at[0, 0, 1] = flip(block, 'dp', 2)
             at[0, 1, 1] = flip(at[0, 1, 0], 'dp', 2)
-            at[1, 0, 1] = flip(at[1, 0, 0], 'dp', 2)
-            at[1, 1, 0] = flip(at[1, 0, 0], 'dp', 1)
+            if x_heavy:
+                at[1, 0, 1] = flip(at[0, 0, 1], 'emb', 2)
+                at[1, 1, 0] = flip(at[0, 1, 0], 'emb', 2)
+            else:
+                at[1, 0, 1] = flip(at[1, 0, 0], 'dp', 2)
+                at[1, 1, 0] = flip(at[1, 0, 0], 'dp', 1)
             at[1, 1, 1] = flip(at[1, 0, 1], 'dp', 1)
             offsets = sorted(at, key=lambda o: (sum(o), o))
             blocks = [at[o] for o in offsets] + [flip(at[o], 'emb', 1) for o in offsets]
             places = [((o[2] * 2 + o[1]), (o[0] * 2 + c)) for c in range(2) for o in offsets]
             return blocks, places
 
-        d2_blocks, places = spread(d_mixed)
-        sources = jnp.stack([(i_dp ^ d) * n_emb + (i_emb ^ e) for d, e in places]).astype(jnp.int32)
-
         ids = jnp.sum(jnp.where(perm_mask, tok_ids[None, :], 0), axis=1)
-        ids, _ = lax.optimization_barrier((ids, d_mixed))
+        ids, _ = lax.optimization_barrier((ids, normed))
         ids_all = share_ids(ids, n_dp, n_emb)
         ids_2d = ids_all.reshape(n_dev, n_tok)
         base = i_emb * range_rows
@@ -630,20 +629,12 @@
         slot = (owner ^ i_emb) * cap + pos - first
         pick = (slot[:, None] == jnp.arange(n_emb * cap, dtype=jnp.int32)[None, :]).astype(BF)
 
-        weights = (w_up, w_down, w_gate, w_proj)
-        saved, us = [], [normed]
-        for l in range(n_layers):
-            x_in = x
-            x, u_next, *kept = layer_fwd(l, l > 0, x, us[-1], returned[l], pick, *weights)
-            saved.append((x_in, *kept))
-            us.append(u_next)
-        set_b = gather(jnp.concatenate(us[1:n_layers], axis=1))
-        resid_out = lax.dot_general(perm, x, (((0,), (0,)), ((), ())), preferred_element_type=F32).astype(BF)
+        cot_in, _ = lax.optimization_barrier((cot_out, served[0]))
+        cot = jnp.dot(perm, cot_in, preferred_element_type=F32).astype(BF)
+        d_mixed = lax.dot_general(cot, w_proj[last], (((1,), (1,)), ((), ())), preferred_element_type=F32).astype(BF)
         d_sets = [None] * n_layers
-        for l in range(last, 0, -1):
-            x_in, up_pre, gate_pre, got = saved[l]
-            cot, d_mixed = layer_bwd(l, cot, d_mixed, x_in, got, up_pre, gate_pre, *weights)
-            d_sets[l - 1] = spread(d_mixed)[0] if l == last else [gather(d_mixed)]
+        d_sets[last], places = spread(d_mixed, False)
+        sources = jnp.stack([(i_dp ^ d) * n_emb + (i_emb ^ e) for d, e in places]).astype(jnp.int32)
 
         n_tiles = range_rows // TILE_ROWS
         lo = jnp.sum((ids_2d < base).astype(jnp.int32), axis=1)
@@ -665,14 +656,28 @@
         edges = jnp.arange(n_tiles + 1, dtype=jnp.int32) * TILE_ROWS
         tiles = jnp.sum((r[None, :] < edges[:, None]).astype(jnp.int32), axis=1)
 
-        set_a, _ = lax.optimization_barrier((set_a, d_mixed))
-        u_sets = [(set_a, 0)] + [(set_b, i * width) for i in range(n_layers - 1)]
-        d_sets[last] = d2_blocks
+        pick, meta, tiles, addrs = lax.optimization_barrier((pick, meta, tiles, addrs))
+
+        weights = (w_up, w_down, w_gate, w_proj)
+        saved, u = [], normed
+        for l in range(n_layers):
+            x_in = x
+            x, u, *kept = layer_fwd(l, l > 0, x, u, returned[l], pick, *weights)
+            saved.append((x_in, *kept))
+            if l < last:
+                u_sets.append(gather(u))
+        resid_out = lax.dot_general(perm, x, (((0,), (0,)), ((), ())), preferred_element_type=F32).astype(BF)
+        for l in range(last, 0, -1):
+            x_in, up_pre, gate_pre, got = saved[l]
+            cot, d_mixed = layer_bwd(l, cot, d_mixed, x_in, got, up_pre, gate_pre, *weights)
+            d_sets[l - 1] = spread(d_mixed, True)[0] if l == last else [gather(d_mixed)]
+
+        u_sets[0], _ = lax.optimization_barrier((u_sets[0], d_mixed))
         grads = None
         out_shape = (n_layers, range_rows // 8, width // 128, 8, 128)
         gates = []
         for l in range(n_layers):
-            gates.append(owner_gate(l, meta, *u_sets[l], w_gate))
+            gates.append(owner_gate(l, meta, u_sets[l], 0, w_gate))
         for l in range(last, -1, -1):
             grads = owner_grad(l, grads, out_shape, meta, tiles, addrs, gates[l], d_sets[l], 0)
         d_tables = grads.transpose(0, 1, 3, 2, 4).reshape(n_layers, range_rows, width)

time: 669 us -> 678 us (1.013)
  local copies, waits for them, and re-layouts: 17.3 us -> 27.4 us
    unnamed x87 -> x99, local copies, waits for them, and re-layouts: 15.8 us -> 25.9 us
  transfers between devices with their start and end apart: 42 -> 43, of which waited for: 16 -> 13; matrix products, arithmetic and copies ran while one was open for 3% -> 3% of each run, Pallas kernels for 39% -> 39%
where the time goes in v5:
time: 678 us; the launch traced here: 673 us
  Pallas kernels  297 us (44%)
  waiting for transfers between devices  288 us (42%)
  local copies, waits for them, and re-layouts  27.4 us (4%)
  starting transfers between devices  24.5 us (4%)
  between operations  14.7 us (2%)
  other arithmetic  13.2 us (2%)
  matrix products  8.96 us (1%)
    ppermute x39, waiting for transfers between devices, flip(): return lax.ppermute(block, axis, [(i, i ^ bit) for i in range(n)])  287 us
    pallas_call x3, Pallas kernels, owner_grad(): pl.pallas_call(functools.partial(owner_kernel, layer, col, len(d_all)), o...  111 us
    pallas_call x3, Pallas kernels, layer_fwd(): pl.pallas_call(functools.partial(forward_kernel, layer, keep), out_shape=...  58.9 us
    pallas_call x3, Pallas kernels, owner_gate(): pl.pallas_call(functools.partial(gate_kernel, layer, col), out_shape=pltp...  50.8 us
    pallas_call x2, Pallas kernels, layer_bwd(): pl.pallas_call(functools.partial(backward_kernel, layer), out_shape=[act,...  40.4 us
    pallas_call x1, Pallas kernels, serve_rows(): pl.pallas_call(functools.partial(serve_kernel, n_layers, cap), out_shape=...  26.5 us
    unnamed x99, local copies, waits for them, and re-layouts  25.9 us
    ppermute x39, starting transfers between devices, flip(): return lax.ppermute(block, axis, [(i, i ^ bit) for i in range(n)])  24.2 us
  transfers between devices with their start and end apart: 43, of which 13 were waited for; matrix products, arithmetic and copies ran while one was open for 3% of the time, Pallas kernels for 39%

profile of v5, /device:TPU:0, one launch (start us, length us, event | category | flops | bytes accessed | tf_op | source)
XLA Modules:
  0.0 673.4 jit_solution(2762792386952211315)
XLA Ops:
  7.2 1.1 convert_reduce_fusion.1
  9.2 1.2 fusion.1.u_ref
  12.3 9.0 %share_ids.1 = s32[16,4,128]{2,1,0:T(4,128)} custom-call(s32[4,128]{1,0:T(4,128)} %bitcast.46), custom_call_target="tpu_custom_call" | custom-call | tf_op jit(solution)/shard_map/share_ids/pallas_call | solution.py:57
  24.8 26.5 %serve_rows.1 = (bf16[256,1024]{1,0:T(8,128)(2,1)S(1)}, bf16[256,1024]{1,0:T(8,128)(2,1)}, bf16[256,1024]{1,0:T(8,128)(2,1)}, bf16[256,1024]{1,0:T(8,128)(2,1)},...) custom-call(s32[4]{0:T(128)S(1)} %get-tuple-element.75.cnt_ref, ...), custom_call_target="tpu_custom_call" | custom-call | flops 20000000000 | bytes 30000000 | tf_op jit(solution)/shard_map/serve_rows/pallas_call | solution.py:344
  56.2 1.9 collective-permute-start.2
  60.1 5.6 sort.7
  68.2 1.5 collective-permute-start.5
  69.7 12.7 %collective-permute-done.1.r2_ref = bf16[256,1024]{1,0:T(8,128)(2,1)S(1)} collective-permute-done((bf16[256,1024]{1,0:T(8,128)(2,1)}, bf16[256,1024]{1,0:T(8,128)(2,1)S(1)}, u32[]{:S(2)}, u32[]{:S(2)}) %collective-permute-start.1) | collective-permute-done | bytes 524320 | tf_op jit(solution)/shard_map/ppermute | solution.py:587
  83.2 21.1 %collective-permute-done.2.r3_ref = bf16[256,1024]{1,0:T(8,128)(2,1)} collective-permute-done((bf16[256,1024]{1,0:T(8,128)(2,1)}, bf16[256,1024]{1,0:T(8,128)(2,1)}, u32[]{:S(2)}, u32[]{:S(2)}) %collective-permute-start.2) | collective-permute-done | bytes 524320 | tf_op jit(solution)/shard_map/ppermute | solution.py:587
  104.4 1.2 copy-done.11
  105.6 1.0 copy-done.20
  106.6 1.0 copy-done.22
  108.7 18.5 %shard_map.95 = (bf16[512,1024]{1,0:T(8,128)(2,1)S(1)}, bf16[512,1024]{1,0:T(8,128)(2,1)}) custom-call(bf16[512,1024]{1,0:T(8,128)(2,1)S(1)} %copy-done.11, bf16[512,1024]{1,0:T(8,128)(2,1)S(1)} %copy-done.5, bf16[256,1024]{1,0:T(8,128)(2,1)S(1)} %copy-done.20, bf16[256,1024]{1,0:T(8,128)(2,1)S(1)} %copy-done.22, bf16[256,1024]{1,0:T(8,128)(2,1)S(1)} %copy-done.24, ...), custom_call_target="tpu_custom_call" | custom-call | flops 11000000512 | bytes 30000000 | tf_op jit(solution)/shard_map/pallas_call | solution.py:196
  127.2 5.7 collective-permute-done.5.r3_ref
  133.7 1.0 copy-done.18
  135.8 20.3 %shard_map.96 = (bf16[512,1024]{1,0:T(8,128)(2,1)S(1)}, bf16[512,1024]{1,0:T(8,128)(2,1)}, f32[512,4096]{1,0:T(8,128)}, f32[512,1024]{1,0:T(8,128)}, bf16[512,1024]{1,0:T(8,128)(2,1)S(1)}) custom-call(bf16[512,1024]{1,0:T(8,128)(2,1)S(1)} %get-tuple-element.41.x_ref, bf16[512,1024]{1,0:T(8,128)(2,1)} %get-tuple-element.42.u_ref, ...), custom_call_target="tpu_custom_call" | custom-call | flops 11000000512 | bytes 30000000 | tf_op jit(solution)/shard_map/pallas_call | solution.py:196
  158.7 1.3 collective-permute-start.8
  159.9 1.9 convolution_convert_fusion.cot_ref
  161.9 3.3 fusion.6.dm_ref.rest_0_
  165.2 14.6 %collective-permute-done.7.r2_ref = bf16[256,1024]{1,0:T(8,128)(2,1)S(1)} collective-permute-done((bf16[256,1024]{1,0:T(8,128)(2,1)}, bf16[256,1024]{1,0:T(8,128)(2,1)S(1)}, u32[]{:S(2)}, u32[]{:S(2)}) %collective-permute-start.7) | collective-permute-done | bytes 524320 | tf_op jit(solution)/shard_map/ppermute | solution.py:587
  179.8 14.2 %collective-permute-done.8.r3_ref = bf16[256,1024]{1,0:T(8,128)(2,1)S(1)} collective-permute-done((bf16[256,1024]{1,0:T(8,128)(2,1)}, bf16[256,1024]{1,0:T(8,128)(2,1)S(1)}, u32[]{:S(2)}, u32[]{:S(2)}) %collective-permute-start.8) | collective-permute-done | bytes 524320 | tf_op jit(solution)/shard_map/ppermute | solution.py:587
  194.1 20.1 %shard_map.97 = (bf16[512,1024]{1,0:T(8,128)(2,1)S(1)}, bf16[512,1024]{1,0:T(8,128)(2,1)}, f32[512,4096]{1,0:T(8,128)}, f32[512,1024]{1,0:T(8,128)}, bf16[512,1024]{1,0:T(8,128)(2,1)S(1)}) custom-call(bf16[512,1024]{1,0:T(8,128)(2,1)S(1)} %copy-done.9, bf16[512,1024]{1,0:T(8,128)(2,1)} %get-tuple-element.48.u_ref, bf16[256,1024]{1,0:T(8,128)(2,1)S(1)} %copy-done.16, ...), custom_call_target="tpu_custom_call" | custom-call | flops 11000000512 | bytes 30000000 | tf_op jit(solution)/shard_map/pallas_call | solution.py:196
  214.2 19.9 %shard_map.98 = (bf16[512,1024]{1,0:T(8,128)(2,1)S(1)}, bf16[512,1024]{1,0:T(8,128)(2,1)S(1)}) custom-call(bf16[512,1024]{1,0:T(8,128)(2,1)S(1)} %convolution_convert_fusion.cot_ref, bf16[512,1024]{1,0:T(8,128)(2,1)S(1)} %fusion.6.dm_ref.rest_0_, bf16[512,1024]{1,0:T(8,128)(2,1)S(1)} %copy-done.9, bf16[512,1024]{1,0:T(8,128)(2,1)S(1)} %get-tuple-element.58.got_ref, ...), custom_call_target="tpu_custom_call" | custom-call | flops 11000000512 | bytes 40000000 | tf_op jit(solution)/shard_map/pallas_call | solution.py:275
  234.1 20.5 %shard_map.99 = (bf16[512,1024]{1,0:T(8,128)(2,1)}, bf16[512,1024]{1,0:T(8,128)(2,1)S(1)}) custom-call(bf16[512,1024]{1,0:T(8,128)(2,1)S(1)} %get-tuple-element.61.cot_ref, bf16[512,1024]{1,0:T(8,128)(2,1)S(1)} %get-tuple-element.62.dm_ref.rest_0_, bf16[512,1024]{1,0:T(8,128)(2,1)S(1)} %get-tuple-element.41.x_ref, bf16[512,1024]{1,0:T(8,128)(2,1)S(1)} %copy-done.13, ...), custom_call_target="tpu_custom_call" | custom-call | flops 11000000512 | bytes 40000000 | tf_op jit(solution)/shard_map/pallas_call | solution.py:275
  255.6 1.4 collective-permute-start.26
  257.0 3.0 collective-permute-start.24
  260.6 35.1 %collective-permute-done.26.rest_3_ = bf16[512,1024]{1,0:T(8,128)(2,1)S(1)} collective-permute-done((bf16[512,1024]{1,0:T(8,128)(2,1)S(1)}, bf16[512,1024]{1,0:T(8,128)(2,1)S(1)}, u32[]{:S(2)}, u32[]{:S(2)}) %collective-permute-start.26) | collective-permute-done | bytes 1048608 | tf_op jit(solution)/shard_map/ppermute | solution.py:587
  296.5 1.2 collective-permute-start.11
  298.1 1.7 collective-permute-start.28
  299.7 36.6 %collective-permute-done.9.rest_1_ = bf16[512,1024]{1,0:T(8,128)(2,1)S(1)} collective-permute-done((bf16[512,1024]{1,0:T(8,128)(2,1)S(1)}, bf16[512,1024]{1,0:T(8,128)(2,1)S(1)}, u32[]{:S(2)}, u32[]{:S(2)}) %collective-permute-start.9) | collective-permute-done | bytes 1048608 | tf_op jit(solution)/shard_map/ppermute | solution.py:587
  336.9 1.6 collective-permute-start.29
  339.0 37.8 %collective-permute-done.28.rest_5_ = bf16[512,1024]{1,0:T(8,128)(2,1)} collective-permute-done((bf16[512,1024]{1,0:T(8,128)(2,1)S(1)}, bf16[512,1024]{1,0:T(8,128)(2,1)}, u32[]{:S(2)}, u32[]{:S(2)}) %collective-permute-start.28) | collective-permute-done | bytes 1048608 | tf_op jit(solution)/shard_map/ppermute | solution.py:587
  377.0 29.8 %collective-permute-done.27.rest_4_ = bf16[512,1024]{1,0:T(8,128)(2,1)} collective-permute-done((bf16[512,1024]{1,0:T(8,128)(2,1)S(1)}, bf16[512,1024]{1,0:T(8,128)(2,1)}, u32[]{:S(2)}, u32[]{:S(2)}) %collective-permute-start.27) | collective-permute-done | bytes 1048608 | tf_op jit(solution)/shard_map/ppermute | solution.py:587
  406.8 1.3 collective-permute-start.13
  409.7 38.3 %collective-permute-done.13.rest_5_ = bf16[512,1024]{1,0:T(8,128)(2,1)S(1)} collective-permute-done((bf16[512,1024]{1,0:T(8,128)(2,1)S(1)}, bf16[512,1024]{1,0:T(8,128)(2,1)S(1)}, u32[]{:S(2)}, u32[]{:S(2)}) %collective-permute-start.13) | collective-permute-done | bytes 1048608 | tf_op jit(solution)/shard_map/ppermute | solution.py:587
  448.0 1.5 collective-permute-start.30
  449.6 3.0 convolution_convert_fusion.1
  452.6 40.2 %collective-permute-done.14.rest_6_ = bf16[512,1024]{1,0:T(8,128)(2,1)} collective-permute-done((bf16[512,1024]{1,0:T(8,128)(2,1)}, bf16[512,1024]{1,0:T(8,128)(2,1)}, u32[]{:S(2)}, u32[]{:S(2)}) %collective-permute-start.14) | collective-permute-done | bytes 1048608 | tf_op jit(solution)/shard_map/ppermute | solution.py:587
  493.4 1.5 collective-permute-start.15
  495.2 2.8 copy-done.2
  498.0 16.9 %shard_map.100.g_hbm = f32[544,8,8,128]{3,2,1,0:T(8,128)} custom-call(s32[65]{0:T(128)S(1)} %concatenate.6.meta_ref, bf16[8192,1024]{1,0:T(8,128)(2,1)} %all-gather.5.cloned.1.call-done.u_hbm, bf16[3,1024,1024]{2,1,0:T(8,128)(2,1)S(1)} %copy-done.2), custom_call_target="tpu_custom_call" | custom-call | flops 10000000000 | bytes 30000000 | tf_op jit(solution)/shard_map/pallas_call | solution.py:430
  514.9 2.8 copy-done.3
  517.7 17.0 %shard_map.102.g_hbm = f32[544,8,8,128]{3,2,1,0:T(8,128)} custom-call(s32[65]{0:T(128)S(1)} %concatenate.6.meta_ref, bf16[8192,1024]{1,0:T(8,128)(2,1)} %all-gather.11.cloned.1.call-done.u_hbm, bf16[3,1024,1024]{2,1,0:T(8,128)(2,1)S(1)} %copy-done.3), custom_call_target="tpu_custom_call" | custom-call | flops 10000000000 | bytes 30000000 | tf_op jit(solution)/shard_map/pallas_call | solution.py:430
  535.9 37.0 %shard_map.103.rest_16_ = f32[3,2048,8,8,128]{4,3,2,1,0:T(8,128)} custom-call(s32[65]{0:T(128)S(1)} %concatenate.6.meta_ref, s32[17]{0:T(128)S(1)} %convert_reduce_fusion.2.tile_ref, s32[4096]{0:T(1024)S(1)} %fusion.18.addr_ref, f32[544,8,8,128]{3,2,1,0:T(8,128)} %shard_map.102.g_hbm, bf16[512,1024]{1,0:T(8,128)(2,1)} %copy-done.7, ...), custom_call_target="tpu_custom_call" | custom-call | flops 40000000000 | bytes 100000000 | tf_op jit(solution)/shard_map/pallas_call | solution.py:537
  572.9 2.8 copy-done.4
  575.6 17.0 %shard_map.101.g_hbm = f32[544,8,8,128]{3,2,1,0:T(8,128)} custom-call(s32[65]{0:T(128)S(1)} %concatenate.6.meta_ref, bf16[8192,1024]{1,0:T(8,128)(2,1)} %all-gather.9.cloned.1.call-done.u_hbm, bf16[3,1024,1024]{2,1,0:T(8,128)(2,1)S(1)} %copy-done.4), custom_call_target="tpu_custom_call" | custom-call | flops 10000000000 | bytes 30000000 | tf_op jit(solution)/shard_map/pallas_call | solution.py:430
  592.7 37.0 %shard_map.104.rest_1_ = f32[3,2048,8,8,128]{4,3,2,1,0:T(8,128)} custom-call(s32[65]{0:T(128)S(1)} %concatenate.6.meta_ref, s32[17]{0:T(128)S(1)} %convert_reduce_fusion.2.tile_ref, s32[4096]{0:T(1024)S(1)} %fusion.18.addr_ref, f32[544,8,8,128]{3,2,1,0:T(8,128)} %shard_map.101.g_hbm, bf16[512,1024]{1,0:T(8,128)(2,1)} %copy-done.6, ...), custom_call_target="tpu_custom_call", output_to_operand_aliasing={{}: (20, {})} | custom-call | flops 40000000000 | bytes 100000000 | tf_op jit(solution)/shard_map/pallas_call | solution.py:537
  629.7 37.0 %shard_map.105 = f32[3,2048,8,8,128]{4,3,2,1,0:T(8,128)} custom-call(s32[65]{0:T(128)S(1)} %concatenate.6.meta_ref, s32[17]{0:T(128)S(1)} %convert_reduce_fusion.2.tile_ref, s32[4096]{0:T(1024)S(1)} %fusion.18.addr_ref, f32[544,8,8,128]{3,2,1,0:T(8,128)} %shard_map.100.g_hbm, ...), custom_call_target="tpu_custom_call", output_to_operand_aliasing={{}: (5, {})} | custom-call | flops 40000000000 | bytes 100000000 | tf_op jit(solution)/shard_map/pallas_call | solution.py:537
  (190 shorter events, 29.4 us)
Async XLA Ops:
  7.2 445.4 %all-gather.5.cloned.1.call-start = ((), (), s32[]{:S(2)}) async-start(), calls=%async_computation | async-start | bytes 17825792 | tf_op jit(solution)/shard_map/all_gather | solution.py:574
  11.5 503.4 %all-gather.11.cloned.1.call-start = ((), (), s32[]{:S(2)}) async-start(), calls=%async_computation.3 | async-start | bytes 17825792 | tf_op jit(solution)/shard_map/all_gather | solution.py:574
  56.2 11.2 %collective-permute-start = (bf16[256,1024]{1,0:T(8,128)(2,1)}, bf16[256,1024]{1,0:T(8,128)(2,1)S(1)}, u32[]{:S(2)}, u32[]{:S(2)}) collective-permute-start(bf16[256,1024]{1,0:T(8,128)(2,1)} %get-tuple-element.37), channel_id=1, source_target_pairs={{0,1},{1,0},{2,3},{3,2},{4,5},{5,4},{6,7},{7,6},{8,9},{9,8},{10,11... | collective-permute-start | bytes 1572872 | tf_op jit(solution)/shard_map/ppermute | solution.py:587
  56.2 26.2 %collective-permute-start.1 = (bf16[256,1024]{1,0:T(8,128)(2,1)}, bf16[256,1024]{1,0:T(8,128)(2,1)S(1)}, u32[]{:S(2)}, u32[]{:S(2)}) collective-permute-start(bf16[256,1024]{1,0:T(8,128)(2,1)} %get-tuple-element.38), channel_id=1, source_target_pairs={{0,2},{1,3},{2,0},{3,1},{4,6},{5,7},{6,4},{7,5},{8,10},{9,11},{10,... | collective-permute-start | bytes 1572872 | tf_op jit(solution)/shard_map/ppermute | solution.py:587
  56.2 48.1 %collective-permute-start.2 = (bf16[256,1024]{1,0:T(8,128)(2,1)}, bf16[256,1024]{1,0:T(8,128)(2,1)}, u32[]{:S(2)}, u32[]{:S(2)}) collective-permute-start(bf16[256,1024]{1,0:T(8,128)(2,1)} %get-tuple-element.39), channel_id=1, source_target_pairs={{0,3},{1,2},{2,1},{3,0},{4,7},{5,6},{6,5},{7,4},{8,11},{9,10},{10,... | collective-permute-start | bytes 1572872 | tf_op jit(solution)/shard_map/ppermute | solution.py:587
  58.1 69.1 %collective-permute-start.3 = (bf16[256,1024]{1,0:T(8,128)(2,1)}, bf16[256,1024]{1,0:T(8,128)(2,1)}, u32[]{:S(2)}, u32[]{:S(2)}) collective-permute-start(bf16[256,1024]{1,0:T(8,128)(2,1)} %get-tuple-element.44), channel_id=1, source_target_pairs={{0,1},{1,0},{2,3},{3,2},{4,5},{5,4},{6,7},{7,6},{8,9},{9,8},{10,11... | collective-permute-start | bytes 1572872 | tf_op jit(solution)/shard_map/ppermute | solution.py:587
  58.4 68.9 %collective-permute-start.4 = (bf16[256,1024]{1,0:T(8,128)(2,1)}, bf16[256,1024]{1,0:T(8,128)(2,1)}, u32[]{:S(2)}, u32[]{:S(2)}) collective-permute-start(bf16[256,1024]{1,0:T(8,128)(2,1)} %get-tuple-element.45), channel_id=1, source_target_pairs={{0,2},{1,3},{2,0},{3,1},{4,6},{5,7},{6,4},{7,5},{8,10},{9,11},{10,... | collective-permute-start | bytes 1572872 | tf_op jit(solution)/shard_map/ppermute | solution.py:587
  68.2 64.7 %collective-permute-start.5 = (bf16[256,1024]{1,0:T(8,128)(2,1)}, bf16[256,1024]{1,0:T(8,128)(2,1)S(1)}, u32[]{:S(2)}, u32[]{:S(2)}) collective-permute-start(bf16[256,1024]{1,0:T(8,128)(2,1)} %copy-done.30), channel_id=1, source_target_pairs={{0,3},{1,2},{2,1},{3,0},{4,7},{5,6},{6,5},{7,4},{8,11},{9,10},{10,... | collective-permute-start | bytes 1572872 | tf_op jit(solution)/shard_map/ppermute | solution.py:587
  157.1 415.8 %all-gather.9.cloned.1.call-start = ((), (), s32[]{:S(2)}) async-start(), calls=%async_computation.2 | async-start | bytes 17825792 | tf_op jit(solution)/shard_map/all_gather | solution.py:574
  157.8 471.9 %all-gather.7.cloned.1.call-start = ((), (), s32[]{:S(2)}) async-start(), calls=%async_computation.1 | async-start | bytes 17825792 | tf_op jit(solution)/shard_map/all_gather | solution.py:574
  158.0 7.2 %collective-permute-start.6 = (bf16[256,1024]{1,0:T(8,128)(2,1)}, bf16[256,1024]{1,0:T(8,128)(2,1)S(1)}, u32[]{:S(2)}, u32[]{:S(2)}) collective-permute-start(bf16[256,1024]{1,0:T(8,128)(2,1)} %copy-done.29), channel_id=1, source_target_pairs={{0,1},{1,0},{2,3},{3,2},{4,5},{5,4},{6,7},{7,6},{8,9},{9,8},{10,11... | collective-permute-start | bytes 1572872 | tf_op jit(solution)/shard_map/ppermute | solution.py:587
  158.2 21.6 %collective-permute-start.7 = (bf16[256,1024]{1,0:T(8,128)(2,1)}, bf16[256,1024]{1,0:T(8,128)(2,1)S(1)}, u32[]{:S(2)}, u32[]{:S(2)}) collective-permute-start(bf16[256,1024]{1,0:T(8,128)(2,1)} %copy-done.28), channel_id=1, source_target_pairs={{0,2},{1,3},{2,0},{3,1},{4,6},{5,7},{6,4},{7,5},{8,10},{9,11},{10,... | collective-permute-start | bytes 1572872 | tf_op jit(solution)/shard_map/ppermute | solution.py:587
  158.7 35.4 %collective-permute-start.8 = (bf16[256,1024]{1,0:T(8,128)(2,1)}, bf16[256,1024]{1,0:T(8,128)(2,1)S(1)}, u32[]{:S(2)}, u32[]{:S(2)}) collective-permute-start(bf16[256,1024]{1,0:T(8,128)(2,1)} %get-tuple-element.52), channel_id=1, source_target_pairs={{0,3},{1,2},{2,1},{3,0},{4,7},{5,6},{6,5},{7,4},{8,11},{9,10},{10,... | collective-permute-start | bytes 1572872 | tf_op jit(solution)/shard_map/ppermute | solution.py:587
  255.6 40.1 %collective-permute-start.26 = (bf16[512,1024]{1,0:T(8,128)(2,1)S(1)}, bf16[512,1024]{1,0:T(8,128)(2,1)S(1)}, u32[]{:S(2)}, u32[]{:S(2)}) collective-permute-start(bf16[512,1024]{1,0:T(8,128)(2,1)S(1)} %fusion.6.dm_ref.rest_0_), channel_id=1, source_target_pairs={{0,2},{1,3},{2,0},{3,1},{4,6},{5,7},{6,4},{7,5},{8,10},{9,11},{10,... | collective-permute-start | bytes 3145736 | tf_op jit(solution)/shard_map/ppermute | solution.py:587
  257.0 39.5 %collective-permute-start.25 = (bf16[512,1024]{1,0:T(8,128)(2,1)S(1)}, bf16[512,1024]{1,0:T(8,128)(2,1)S(1)}, u32[]{:S(2)}, u32[]{:S(2)}) collective-permute-start(bf16[512,1024]{1,0:T(8,128)(2,1)S(1)} %fusion.6.dm_ref.rest_0_), channel_id=1, source_target_pairs={{0,4},{4,0},{8,12},{12,8},{1,5},{5,1},{9,13},{13,9},{2,6},{6,2},{1... | collective-permute-start | bytes 3145736 | tf_op jit(solution)/shard_map/ppermute | solution.py:587
  257.0 40.7 %collective-permute-start.24 = (bf16[512,1024]{1,0:T(8,128)(2,1)S(1)}, bf16[512,1024]{1,0:T(8,128)(2,1)S(1)}, u32[]{:S(2)}, u32[]{:S(2)}) collective-permute-start(bf16[512,1024]{1,0:T(8,128)(2,1)S(1)} %fusion.6.dm_ref.rest_0_), channel_id=1, source_target_pairs={{0,8},{4,12},{8,0},{12,4},{1,9},{5,13},{9,1},{13,5},{2,10},{6,14},... | collective-permute-start | bytes 3145736 | tf_op jit(solution)/shard_map/ppermute | solution.py:587
  260.0 38.1 %collective-permute-start.31 = (bf16[512,1024]{1,0:T(8,128)(2,1)S(1)}, bf16[512,1024]{1,0:T(8,128)(2,1)S(1)}, u32[]{:S(2)}, u32[]{:S(2)}) collective-permute-start(bf16[512,1024]{1,0:T(8,128)(2,1)S(1)} %fusion.6.dm_ref.rest_0_), channel_id=1, source_target_pairs={{0,1},{1,0},{2,3},{3,2},{4,5},{5,4},{6,7},{7,6},{8,9},{9,8},{10,11... | collective-permute-start | bytes 3145736 | tf_op jit(solution)/shard_map/ppermute | solution.py:587
  260.3 76.0 %collective-permute-start.9 = (bf16[512,1024]{1,0:T(8,128)(2,1)S(1)}, bf16[512,1024]{1,0:T(8,128)(2,1)S(1)}, u32[]{:S(2)}, u32[]{:S(2)}) collective-permute-start(bf16[512,1024]{1,0:T(8,128)(2,1)S(1)} %get-tuple-element.62.dm_ref.rest_0_), channel_id=1, source_target_pairs={{0,8},{4,12},{8,0},{12,4},{1,9},{5,13},{9,1},{13,5},{2,10},{6,14},... | collective-permute-start | bytes 3145736 | tf_op jit(solution)/shard_map/ppermute | solution.py:587
  295.7 153.9 %copy-start.35 = (bf16[512,1024]{1,0:T(8,128)(2,1)}, bf16[512,1024]{1,0:T(8,128)(2,1)S(1)}, u32[]{:S(2)}) copy-start(bf16[512,1024]{1,0:T(8,128)(2,1)S(1)} %collective-permute-done.26.rest_3_) | copy-start | bytes 3145732
  295.7 41.2 %collective-permute-start.10 = (bf16[512,1024]{1,0:T(8,128)(2,1)S(1)}, bf16[512,1024]{1,0:T(8,128)(2,1)}, u32[]{:S(2)}, u32[]{:S(2)}) collective-permute-start(bf16[512,1024]{1,0:T(8,128)(2,1)S(1)} %get-tuple-element.62.dm_ref.rest_0_), channel_id=1, source_target_pairs={{0,4},{4,0},{8,12},{12,8},{1,5},{5,1},{9,13},{13,9},{2,6},{6,2},{1... | collective-permute-start | bytes 3145736 | tf_op jit(solution)/shard_map/ppermute | solution.py:587
  296.5 153.1 %copy-start.36 = (bf16[512,1024]{1,0:T(8,128)(2,1)}, bf16[512,1024]{1,0:T(8,128)(2,1)S(1)}, u32[]{:S(2)}) copy-start(bf16[512,1024]{1,0:T(8,128)(2,1)S(1)} %collective-permute-done.25.rest_2_) | copy-start | bytes 3145732
  296.5 42.1 %collective-permute-start.11 = (bf16[512,1024]{1,0:T(8,128)(2,1)S(1)}, bf16[512,1024]{1,0:T(8,128)(2,1)S(1)}, u32[]{:S(2)}, u32[]{:S(2)}) collective-permute-start(bf16[512,1024]{1,0:T(8,128)(2,1)S(1)} %get-tuple-element.62.dm_ref.rest_0_), channel_id=1, source_target_pairs={{0,2},{1,3},{2,0},{3,1},{4,6},{5,7},{6,4},{7,5},{8,10},{9,11},{10,... | collective-permute-start | bytes 3145736 | tf_op jit(solution)/shard_map/ppermute | solution.py:587
  297.7 151.9 %copy-start.37 = (bf16[512,1024]{1,0:T(8,128)(2,1)}, bf16[512,1024]{1,0:T(8,128)(2,1)S(1)}, u32[]{:S(2)}) copy-start(bf16[512,1024]{1,0:T(8,128)(2,1)S(1)} %collective-permute-done.24.rest_1_) | copy-start | bytes 3145732
  297.7 40.9 %collective-permute-start.16 = (bf16[512,1024]{1,0:T(8,128)(2,1)S(1)}, bf16[512,1024]{1,0:T(8,128)(2,1)S(1)}, u32[]{:S(2)}, u32[]{:S(2)}) collective-permute-start(bf16[512,1024]{1,0:T(8,128)(2,1)S(1)} %get-tuple-element.62.dm_ref.rest_0_), channel_id=1, source_target_pairs={{0,1},{1,0},{2,3},{3,2},{4,5},{5,4},{6,7},{7,6},{8,9},{9,8},{10,11... | collective-permute-start | bytes 3145736 | tf_op jit(solution)/shard_map/ppermute | solution.py:587
  298.1 151.5 %copy-start.38 = (bf16[512,1024]{1,0:T(8,128)(2,1)}, bf16[512,1024]{1,0:T(8,128)(2,1)S(1)}, u32[]{:S(2)}) copy-start(bf16[512,1024]{1,0:T(8,128)(2,1)S(1)} %collective-permute-done.31.rest_8_) | copy-start | bytes 3145732
  298.1 78.8 %collective-permute-start.28 = (bf16[512,1024]{1,0:T(8,128)(2,1)S(1)}, bf16[512,1024]{1,0:T(8,128)(2,1)}, u32[]{:S(2)}, u32[]{:S(2)}) collective-permute-start(bf16[512,1024]{1,0:T(8,128)(2,1)S(1)} %collective-permute-done.26.rest_3_), channel_id=1, source_target_pairs={{0,8},{4,12},{8,0},{12,4},{1,9},{5,13},{9,1},{13,5},{2,10},{6,14},... | collective-permute-start | bytes 3145736 | tf_op jit(solution)/shard_map/ppermute | solution.py:587
  336.3 178.5 %copy-start.31 = (bf16[512,1024]{1,0:T(8,128)(2,1)}, bf16[512,1024]{1,0:T(8,128)(2,1)S(1)}, u32[]{:S(2)}) copy-start(bf16[512,1024]{1,0:T(8,128)(2,1)S(1)} %collective-permute-done.9.rest_1_) | copy-start | bytes 3145732
  336.3 70.5 %collective-permute-start.27 = (bf16[512,1024]{1,0:T(8,128)(2,1)S(1)}, bf16[512,1024]{1,0:T(8,128)(2,1)}, u32[]{:S(2)}, u32[]{:S(2)}) collective-permute-start(bf16[512,1024]{1,0:T(8,128)(2,1)S(1)} %collective-permute-done.25.rest_2_), channel_id=1, source_target_pairs={{0,8},{4,12},{8,0},{12,4},{1,9},{5,13},{9,1},{13,5},{2,10},{6,14},... | collective-permute-start | bytes 3145736 | tf_op jit(solution)/shard_map/ppermute | solution.py:587
  336.9 71.3 %collective-permute-start.29 = (bf16[512,1024]{1,0:T(8,128)(2,1)S(1)}, bf16[512,1024]{1,0:T(8,128)(2,1)}, u32[]{:S(2)}, u32[]{:S(2)}) collective-permute-start(bf16[512,1024]{1,0:T(8,128)(2,1)S(1)} %collective-permute-done.26.rest_3_), channel_id=1, source_target_pairs={{0,4},{4,0},{8,12},{12,8},{1,5},{5,1},{9,13},{13,9},{2,6},{6,2},{1... | collective-permute-start | bytes 3145736 | tf_op jit(solution)/shard_map/ppermute | solution.py:587
  338.5 70.3 %collective-permute-start.32 = (bf16[512,1024]{1,0:T(8,128)(2,1)S(1)}, bf16[512,1024]{1,0:T(8,128)(2,1)S(1)}, u32[]{:S(2)}, u32[]{:S(2)}) collective-permute-start(bf16[512,1024]{1,0:T(8,128)(2,1)S(1)} %collective-permute-done.24.rest_1_), channel_id=1, source_target_pairs={{0,1},{1,0},{2,3},{3,2},{4,5},{5,4},{6,7},{7,6},{8,9},{9,8},{10,11... | collective-permute-start | bytes 3145736 | tf_op jit(solution)/shard_map/ppermute | solution.py:587
  338.5 70.7 %collective-permute-start.33 = (bf16[512,1024]{1,0:T(8,128)(2,1)S(1)}, bf16[512,1024]{1,0:T(8,128)(2,1)S(1)}, u32[]{:S(2)}, u32[]{:S(2)}) collective-permute-start(bf16[512,1024]{1,0:T(8,128)(2,1)S(1)} %collective-permute-done.25.rest_2_), channel_id=1, source_target_pairs={{0,1},{1,0},{2,3},{3,2},{4,5},{5,4},{6,7},{7,6},{8,9},{9,8},{10,11... | collective-permute-start | bytes 3145736 | tf_op jit(solution)/shard_map/ppermute | solution.py:587
  376.9 32.4 %collective-permute-start.34 = (bf16[512,1024]{1,0:T(8,128)(2,1)S(1)}, bf16[512,1024]{1,0:T(8,128)(2,1)S(1)}, u32[]{:S(2)}, u32[]{:S(2)}) collective-permute-start(bf16[512,1024]{1,0:T(8,128)(2,1)S(1)} %collective-permute-done.26.rest_3_), channel_id=1, source_target_pairs={{0,1},{1,0},{2,3},{3,2},{4,5},{5,4},{6,7},{7,6},{8,9},{9,8},{10,11... | collective-permute-start | bytes 3145736 | tf_op jit(solution)/shard_map/ppermute | solution.py:587
  406.8 41.2 %collective-permute-start.13 = (bf16[512,1024]{1,0:T(8,128)(2,1)S(1)}, bf16[512,1024]{1,0:T(8,128)(2,1)S(1)}, u32[]{:S(2)}, u32[]{:S(2)}) collective-permute-start(bf16[512,1024]{1,0:T(8,128)(2,1)S(1)} %collective-permute-done.9.rest_1_), channel_id=1, source_target_pairs={{0,2},{1,3},{2,0},{3,1},{4,6},{5,7},{6,4},{7,5},{8,10},{9,11},{10,... | collective-permute-start | bytes 3145736 | tf_op jit(solution)/shard_map/ppermute | solution.py:587
  408.2 44.4 %collective-permute-start.12 = (bf16[512,1024]{1,0:T(8,128)(2,1)}, bf16[512,1024]{1,0:T(8,128)(2,1)S(1)}, u32[]{:S(2)}, u32[]{:S(2)}) collective-permute-start(bf16[512,1024]{1,0:T(8,128)(2,1)} %collective-permute-done.10.rest_2_), channel_id=1, source_target_pairs={{0,8},{4,12},{8,0},{12,4},{1,9},{5,13},{9,1},{13,5},{2,10},{6,14},... | collective-permute-start | bytes 3145736 | tf_op jit(solution)/shard_map/ppermute | solution.py:587
  408.8 84.0 %collective-permute-start.14 = (bf16[512,1024]{1,0:T(8,128)(2,1)}, bf16[512,1024]{1,0:T(8,128)(2,1)}, u32[]{:S(2)}, u32[]{:S(2)}) collective-permute-start(bf16[512,1024]{1,0:T(8,128)(2,1)} %collective-permute-done.10.rest_2_), channel_id=1, source_target_pairs={{0,2},{1,3},{2,0},{3,1},{4,6},{5,7},{6,4},{7,5},{8,10},{9,11},{10,... | collective-permute-start | bytes 3145736 | tf_op jit(solution)/shard_map/ppermute | solution.py:587
  409.2 83.6 %collective-permute-start.17 = (bf16[512,1024]{1,0:T(8,128)(2,1)S(1)}, bf16[512,1024]{1,0:T(8,128)(2,1)}, u32[]{:S(2)}, u32[]{:S(2)}) collective-permute-start(bf16[512,1024]{1,0:T(8,128)(2,1)S(1)} %collective-permute-done.9.rest_1_), channel_id=1, source_target_pairs={{0,1},{1,0},{2,3},{3,2},{4,5},{5,4},{6,7},{7,6},{8,9},{9,8},{10,11... | collective-permute-start | bytes 3145736 | tf_op jit(solution)/shard_map/ppermute | solution.py:587
  409.2 84.1 %collective-permute-start.18 = (bf16[512,1024]{1,0:T(8,128)(2,1)}, bf16[512,1024]{1,0:T(8,128)(2,1)}, u32[]{:S(2)}, u32[]{:S(2)}) collective-permute-start(bf16[512,1024]{1,0:T(8,128)(2,1)} %collective-permute-done.10.rest_2_), channel_id=1, source_target_pairs={{0,1},{1,0},{2,3},{3,2},{4,5},{5,4},{6,7},{7,6},{8,9},{9,8},{10,11... | collective-permute-start | bytes 3145736 | tf_op jit(solution)/shard_map/ppermute | solution.py:587
  448.0 47.1 %collective-permute-start.30 = (bf16[512,1024]{1,0:T(8,128)(2,1)}, bf16[512,1024]{1,0:T(8,128)(2,1)}, u32[]{:S(2)}, u32[]{:S(2)}) collective-permute-start(bf16[512,1024]{1,0:T(8,128)(2,1)} %collective-permute-done.28.rest_5_), channel_id=1, source_target_pairs={{0,4},{4,0},{8,12},{12,8},{1,5},{5,1},{9,13},{13,9},{2,6},{6,2},{1... | collective-permute-start | bytes 3145736 | tf_op jit(solution)/shard_map/ppermute | solution.py:587
  452.6 82.2 %collective-permute-start.36 = (bf16[512,1024]{1,0:T(8,128)(2,1)}, bf16[512,1024]{1,0:T(8,128)(2,1)}, u32[]{:S(2)}, u32[]{:S(2)}) collective-permute-start(bf16[512,1024]{1,0:T(8,128)(2,1)} %collective-permute-done.28.rest_5_), channel_id=1, source_target_pairs={{0,1},{1,0},{2,3},{3,2},{4,5},{5,4},{6,7},{7,6},{8,9},{9,8},{10,11... | collective-permute-start | bytes 3145736 | tf_op jit(solution)/shard_map/ppermute | solution.py:587
  492.8 41.9 %collective-permute-start.35 = (bf16[512,1024]{1,0:T(8,128)(2,1)}, bf16[512,1024]{1,0:T(8,128)(2,1)}, u32[]{:S(2)}, u32[]{:S(2)}) collective-permute-start(bf16[512,1024]{1,0:T(8,128)(2,1)} %collective-permute-done.27.rest_4_), channel_id=1, source_target_pairs={{0,1},{1,0},{2,3},{3,2},{4,5},{5,4},{6,7},{7,6},{8,9},{9,8},{10,11... | collective-permute-start | bytes 3145736 | tf_op jit(solution)/shard_map/ppermute | solution.py:587
  492.8 42.4 %collective-permute-start.37 = (bf16[512,1024]{1,0:T(8,128)(2,1)}, bf16[512,1024]{1,0:T(8,128)(2,1)}, u32[]{:S(2)}, u32[]{:S(2)}) collective-permute-start(bf16[512,1024]{1,0:T(8,128)(2,1)} %collective-permute-done.29.rest_6_), channel_id=1, source_target_pairs={{0,1},{1,0},{2,3},{3,2},{4,5},{5,4},{6,7},{7,6},{8,9},{9,8},{10,11... | collective-permute-start | bytes 3145736 | tf_op jit(solution)/shard_map/ppermute | solution.py:587
  493.4 42.0 %collective-permute-start.15 = (bf16[512,1024]{1,0:T(8,128)(2,1)S(1)}, bf16[512,1024]{1,0:T(8,128)(2,1)}, u32[]{:S(2)}, u32[]{:S(2)}) collective-permute-start(bf16[512,1024]{1,0:T(8,128)(2,1)S(1)} %collective-permute-done.13.rest_5_), channel_id=1, source_target_pairs={{0,4},{4,0},{8,12},{12,8},{1,5},{5,1},{9,13},{13,9},{2,6},{6,2},{1... | collective-permute-start | bytes 3145736 | tf_op jit(solution)/shard_map/ppermute | solution.py:587
  495.2 40.6 %collective-permute-start.38 = (bf16[512,1024]{1,0:T(8,128)(2,1)}, bf16[512,1024]{1,0:T(8,128)(2,1)}, u32[]{:S(2)}, u32[]{:S(2)}) collective-permute-start(bf16[512,1024]{1,0:T(8,128)(2,1)} %collective-permute-done.30.rest_7_), channel_id=1, source_target_pairs={{0,1},{1,0},{2,3},{3,2},{4,5},{5,4},{6,7},{7,6},{8,9},{9,8},{10,11... | collective-permute-start | bytes 3145736 | tf_op jit(solution)/shard_map/ppermute | solution.py:587
  534.7 57.9 %collective-permute-start.19 = (bf16[512,1024]{1,0:T(8,128)(2,1)S(1)}, bf16[512,1024]{1,0:T(8,128)(2,1)}, u32[]{:S(2)}, u32[]{:S(2)}) collective-permute-start(bf16[512,1024]{1,0:T(8,128)(2,1)S(1)} %copy-done.33), channel_id=1, source_target_pairs={{0,1},{1,0},{2,3},{3,2},{4,5},{5,4},{6,7},{7,6},{8,9},{9,8},{10,11... | collective-permute-start | bytes 3145736 | tf_op jit(solution)/shard_map/ppermute | solution.py:587
  534.8 57.8 %collective-permute-start.21 = (bf16[512,1024]{1,0:T(8,128)(2,1)S(1)}, bf16[512,1024]{1,0:T(8,128)(2,1)}, u32[]{:S(2)}, u32[]{:S(2)}) collective-permute-start(bf16[512,1024]{1,0:T(8,128)(2,1)S(1)} %collective-permute-done.13.rest_5_), channel_id=1, source_target_pairs={{0,1},{1,0},{2,3},{3,2},{4,5},{5,4},{6,7},{7,6},{8,9},{9,8},{10,11... | collective-permute-start | bytes 3145736 | tf_op jit(solution)/shard_map/ppermute | solution.py:587
  535.3 57.4 %collective-permute-start.20 = (bf16[512,1024]{1,0:T(8,128)(2,1)S(1)}, bf16[512,1024]{1,0:T(8,128)(2,1)}, u32[]{:S(2)}, u32[]{:S(2)}) collective-permute-start(bf16[512,1024]{1,0:T(8,128)(2,1)S(1)} %copy-done.41), channel_id=1, source_target_pairs={{0,1},{1,0},{2,3},{3,2},{4,5},{5,4},{6,7},{7,6},{8,9},{9,8},{10,11... | collective-permute-start | bytes 3145736 | tf_op jit(solution)/shard_map/ppermute | solution.py:587
  535.3 57.3 %collective-permute-start.22 = (bf16[512,1024]{1,0:T(8,128)(2,1)}, bf16[512,1024]{1,0:T(8,128)(2,1)}, u32[]{:S(2)}, u32[]{:S(2)}) collective-permute-start(bf16[512,1024]{1,0:T(8,128)(2,1)} %collective-permute-done.14.rest_6_), channel_id=1, source_target_pairs={{0,1},{1,0},{2,3},{3,2},{4,5},{5,4},{6,7},{7,6},{8,9},{9,8},{10,11... | collective-permute-start | bytes 3145736 | tf_op jit(solution)/shard_map/ppermute | solution.py:587
  535.8 56.9 %collective-permute-start.23 = (bf16[512,1024]{1,0:T(8,128)(2,1)}, bf16[512,1024]{1,0:T(8,128)(2,1)}, u32[]{:S(2)}, u32[]{:S(2)}) collective-permute-start(bf16[512,1024]{1,0:T(8,128)(2,1)} %collective-permute-done.15.rest_7_), channel_id=1, source_target_pairs={{0,1},{1,0},{2,3},{3,2},{4,5},{5,4},{6,7},{7,6},{8,9},{9,8},{10,11... | collective-permute-start | bytes 3145736 | tf_op jit(solution)/shard_map/ppermute | solution.py:587
  (43 other events, 979.4 us)
Sparse Core Ops, SparseCore 0:
  11.6 107.5 all-gather.4
  157.2 87.6 all-gather.10
  247.1 127.8 all-gather.8
  377.1 122.7 all-gather.6

commit v6 on v5

--- a/solution.py
+++ b/solution.py
@@ -360,8 +360,7 @@
 MAX_ROWS = 17 * BLK
 
 
-def pull_runs(meta_ref, srcs, col, dst, sem):
-    width = dst.shape[1]
+def pull_runs(meta_ref, srcs, dst, sem):
 
     def run(src, k, base):
         lo, off = meta_ref[k], meta_ref[2 * N_SRC + k]
@@ -369,7 +368,7 @@
         def chunk(c, _):
             a = pl.multiple_of(base + lo + c * CHUNK, CHUNK)
             b = pl.multiple_of((off + c) * CHUNK, CHUNK)
-            pltpu.make_async_copy(src.at[pl.ds(a, CHUNK), col:col + width], dst.at[pl.ds(b, CHUNK), :], sem).start()
+            pltpu.make_async_copy(src.at[pl.ds(a, CHUNK), :], dst.at[pl.ds(b, CHUNK), :], sem).start()
             return 0
 
         lax.fori_loop(0, meta_ref[N_SRC + k], chunk, 0)
@@ -382,11 +381,9 @@
             run(src, meta_ref[3 * N_SRC + 1 + j], 0)
 
 
-def drain_runs(meta_ref, srcs, col, dst, sem):
-    width = dst.shape[1]
-
+def drain_runs(meta_ref, srcs, dst, sem):
     def one(c, _):
-        pltpu.make_async_copy(srcs[0].at[pl.ds(0, CHUNK), col:col + width], dst.at[pl.ds(0, CHUNK), :], sem).wait()
+        pltpu.make_async_copy(srcs[0].at[pl.ds(0, CHUNK), :], dst.at[pl.ds(0, CHUNK), :], sem).wait()
         return 0
 
     lax.fori_loop(0, meta_ref[3 * N_SRC], one, 0)
@@ -396,9 +393,10 @@
     return lax.div(meta_ref[3 * N_SRC] * CHUNK + BLK - 1, BLK)
 
 
-def gate_kernel(layer, col, meta_ref, u_hbm, w_ref, out, uc, stage, sem_u, sem_o):
-    pull_runs(meta_ref, [u_hbm], col, uc, sem_u)
-    drain_runs(meta_ref, [u_hbm], col, uc, sem_u)
+def gate_kernel(layer, meta_ref, w_ref, *rest):
+    u_hbm, (out, uc, stage, sem_u, sem_o) = rest[:-5], rest[-5:]
+    pull_runs(meta_ref, u_hbm, uc, sem_u)
+    drain_runs(meta_ref, u_hbm, uc, sem_u)
     total = n_blocks(meta_ref)
 
     def out_copy(b):
@@ -423,14 +421,14 @@
     lax.fori_loop(jnp.maximum(total - 2, 0), total, lambda b, c: (out_copy(b).wait(), c)[1], 0)
 
 
-def owner_gate(layer, meta, u_all, col, w_gate):
+def owner_gate(layer, meta, u_all, w_gate):
     smem = pl.BlockSpec(memory_space=pltpu.SMEM)
     hbm = pl.BlockSpec(memory_space=pltpu.HBM)
     width = w_gate.shape[2]
     return pl.pallas_call(
-        functools.partial(gate_kernel, layer, col),
+        functools.partial(gate_kernel, layer),
         out_shape=pltpu.HBM((MAX_ROWS // 8, width // 128, 8, 128), F32),
-        in_specs=[smem, hbm, pl.BlockSpec(memory_space=pltpu.VMEM)],
+        in_specs=[smem, pl.BlockSpec(memory_space=pltpu.VMEM)] + [hbm] * len(u_all),
         out_specs=hbm,
         scratch_shapes=[
             pltpu.VMEM((MAX_ROWS, width), BF),
@@ -440,13 +438,13 @@
         ],
         compiler_params=pltpu.CompilerParams(vmem_limit_bytes=28 << 20),
         cost_estimate=pl.CostEstimate(flops=10_000_000_000, bytes_accessed=30_000_000, transcendentals=0),
-    )(meta, *in_hbm(u_all), w_gate)
+    )(meta, w_gate, *in_hbm(*u_all))
 
 
 UNROLL = 8
 
 
-def owner_kernel(layer, col, n_src, meta_ref, tile_ref, addr_ref, g_hbm, *rest):
+def owner_kernel(layer, n_src, meta_ref, tile_ref, addr_ref, g_hbm, *rest):
     d_hbm = rest[:n_src]
     out, dc, prod, acc, sem_d, sem_g, sem_o = rest[-7:]
     n_tiles = tile_ref.shape[0] - 1
@@ -457,7 +455,7 @@
         return pltpu.make_async_copy(
             g_hbm.at[pl.ds(b * n, n)], prod.reshape(MAX_ROWS // 8, 8, 8, 128).at[pl.ds(b * n, n)], sem_g.at[b])
 
-    pull_runs(meta_ref, d_hbm, col, dc, sem_d)
+    pull_runs(meta_ref, d_hbm, dc, sem_d)
     lax.fori_loop(0, total, lambda b, c: (g_copy(b).start(), c)[1], 0)
 
     def clear(buf):
@@ -469,7 +467,7 @@
 
     clear(0)
     clear(1)
-    drain_runs(meta_ref, d_hbm, col, dc, sem_d)
+    drain_runs(meta_ref, d_hbm, dc, sem_d)
 
     def block(b, _):
         g_copy(b).wait()
@@ -523,7 +521,7 @@
     out_copy(n_tiles - 1, (n_tiles - 1) % 2).wait()
 
 
-def owner_grad(layer, out_prev, out_shape, meta, tiles, addrs, g_rows, d_all, col):
+def owner_grad(layer, out_prev, out_shape, meta, tiles, addrs, g_rows, d_all):
     smem = pl.BlockSpec(memory_space=pltpu.SMEM)
     hbm = pl.BlockSpec(memory_space=pltpu.HBM)
     width = g_rows.shape[1] * 128
@@ -535,7 +533,7 @@
         specs.append(hbm)
         aliases = {len(args) - 1: 0}
     return pl.pallas_call(
-        functools.partial(owner_kernel, layer, col, len(d_all)),
+        functools.partial(owner_kernel, layer, len(d_all)),
         out_shape=jax.ShapeDtypeStruct(out_shape, F32),
         in_specs=specs,
         out_specs=hbm,
@@ -580,7 +578,7 @@
         perm = perm_mask.astype(BF)
         x = jnp.dot(perm, resid_in, preferred_element_type=F32).astype(BF)
         normed = rms_norm(x.astype(F32)).astype(BF)
-        u_sets = [gather(normed)]
+        u_sets = [[gather(normed)]]
 
         def flip(block, axis, bit):
             n = mesh.shape[axis]
@@ -665,21 +663,21 @@
             x, u, *kept = layer_fwd(l, l > 0, x, u, returned[l], pick, *weights)
             saved.append((x_in, *kept))
             if l < last:
-                u_sets.append(gather(u))
+                u_sets.append(spread(u, False)[0] if l == 0 else [gather(u)])
         resid_out = lax.dot_general(perm, x, (((0,), (0,)), ((), ())), preferred_element_type=F32).astype(BF)
         for l in range(last, 0, -1):
             x_in, up_pre, gate_pre, got = saved[l]
             cot, d_mixed = layer_bwd(l, cot, d_mixed, x_in, got, up_pre, gate_pre, *weights)
-            d_sets[l - 1] = spread(d_mixed, True)[0] if l == last else [gather(d_mixed)]
-
-        u_sets[0], _ = lax.optimization_barrier((u_sets[0], d_mixed))
+            d_sets[l - 1] = [gather(d_mixed)]
+
+        u_sets[0][0], _ = lax.optimization_barrier((u_sets[0][0], d_mixed))
         grads = None
         out_shape = (n_layers, range_rows // 8, width // 128, 8, 128)
         gates = []
         for l in range(n_layers):
-            gates.append(owner_gate(l, meta, u_sets[l], 0, w_gate))
+            gates.append(owner_gate(l, meta, u_sets[l], w_gate))
         for l in range(last, -1, -1):
-            grads = owner_grad(l, grads, out_shape, meta, tiles, addrs, gates[l], d_sets[l], 0)
+            grads = owner_grad(l, grads, out_shape, meta, tiles, addrs, gates[l], d_sets[l])
         d_tables = grads.transpose(0, 1, 3, 2, 4).reshape(n_layers, range_rows, width)
         return resid_out, d_tables
 

time: 678 us -> 677 us (level)
    unnamed x99 -> x111, local copies, waits for them, and re-layouts: 25.9 us -> 27.7 us
  transfers between devices with their start and end apart: 43 -> 43, of which waited for: 13 -> 19; matrix products, arithmetic and copies ran while one was open for 3% -> 3% of each run, Pallas kernels for 39% -> 39%
where the time goes in v6:
time: 677 us; the launch traced here: 672 us
  Pallas kernels  297 us (44%)
  waiting for transfers between devices  284 us (42%)
  local copies, waits for them, and re-layouts  29.3 us (4%)
  starting transfers between devices  25.1 us (4%)
  between operations  14.7 us (2%)
  other arithmetic  13.2 us (2%)
  matrix products  8.91 us (1%)
    ppermute x39, waiting for transfers between devices, flip(): return lax.ppermute(block, axis, [(i, i ^ bit) for i in range(n)])  284 us
    pallas_call x3, Pallas kernels, owner_grad(): pl.pallas_call(functools.partial(owner_kernel, layer, len(d_all)), out_sh...  111 us
    pallas_call x3, Pallas kernels, layer_fwd(): pl.pallas_call(functools.partial(forward_kernel, layer, keep), out_shape=...  57.6 us
    pallas_call x3, Pallas kernels, owner_gate(): pl.pallas_call(functools.partial(gate_kernel, layer), out_shape=pltpu.HBM...  51 us
    pallas_call x2, Pallas kernels, layer_bwd(): pl.pallas_call(functools.partial(backward_kernel, layer), out_shape=[act,...  42 us
    unnamed x111, local copies, waits for them, and re-layouts  27.7 us
    pallas_call x1, Pallas kernels, serve_rows(): pl.pallas_call(functools.partial(serve_kernel, n_layers, cap), out_shape=...  26.5 us
    ppermute x39, starting transfers between devices, flip(): return lax.ppermute(block, axis, [(i, i ^ bit) for i in range(n)])  24.6 us
  transfers between devices with their start and end apart: 43, of which 19 were waited for; matrix products, arithmetic and copies ran while one was open for 3% of the time, Pallas kernels for 39%

profile of v6, /device:TPU:0, one launch (start us, length us, event | category | flops | bytes accessed | tf_op | source)
XLA Modules:
  0.0 672.4 jit_solution(12834719847433853132)
XLA Ops:
  9.2 1.2 fusion.1.u_ref
  12.3 9.0 %share_ids.1 = s32[16,4,128]{2,1,0:T(4,128)} custom-call(s32[4,128]{1,0:T(4,128)} %bitcast.46), custom_call_target="tpu_custom_call" | custom-call | tf_op jit(solution)/shard_map/share_ids/pallas_call | solution.py:57
  24.9 26.5 %serve_rows.1 = (bf16[256,1024]{1,0:T(8,128)(2,1)S(1)}, bf16[256,1024]{1,0:T(8,128)(2,1)}, bf16[256,1024]{1,0:T(8,128)(2,1)}, bf16[256,1024]{1,0:T(8,128)(2,1)},...) custom-call(s32[4]{0:T(128)S(1)} %get-tuple-element.75.cnt_ref, ...), custom_call_target="tpu_custom_call" | custom-call | flops 20000000000 | bytes 30000000 | tf_op jit(solution)/shard_map/serve_rows/pallas_call | solution.py:344
  56.2 1.9 collective-permute-start.2
  60.1 5.6 sort.7
  68.3 1.5 collective-permute-start.5
  69.7 12.7 %collective-permute-done.1.r2_ref = bf16[256,1024]{1,0:T(8,128)(2,1)S(1)} collective-permute-done((bf16[256,1024]{1,0:T(8,128)(2,1)}, bf16[256,1024]{1,0:T(8,128)(2,1)S(1)}, u32[]{:S(2)}, u32[]{:S(2)}) %collective-permute-start.1) | collective-permute-done | bytes 524320 | tf_op jit(solution)/shard_map/ppermute | solution.py:585
  83.2 21.1 %collective-permute-done.2.r3_ref = bf16[256,1024]{1,0:T(8,128)(2,1)} collective-permute-done((bf16[256,1024]{1,0:T(8,128)(2,1)}, bf16[256,1024]{1,0:T(8,128)(2,1)}, u32[]{:S(2)}, u32[]{:S(2)}) %collective-permute-start.2) | collective-permute-done | bytes 524320 | tf_op jit(solution)/shard_map/ppermute | solution.py:585
  108.7 17.6 %shard_map.95 = (bf16[512,1024]{1,0:T(8,128)(2,1)S(1)}, bf16[512,1024]{1,0:T(8,128)(2,1)S(1)}) custom-call(bf16[512,1024]{1,0:T(8,128)(2,1)S(1)} %copy-done.12, bf16[512,1024]{1,0:T(8,128)(2,1)S(1)} %copy-done.5, bf16[256,1024]{1,0:T(8,128)(2,1)S(1)} %copy-done.23, bf16[256,1024]{1,0:T(8,128)(2,1)S(1)} %copy-done.25, bf16[256,1024]{1,0:T(8,128)(2,1)S(1)} %copy-done.27, ...), custom_call_target="tpu_custom_call" | custom-call | flops 11000000512 | bytes 30000000 | tf_op jit(solution)/shard_map/pallas_call | solution.py:196
  126.3 6.6 collective-permute-done.5.r3_ref
  132.9 19.9 %shard_map.96 = (bf16[512,1024]{1,0:T(8,128)(2,1)S(1)}, bf16[512,1024]{1,0:T(8,128)(2,1)}, f32[512,4096]{1,0:T(8,128)}, f32[512,1024]{1,0:T(8,128)}, bf16[512,1024]{1,0:T(8,128)(2,1)S(1)}) custom-call(bf16[512,1024]{1,0:T(8,128)(2,1)S(1)} %get-tuple-element.41.x_ref, bf16[512,1024]{1,0:T(8,128)(2,1)S(1)} %get-tuple-element.42.u_ref.rest_0_, ...), custom_call_target="tpu_custom_call" | custom-call | flops 11000000512 | bytes 30000000 | tf_op jit(solution)/shard_map/pallas_call | solution.py:196
  155.7 1.3 collective-permute-start.8
  157.0 1.9 convolution_convert_fusion.cot_ref
  159.0 3.2 fusion.6.dm_ref.rest_0_
  162.2 14.0 %collective-permute-done.7.r2_ref = bf16[256,1024]{1,0:T(8,128)(2,1)S(1)} collective-permute-done((bf16[256,1024]{1,0:T(8,128)(2,1)}, bf16[256,1024]{1,0:T(8,128)(2,1)S(1)}, u32[]{:S(2)}, u32[]{:S(2)}) %collective-permute-start.7) | collective-permute-done | bytes 524320 | tf_op jit(solution)/shard_map/ppermute | solution.py:585
  176.2 14.2 %collective-permute-done.8.r3_ref = bf16[256,1024]{1,0:T(8,128)(2,1)S(1)} collective-permute-done((bf16[256,1024]{1,0:T(8,128)(2,1)}, bf16[256,1024]{1,0:T(8,128)(2,1)S(1)}, u32[]{:S(2)}, u32[]{:S(2)}) %collective-permute-start.8) | collective-permute-done | bytes 524320 | tf_op jit(solution)/shard_map/ppermute | solution.py:585
  190.4 20.1 %shard_map.97 = (bf16[512,1024]{1,0:T(8,128)(2,1)S(1)}, bf16[512,1024]{1,0:T(8,128)(2,1)}, f32[512,4096]{1,0:T(8,128)}, f32[512,1024]{1,0:T(8,128)}, bf16[512,1024]{1,0:T(8,128)(2,1)S(1)}) custom-call(bf16[512,1024]{1,0:T(8,128)(2,1)S(1)} %copy-done.8, bf16[512,1024]{1,0:T(8,128)(2,1)} %get-tuple-element.48.u_ref, bf16[256,1024]{1,0:T(8,128)(2,1)S(1)} %copy-done.19, ...), custom_call_target="tpu_custom_call" | custom-call | flops 11000000512 | bytes 30000000 | tf_op jit(solution)/shard_map/pallas_call | solution.py:196
  210.5 20.9 %shard_map.98 = (bf16[512,1024]{1,0:T(8,128)(2,1)S(1)}, bf16[512,1024]{1,0:T(8,128)(2,1)}) custom-call(bf16[512,1024]{1,0:T(8,128)(2,1)S(1)} %convolution_convert_fusion.cot_ref, bf16[512,1024]{1,0:T(8,128)(2,1)S(1)} %fusion.6.dm_ref.rest_0_, bf16[512,1024]{1,0:T(8,128)(2,1)S(1)} %copy-done.8, bf16[512,1024]{1,0:T(8,128)(2,1)S(1)} %get-tuple-element.58.got_ref, ...), custom_call_target="tpu_custom_call" | custom-call | flops 11000000512 | bytes 40000000 | tf_op jit(solution)/shard_map/pallas_call | solution.py:275
  232.6 1.4 copy-done.14
  235.3 21.1 %shard_map.99 = (bf16[512,1024]{1,0:T(8,128)(2,1)}, bf16[512,1024]{1,0:T(8,128)(2,1)S(1)}) custom-call(bf16[512,1024]{1,0:T(8,128)(2,1)S(1)} %copy-done.16, bf16[512,1024]{1,0:T(8,128)(2,1)} %get-tuple-element.62.dm_ref, bf16[512,1024]{1,0:T(8,128)(2,1)S(1)} %get-tuple-element.41.x_ref, bf16[512,1024]{1,0:T(8,128)(2,1)S(1)} %copy-done.14, ...), custom_call_target="tpu_custom_call" | custom-call | flops 11000000512 | bytes 40000000 | tf_op jit(solution)/shard_map/pallas_call | solution.py:275
  257.4 1.5 collective-permute-start.26
  259.0 2.9 collective-permute-start.24
  262.4 1.2 collective-permute-start.11
  263.6 33.6 %collective-permute-done.26.rest_3_ = bf16[512,1024]{1,0:T(8,128)(2,1)S(1)} collective-permute-done((bf16[512,1024]{1,0:T(8,128)(2,1)S(1)}, bf16[512,1024]{1,0:T(8,128)(2,1)S(1)}, u32[]{:S(2)}, u32[]{:S(2)}) %collective-permute-start.26) | collective-permute-done | bytes 1048608 | tf_op jit(solution)/shard_map/ppermute | solution.py:585
  298.4 1.5 collective-permute-done.25.rest_2_
  299.9 1.6 collective-permute-start.9
  302.8 33.5 %collective-permute-done.11.rest_3_ = bf16[512,1024]{1,0:T(8,128)(2,1)S(1)} collective-permute-done((bf16[512,1024]{1,0:T(8,128)(2,1)S(1)}, bf16[512,1024]{1,0:T(8,128)(2,1)S(1)}, u32[]{:S(2)}, u32[]{:S(2)}) %collective-permute-start.11) | collective-permute-done | bytes 1048608 | tf_op jit(solution)/shard_map/ppermute | solution.py:585
  336.9 2.6 collective-permute-done.10.rest_2_
  339.6 7.1 %collective-permute-done.9.rest_1_ = bf16[512,1024]{1,0:T(8,128)(2,1)S(1)} collective-permute-done((bf16[512,1024]{1,0:T(8,128)(2,1)S(1)}, bf16[512,1024]{1,0:T(8,128)(2,1)S(1)}, u32[]{:S(2)}, u32[]{:S(2)}) %collective-permute-start.9) | collective-permute-done | bytes 1048608 | tf_op jit(solution)/shard_map/ppermute | solution.py:585
  347.6 30.8 %collective-permute-done.28.rest_5_ = bf16[512,1024]{1,0:T(8,128)(2,1)S(1)} collective-permute-done((bf16[512,1024]{1,0:T(8,128)(2,1)S(1)}, bf16[512,1024]{1,0:T(8,128)(2,1)S(1)}, u32[]{:S(2)}, u32[]{:S(2)}) %collective-permute-start.28) | collective-permute-done | bytes 1048608 | tf_op jit(solution)/shard_map/ppermute | solution.py:585
  378.4 37.6 %collective-permute-done.13.rest_5_ = bf16[512,1024]{1,0:T(8,128)(2,1)S(1)} collective-permute-done((bf16[512,1024]{1,0:T(8,128)(2,1)S(1)}, bf16[512,1024]{1,0:T(8,128)(2,1)S(1)}, u32[]{:S(2)}, u32[]{:S(2)}) %collective-permute-start.13) | collective-permute-done | bytes 1048608 | tf_op jit(solution)/shard_map/ppermute | solution.py:585
  417.0 37.8 %collective-permute-done.12.rest_4_ = bf16[512,1024]{1,0:T(8,128)(2,1)S(1)} collective-permute-done((bf16[512,1024]{1,0:T(8,128)(2,1)S(1)}, bf16[512,1024]{1,0:T(8,128)(2,1)S(1)}, u32[]{:S(2)}, u32[]{:S(2)}) %collective-permute-start.12) | collective-permute-done | bytes 1048608 | tf_op jit(solution)/shard_map/ppermute | solution.py:585
  455.9 1.6 collective-permute-done.19.rest_11_
  459.3 2.5 collective-permute-start.27
  461.7 1.3 collective-permute-done.22.rest_14_
  463.2 1.8 collective-permute-done.23.rest_15_
  465.7 3.0 convolution_convert_fusion.1
  468.8 2.8 copy-done.2
  471.6 17.2 %shard_map.101.g_hbm = f32[544,8,8,128]{3,2,1,0:T(8,128)} custom-call(s32[65]{0:T(128)S(1)} %concatenate.6.meta_ref, bf16[3,1024,1024]{2,1,0:T(8,128)(2,1)S(1)} %copy-done.2, bf16[512,1024]{1,0:T(8,128)(2,1)} %copy-done.9, bf16[512,1024]{1,0:T(8,128)(2,1)} %copy-done.38, bf16[512,1024]{1,0:T(8,128)(2,1)} %copy-done.37, bf16[512,1024]{1,0:T(8,128)(2,1)} %copy-done.36, ...), custom_call_target="tpu_custom_call" | custom-call | flops 10000000000 | bytes 30000000 | tf_op jit(solution)/shard_map/pallas_call | solution.py:428
  488.8 9.2 %collective-permute-done.27.rest_4_ = bf16[512,1024]{1,0:T(8,128)(2,1)} collective-permute-done((bf16[512,1024]{1,0:T(8,128)(2,1)}, bf16[512,1024]{1,0:T(8,128)(2,1)}, u32[]{:S(2)}, u32[]{:S(2)}) %collective-permute-start.27) | collective-permute-done | bytes 1048608 | tf_op jit(solution)/shard_map/ppermute | solution.py:585
  499.0 16.0 %collective-permute-done.30.rest_7_ = bf16[512,1024]{1,0:T(8,128)(2,1)} collective-permute-done((bf16[512,1024]{1,0:T(8,128)(2,1)S(1)}, bf16[512,1024]{1,0:T(8,128)(2,1)}, u32[]{:S(2)}, u32[]{:S(2)}) %collective-permute-start.30) | collective-permute-done | bytes 1048608 | tf_op jit(solution)/shard_map/ppermute | solution.py:585
  515.0 2.8 copy-done.3
  517.8 17.0 %shard_map.100.g_hbm = f32[544,8,8,128]{3,2,1,0:T(8,128)} custom-call(s32[65]{0:T(128)S(1)} %concatenate.6.meta_ref, bf16[3,1024,1024]{2,1,0:T(8,128)(2,1)S(1)} %copy-done.3, bf16[8192,1024]{1,0:T(8,128)(2,1)} %all-gather.5.cloned.1.call-done.rest_0_), custom_call_target="tpu_custom_call" | custom-call | flops 10000000000 | bytes 30000000 | tf_op jit(solution)/shard_map/pallas_call | solution.py:428
  534.8 2.8 copy-done.4
  537.6 16.9 %shard_map.102.g_hbm = f32[544,8,8,128]{3,2,1,0:T(8,128)} custom-call(s32[65]{0:T(128)S(1)} %concatenate.6.meta_ref, bf16[3,1024,1024]{2,1,0:T(8,128)(2,1)S(1)} %copy-done.4, bf16[8192,1024]{1,0:T(8,128)(2,1)} %all-gather.11.cloned.1.call-done.rest_0_), custom_call_target="tpu_custom_call" | custom-call | flops 10000000000 | bytes 30000000 | tf_op jit(solution)/shard_map/pallas_call | solution.py:428
  554.6 37.0 %shard_map.103.rest_1_ = f32[3,2048,8,8,128]{4,3,2,1,0:T(8,128)} custom-call(s32[65]{0:T(128)S(1)} %concatenate.6.meta_ref, s32[17]{0:T(128)S(1)} %convert_reduce_fusion.2.tile_ref, s32[4096]{0:T(1024)S(1)} %fusion.18.addr_ref, f32[544,8,8,128]{3,2,1,0:T(8,128)} %shard_map.102.g_hbm, bf16[512,1024]{1,0:T(8,128)(2,1)} %copy-done.6, ...), custom_call_target="tpu_custom_call" | custom-call | flops 40000000000 | bytes 100000000 | tf_op jit(solution)/shard_map/pallas_call | solution.py:535
  591.6 37.0 %shard_map.104.rest_1_ = f32[3,2048,8,8,128]{4,3,2,1,0:T(8,128)} custom-call(s32[65]{0:T(128)S(1)} %concatenate.6.meta_ref, s32[17]{0:T(128)S(1)} %convert_reduce_fusion.2.tile_ref, s32[4096]{0:T(1024)S(1)} %fusion.18.addr_ref, f32[544,8,8,128]{3,2,1,0:T(8,128)} %shard_map.101.g_hbm, ...), custom_call_target="tpu_custom_call", output_to_operand_aliasing={{}: (5, {})} | custom-call | flops 40000000000 | bytes 100000000 | tf_op jit(solution)/shard_map/pallas_call | solution.py:535
  628.6 37.0 %shard_map.105 = f32[3,2048,8,8,128]{4,3,2,1,0:T(8,128)} custom-call(s32[65]{0:T(128)S(1)} %concatenate.6.meta_ref, s32[17]{0:T(128)S(1)} %convert_reduce_fusion.2.tile_ref, s32[4096]{0:T(1024)S(1)} %fusion.18.addr_ref, f32[544,8,8,128]{3,2,1,0:T(8,128)} %shard_map.100.g_hbm, ...), custom_call_target="tpu_custom_call", output_to_operand_aliasing={{}: (5, {})} | custom-call | flops 40000000000 | bytes 100000000 | tf_op jit(solution)/shard_map/pallas_call | solution.py:535
  (202 shorter events, 38.8 us)
Async XLA Ops:
  7.2 481.6 %all-gather.5.cloned.1.call-start = ((), (), s32[]{:S(2)}) async-start(), calls=%async_computation | async-start | bytes 17825792 | tf_op jit(solution)/shard_map/all_gather | solution.py:572
  11.5 523.4 %all-gather.11.cloned.1.call-start = ((), (), s32[]{:S(2)}) async-start(), calls=%async_computation.3 | async-start | bytes 17825792 | tf_op jit(solution)/shard_map/all_gather | solution.py:572
  56.2 11.2 %collective-permute-start = (bf16[256,1024]{1,0:T(8,128)(2,1)}, bf16[256,1024]{1,0:T(8,128)(2,1)S(1)}, u32[]{:S(2)}, u32[]{:S(2)}) collective-permute-start(bf16[256,1024]{1,0:T(8,128)(2,1)} %get-tuple-element.37), channel_id=1, source_target_pairs={{0,1},{1,0},{2,3},{3,2},{4,5},{5,4},{6,7},{7,6},{8,9},{9,8},{10,11... | collective-permute-start | bytes 1572872 | tf_op jit(solution)/shard_map/ppermute | solution.py:585
  56.2 26.2 %collective-permute-start.1 = (bf16[256,1024]{1,0:T(8,128)(2,1)}, bf16[256,1024]{1,0:T(8,128)(2,1)S(1)}, u32[]{:S(2)}, u32[]{:S(2)}) collective-permute-start(bf16[256,1024]{1,0:T(8,128)(2,1)} %get-tuple-element.38), channel_id=1, source_target_pairs={{0,2},{1,3},{2,0},{3,1},{4,6},{5,7},{6,4},{7,5},{8,10},{9,11},{10,... | collective-permute-start | bytes 1572872 | tf_op jit(solution)/shard_map/ppermute | solution.py:585
  56.2 48.1 %collective-permute-start.2 = (bf16[256,1024]{1,0:T(8,128)(2,1)}, bf16[256,1024]{1,0:T(8,128)(2,1)}, u32[]{:S(2)}, u32[]{:S(2)}) collective-permute-start(bf16[256,1024]{1,0:T(8,128)(2,1)} %get-tuple-element.39), channel_id=1, source_target_pairs={{0,3},{1,2},{2,1},{3,0},{4,7},{5,6},{6,5},{7,4},{8,11},{9,10},{10,... | collective-permute-start | bytes 1572872 | tf_op jit(solution)/shard_map/ppermute | solution.py:585
  58.1 68.2 %collective-permute-start.3 = (bf16[256,1024]{1,0:T(8,128)(2,1)}, bf16[256,1024]{1,0:T(8,128)(2,1)}, u32[]{:S(2)}, u32[]{:S(2)}) collective-permute-start(bf16[256,1024]{1,0:T(8,128)(2,1)} %get-tuple-element.44), channel_id=1, source_target_pairs={{0,1},{1,0},{2,3},{3,2},{4,5},{5,4},{6,7},{7,6},{8,9},{9,8},{10,11... | collective-permute-start | bytes 1572872 | tf_op jit(solution)/shard_map/ppermute | solution.py:585
  58.4 68.0 %collective-permute-start.4 = (bf16[256,1024]{1,0:T(8,128)(2,1)}, bf16[256,1024]{1,0:T(8,128)(2,1)}, u32[]{:S(2)}, u32[]{:S(2)}) collective-permute-start(bf16[256,1024]{1,0:T(8,128)(2,1)} %get-tuple-element.45), channel_id=1, source_target_pairs={{0,2},{1,3},{2,0},{3,1},{4,6},{5,7},{6,4},{7,5},{8,10},{9,11},{10,... | collective-permute-start | bytes 1572872 | tf_op jit(solution)/shard_map/ppermute | solution.py:585
  68.3 64.6 %collective-permute-start.5 = (bf16[256,1024]{1,0:T(8,128)(2,1)}, bf16[256,1024]{1,0:T(8,128)(2,1)S(1)}, u32[]{:S(2)}, u32[]{:S(2)}) collective-permute-start(bf16[256,1024]{1,0:T(8,128)(2,1)} %copy-done.31), channel_id=1, source_target_pairs={{0,3},{1,2},{2,1},{3,0},{4,7},{5,6},{6,5},{7,4},{8,11},{9,10},{10,... | collective-permute-start | bytes 1572872 | tf_op jit(solution)/shard_map/ppermute | solution.py:585
  154.9 436.7 %all-gather.9.cloned.1.call-start = ((), (), s32[]{:S(2)}) async-start(), calls=%async_computation.2 | async-start | bytes 17825792 | tf_op jit(solution)/shard_map/all_gather | solution.py:572
  155.1 7.1 %collective-permute-start.6 = (bf16[256,1024]{1,0:T(8,128)(2,1)}, bf16[256,1024]{1,0:T(8,128)(2,1)S(1)}, u32[]{:S(2)}, u32[]{:S(2)}) collective-permute-start(bf16[256,1024]{1,0:T(8,128)(2,1)} %copy-done.30), channel_id=1, source_target_pairs={{0,1},{1,0},{2,3},{3,2},{4,5},{5,4},{6,7},{7,6},{8,9},{9,8},{10,11... | collective-permute-start | bytes 1572872 | tf_op jit(solution)/shard_map/ppermute | solution.py:585
  155.3 20.9 %collective-permute-start.7 = (bf16[256,1024]{1,0:T(8,128)(2,1)}, bf16[256,1024]{1,0:T(8,128)(2,1)S(1)}, u32[]{:S(2)}, u32[]{:S(2)}) collective-permute-start(bf16[256,1024]{1,0:T(8,128)(2,1)} %copy-done.29), channel_id=1, source_target_pairs={{0,2},{1,3},{2,0},{3,1},{4,6},{5,7},{6,4},{7,5},{8,10},{9,11},{10,... | collective-permute-start | bytes 1572872 | tf_op jit(solution)/shard_map/ppermute | solution.py:585
  155.7 34.6 %collective-permute-start.8 = (bf16[256,1024]{1,0:T(8,128)(2,1)}, bf16[256,1024]{1,0:T(8,128)(2,1)S(1)}, u32[]{:S(2)}, u32[]{:S(2)}) collective-permute-start(bf16[256,1024]{1,0:T(8,128)(2,1)} %get-tuple-element.52), channel_id=1, source_target_pairs={{0,3},{1,2},{2,1},{3,0},{4,7},{5,6},{6,5},{7,4},{8,11},{9,10},{10,... | collective-permute-start | bytes 1572872 | tf_op jit(solution)/shard_map/ppermute | solution.py:585
  232.4 396.2 %all-gather.7.cloned.1.call-start = ((), (), s32[]{:S(2)}) async-start(), calls=%async_computation.1 | async-start | bytes 17825792 | tf_op jit(solution)/shard_map/all_gather | solution.py:572
  257.4 39.8 %collective-permute-start.26 = (bf16[512,1024]{1,0:T(8,128)(2,1)S(1)}, bf16[512,1024]{1,0:T(8,128)(2,1)S(1)}, u32[]{:S(2)}, u32[]{:S(2)}) collective-permute-start(bf16[512,1024]{1,0:T(8,128)(2,1)S(1)} %fusion.6.dm_ref.rest_0_), channel_id=1, source_target_pairs={{0,2},{1,3},{2,0},{3,1},{4,6},{5,7},{6,4},{7,5},{8,10},{9,11},{10,... | collective-permute-start | bytes 3145736 | tf_op jit(solution)/shard_map/ppermute | solution.py:585
  258.9 40.9 %collective-permute-start.25 = (bf16[512,1024]{1,0:T(8,128)(2,1)S(1)}, bf16[512,1024]{1,0:T(8,128)(2,1)}, u32[]{:S(2)}, u32[]{:S(2)}) collective-permute-start(bf16[512,1024]{1,0:T(8,128)(2,1)S(1)} %fusion.6.dm_ref.rest_0_), channel_id=1, source_target_pairs={{0,4},{4,0},{8,12},{12,8},{1,5},{5,1},{9,13},{13,9},{2,6},{6,2},{1... | collective-permute-start | bytes 3145736 | tf_op jit(solution)/shard_map/ppermute | solution.py:585
  259.0 42.5 %collective-permute-start.24 = (bf16[512,1024]{1,0:T(8,128)(2,1)S(1)}, bf16[512,1024]{1,0:T(8,128)(2,1)}, u32[]{:S(2)}, u32[]{:S(2)}) collective-permute-start(bf16[512,1024]{1,0:T(8,128)(2,1)S(1)} %fusion.6.dm_ref.rest_0_), channel_id=1, source_target_pairs={{0,8},{4,12},{8,0},{12,4},{1,9},{5,13},{9,1},{13,5},{2,10},{6,14},... | collective-permute-start | bytes 3145736 | tf_op jit(solution)/shard_map/ppermute | solution.py:585
  261.8 40.1 %collective-permute-start.31 = (bf16[512,1024]{1,0:T(8,128)(2,1)S(1)}, bf16[512,1024]{1,0:T(8,128)(2,1)S(1)}, u32[]{:S(2)}, u32[]{:S(2)}) collective-permute-start(bf16[512,1024]{1,0:T(8,128)(2,1)S(1)} %fusion.6.dm_ref.rest_0_), channel_id=1, source_target_pairs={{0,1},{1,0},{2,3},{3,2},{4,5},{5,4},{6,7},{7,6},{8,9},{9,8},{10,11... | collective-permute-start | bytes 3145736 | tf_op jit(solution)/shard_map/ppermute | solution.py:585
  262.4 73.9 %collective-permute-start.11 = (bf16[512,1024]{1,0:T(8,128)(2,1)S(1)}, bf16[512,1024]{1,0:T(8,128)(2,1)S(1)}, u32[]{:S(2)}, u32[]{:S(2)}) collective-permute-start(bf16[512,1024]{1,0:T(8,128)(2,1)S(1)} %copy-done.10), channel_id=1, source_target_pairs={{0,2},{1,3},{2,0},{3,1},{4,6},{5,7},{6,4},{7,5},{8,10},{9,11},{10,... | collective-permute-start | bytes 3145736 | tf_op jit(solution)/shard_map/ppermute | solution.py:585
  297.2 200.7 %copy-start.32 = (bf16[512,1024]{1,0:T(8,128)(2,1)}, bf16[512,1024]{1,0:T(8,128)(2,1)S(1)}, u32[]{:S(2)}) copy-start(bf16[512,1024]{1,0:T(8,128)(2,1)S(1)} %collective-permute-done.26.rest_3_) | copy-start | bytes 3145732
  297.2 42.3 %collective-permute-start.10 = (bf16[512,1024]{1,0:T(8,128)(2,1)S(1)}, bf16[512,1024]{1,0:T(8,128)(2,1)S(1)}, u32[]{:S(2)}, u32[]{:S(2)}) collective-permute-start(bf16[512,1024]{1,0:T(8,128)(2,1)S(1)} %copy-done.10), channel_id=1, source_target_pairs={{0,4},{4,0},{8,12},{12,8},{1,5},{5,1},{9,13},{13,9},{2,6},{6,2},{1... | collective-permute-start | bytes 3145736 | tf_op jit(solution)/shard_map/ppermute | solution.py:585
  299.9 46.8 %collective-permute-start.9 = (bf16[512,1024]{1,0:T(8,128)(2,1)S(1)}, bf16[512,1024]{1,0:T(8,128)(2,1)S(1)}, u32[]{:S(2)}, u32[]{:S(2)}) collective-permute-start(bf16[512,1024]{1,0:T(8,128)(2,1)S(1)} %copy-done.10), channel_id=1, source_target_pairs={{0,8},{4,12},{8,0},{12,4},{1,9},{5,13},{9,1},{13,5},{2,10},{6,14},... | collective-permute-start | bytes 3145736 | tf_op jit(solution)/shard_map/ppermute | solution.py:585
  301.5 46.2 %collective-permute-start.16 = (bf16[512,1024]{1,0:T(8,128)(2,1)S(1)}, bf16[512,1024]{1,0:T(8,128)(2,1)S(1)}, u32[]{:S(2)}, u32[]{:S(2)}) collective-permute-start(bf16[512,1024]{1,0:T(8,128)(2,1)S(1)} %copy-done.10), channel_id=1, source_target_pairs={{0,1},{1,0},{2,3},{3,2},{4,5},{5,4},{6,7},{7,6},{8,9},{9,8},{10,11... | collective-permute-start | bytes 3145736 | tf_op jit(solution)/shard_map/ppermute | solution.py:585
  301.9 154.1 %copy-start.33 = (bf16[512,1024]{1,0:T(8,128)(2,1)}, bf16[512,1024]{1,0:T(8,128)(2,1)S(1)}, u32[]{:S(2)}) copy-start(bf16[512,1024]{1,0:T(8,128)(2,1)S(1)} %collective-permute-done.31.rest_8_) | copy-start | bytes 3145732
  301.9 76.5 %collective-permute-start.28 = (bf16[512,1024]{1,0:T(8,128)(2,1)S(1)}, bf16[512,1024]{1,0:T(8,128)(2,1)S(1)}, u32[]{:S(2)}, u32[]{:S(2)}) collective-permute-start(bf16[512,1024]{1,0:T(8,128)(2,1)S(1)} %collective-permute-done.26.rest_3_), channel_id=1, source_target_pairs={{0,8},{4,12},{8,0},{12,4},{1,9},{5,13},{9,1},{13,5},{2,10},{6,14},... | collective-permute-start | bytes 3145736 | tf_op jit(solution)/shard_map/ppermute | solution.py:585
  336.3 132.4 %copy-start.36 = (bf16[512,1024]{1,0:T(8,128)(2,1)}, bf16[512,1024]{1,0:T(8,128)(2,1)S(1)}, u32[]{:S(2)}) copy-start(bf16[512,1024]{1,0:T(8,128)(2,1)S(1)} %collective-permute-done.11.rest_3_) | copy-start | bytes 3145732
  336.3 79.7 %collective-permute-start.13 = (bf16[512,1024]{1,0:T(8,128)(2,1)S(1)}, bf16[512,1024]{1,0:T(8,128)(2,1)S(1)}, u32[]{:S(2)}, u32[]{:S(2)}) collective-permute-start(bf16[512,1024]{1,0:T(8,128)(2,1)S(1)} %collective-permute-done.11.rest_3_), channel_id=1, source_target_pairs={{0,8},{4,12},{8,0},{12,4},{1,9},{5,13},{9,1},{13,5},{2,10},{6,14},... | collective-permute-start | bytes 3145736 | tf_op jit(solution)/shard_map/ppermute | solution.py:585
  339.6 129.1 %copy-start.37 = (bf16[512,1024]{1,0:T(8,128)(2,1)}, bf16[512,1024]{1,0:T(8,128)(2,1)S(1)}, u32[]{:S(2)}) copy-start(bf16[512,1024]{1,0:T(8,128)(2,1)S(1)} %collective-permute-done.10.rest_2_) | copy-start | bytes 3145732
  339.6 115.3 %collective-permute-start.12 = (bf16[512,1024]{1,0:T(8,128)(2,1)S(1)}, bf16[512,1024]{1,0:T(8,128)(2,1)S(1)}, u32[]{:S(2)}, u32[]{:S(2)}) collective-permute-start(bf16[512,1024]{1,0:T(8,128)(2,1)S(1)} %collective-permute-done.10.rest_2_), channel_id=1, source_target_pairs={{0,8},{4,12},{8,0},{12,4},{1,9},{5,13},{9,1},{13,5},{2,10},{6,14},... | collective-permute-start | bytes 3145736 | tf_op jit(solution)/shard_map/ppermute | solution.py:585
  346.7 122.0 %copy-start.38 = (bf16[512,1024]{1,0:T(8,128)(2,1)}, bf16[512,1024]{1,0:T(8,128)(2,1)S(1)}, u32[]{:S(2)}) copy-start(bf16[512,1024]{1,0:T(8,128)(2,1)S(1)} %collective-permute-done.9.rest_1_) | copy-start | bytes 3145732
  346.7 108.2 %collective-permute-start.14 = (bf16[512,1024]{1,0:T(8,128)(2,1)S(1)}, bf16[512,1024]{1,0:T(8,128)(2,1)S(1)}, u32[]{:S(2)}, u32[]{:S(2)}) collective-permute-start(bf16[512,1024]{1,0:T(8,128)(2,1)S(1)} %collective-permute-done.11.rest_3_), channel_id=1, source_target_pairs={{0,4},{4,0},{8,12},{12,8},{1,5},{5,1},{9,13},{13,9},{2,6},{6,2},{1... | collective-permute-start | bytes 3145736 | tf_op jit(solution)/shard_map/ppermute | solution.py:585
  347.6 107.7 %collective-permute-start.17 = (bf16[512,1024]{1,0:T(8,128)(2,1)S(1)}, bf16[512,1024]{1,0:T(8,128)(2,1)S(1)}, u32[]{:S(2)}, u32[]{:S(2)}) collective-permute-start(bf16[512,1024]{1,0:T(8,128)(2,1)S(1)} %collective-permute-done.9.rest_1_), channel_id=1, source_target_pairs={{0,1},{1,0},{2,3},{3,2},{4,5},{5,4},{6,7},{7,6},{8,9},{9,8},{10,11... | collective-permute-start | bytes 3145736 | tf_op jit(solution)/shard_map/ppermute | solution.py:585
  378.4 77.0 %collective-permute-start.18 = (bf16[512,1024]{1,0:T(8,128)(2,1)S(1)}, bf16[512,1024]{1,0:T(8,128)(2,1)S(1)}, u32[]{:S(2)}, u32[]{:S(2)}) collective-permute-start(bf16[512,1024]{1,0:T(8,128)(2,1)S(1)} %collective-permute-done.10.rest_2_), channel_id=1, source_target_pairs={{0,1},{1,0},{2,3},{3,2},{4,5},{5,4},{6,7},{7,6},{8,9},{9,8},{10,11... | collective-permute-start | bytes 3145736 | tf_op jit(solution)/shard_map/ppermute | solution.py:585
  416.0 39.8 %collective-permute-start.15 = (bf16[512,1024]{1,0:T(8,128)(2,1)S(1)}, bf16[512,1024]{1,0:T(8,128)(2,1)S(1)}, u32[]{:S(2)}, u32[]{:S(2)}) collective-permute-start(bf16[512,1024]{1,0:T(8,128)(2,1)S(1)} %collective-permute-done.13.rest_5_), channel_id=1, source_target_pairs={{0,4},{4,0},{8,12},{12,8},{1,5},{5,1},{9,13},{13,9},{2,6},{6,2},{1... | collective-permute-start | bytes 3145736 | tf_op jit(solution)/shard_map/ppermute | solution.py:585
  454.8 2.7 collective-permute-start.19
  454.8 4.4 collective-permute-start.20
  455.4 6.4 collective-permute-start.21
  455.4 7.6 %collective-permute-start.22 = (bf16[512,1024]{1,0:T(8,128)(2,1)S(1)}, bf16[512,1024]{1,0:T(8,128)(2,1)S(1)}, u32[]{:S(2)}, u32[]{:S(2)}) collective-permute-start(bf16[512,1024]{1,0:T(8,128)(2,1)S(1)} %collective-permute-done.14.rest_6_), channel_id=1, source_target_pairs={{0,1},{1,0},{2,3},{3,2},{4,5},{5,4},{6,7},{7,6},{8,9},{9,8},{10,11... | collective-permute-start | bytes 3145736 | tf_op jit(solution)/shard_map/ppermute | solution.py:585
  455.9 9.1 %collective-permute-start.23 = (bf16[512,1024]{1,0:T(8,128)(2,1)S(1)}, bf16[512,1024]{1,0:T(8,128)(2,1)S(1)}, u32[]{:S(2)}, u32[]{:S(2)}) collective-permute-start(bf16[512,1024]{1,0:T(8,128)(2,1)S(1)} %collective-permute-done.15.rest_7_), channel_id=1, source_target_pairs={{0,1},{1,0},{2,3},{3,2},{4,5},{5,4},{6,7},{7,6},{8,9},{9,8},{10,11... | collective-permute-start | bytes 3145736 | tf_op jit(solution)/shard_map/ppermute | solution.py:585
  457.5 40.5 %collective-permute-start.29 = (bf16[512,1024]{1,0:T(8,128)(2,1)S(1)}, bf16[512,1024]{1,0:T(8,128)(2,1)S(1)}, u32[]{:S(2)}, u32[]{:S(2)}) collective-permute-start(bf16[512,1024]{1,0:T(8,128)(2,1)S(1)} %collective-permute-done.26.rest_3_), channel_id=1, source_target_pairs={{0,4},{4,0},{8,12},{12,8},{1,5},{5,1},{9,13},{13,9},{2,6},{6,2},{1... | collective-permute-start | bytes 3145736 | tf_op jit(solution)/shard_map/ppermute | solution.py:585
  459.3 38.7 %collective-permute-start.27 = (bf16[512,1024]{1,0:T(8,128)(2,1)}, bf16[512,1024]{1,0:T(8,128)(2,1)}, u32[]{:S(2)}, u32[]{:S(2)}) collective-permute-start(bf16[512,1024]{1,0:T(8,128)(2,1)} %collective-permute-done.25.rest_2_), channel_id=1, source_target_pairs={{0,8},{4,12},{8,0},{12,4},{1,9},{5,13},{9,1},{13,5},{2,10},{6,14},... | collective-permute-start | bytes 3145736 | tf_op jit(solution)/shard_map/ppermute | solution.py:585
  461.7 36.8 %collective-permute-start.33 = (bf16[512,1024]{1,0:T(8,128)(2,1)}, bf16[512,1024]{1,0:T(8,128)(2,1)}, u32[]{:S(2)}, u32[]{:S(2)}) collective-permute-start(bf16[512,1024]{1,0:T(8,128)(2,1)} %collective-permute-done.25.rest_2_), channel_id=1, source_target_pairs={{0,1},{1,0},{2,3},{3,2},{4,5},{5,4},{6,7},{7,6},{8,9},{9,8},{10,11... | collective-permute-start | bytes 3145736 | tf_op jit(solution)/shard_map/ppermute | solution.py:585
  463.1 35.5 %collective-permute-start.32 = (bf16[512,1024]{1,0:T(8,128)(2,1)}, bf16[512,1024]{1,0:T(8,128)(2,1)}, u32[]{:S(2)}, u32[]{:S(2)}) collective-permute-start(bf16[512,1024]{1,0:T(8,128)(2,1)} %collective-permute-done.24.rest_1_), channel_id=1, source_target_pairs={{0,1},{1,0},{2,3},{3,2},{4,5},{5,4},{6,7},{7,6},{8,9},{9,8},{10,11... | collective-permute-start | bytes 3145736 | tf_op jit(solution)/shard_map/ppermute | solution.py:585
  465.0 50.0 %collective-permute-start.30 = (bf16[512,1024]{1,0:T(8,128)(2,1)S(1)}, bf16[512,1024]{1,0:T(8,128)(2,1)}, u32[]{:S(2)}, u32[]{:S(2)}) collective-permute-start(bf16[512,1024]{1,0:T(8,128)(2,1)S(1)} %collective-permute-done.28.rest_5_), channel_id=1, source_target_pairs={{0,4},{4,0},{8,12},{12,8},{1,5},{5,1},{9,13},{13,9},{2,6},{6,2},{1... | collective-permute-start | bytes 3145736 | tf_op jit(solution)/shard_map/ppermute | solution.py:585
  498.0 56.6 %collective-permute-start.34 = (bf16[512,1024]{1,0:T(8,128)(2,1)S(1)}, bf16[512,1024]{1,0:T(8,128)(2,1)}, u32[]{:S(2)}, u32[]{:S(2)}) collective-permute-start(bf16[512,1024]{1,0:T(8,128)(2,1)S(1)} %collective-permute-done.26.rest_3_), channel_id=1, source_target_pairs={{0,1},{1,0},{2,3},{3,2},{4,5},{5,4},{6,7},{7,6},{8,9},{9,8},{10,11... | collective-permute-start | bytes 3145736 | tf_op jit(solution)/shard_map/ppermute | solution.py:585
  498.0 56.6 %collective-permute-start.36 = (bf16[512,1024]{1,0:T(8,128)(2,1)S(1)}, bf16[512,1024]{1,0:T(8,128)(2,1)}, u32[]{:S(2)}, u32[]{:S(2)}) collective-permute-start(bf16[512,1024]{1,0:T(8,128)(2,1)S(1)} %collective-permute-done.28.rest_5_), channel_id=1, source_target_pairs={{0,1},{1,0},{2,3},{3,2},{4,5},{5,4},{6,7},{7,6},{8,9},{9,8},{10,11... | collective-permute-start | bytes 3145736 | tf_op jit(solution)/shard_map/ppermute | solution.py:585
  498.5 56.0 %collective-permute-start.35 = (bf16[512,1024]{1,0:T(8,128)(2,1)}, bf16[512,1024]{1,0:T(8,128)(2,1)}, u32[]{:S(2)}, u32[]{:S(2)}) collective-permute-start(bf16[512,1024]{1,0:T(8,128)(2,1)} %collective-permute-done.27.rest_4_), channel_id=1, source_target_pairs={{0,1},{1,0},{2,3},{3,2},{4,5},{5,4},{6,7},{7,6},{8,9},{9,8},{10,11... | collective-permute-start | bytes 3145736 | tf_op jit(solution)/shard_map/ppermute | solution.py:585
  498.6 56.0 %collective-permute-start.37 = (bf16[512,1024]{1,0:T(8,128)(2,1)S(1)}, bf16[512,1024]{1,0:T(8,128)(2,1)}, u32[]{:S(2)}, u32[]{:S(2)}) collective-permute-start(bf16[512,1024]{1,0:T(8,128)(2,1)S(1)} %collective-permute-done.29.rest_6_), channel_id=1, source_target_pairs={{0,1},{1,0},{2,3},{3,2},{4,5},{5,4},{6,7},{7,6},{8,9},{9,8},{10,11... | collective-permute-start | bytes 3145736 | tf_op jit(solution)/shard_map/ppermute | solution.py:585
  515.0 39.5 %collective-permute-start.38 = (bf16[512,1024]{1,0:T(8,128)(2,1)}, bf16[512,1024]{1,0:T(8,128)(2,1)}, u32[]{:S(2)}, u32[]{:S(2)}) collective-permute-start(bf16[512,1024]{1,0:T(8,128)(2,1)} %collective-permute-done.30.rest_7_), channel_id=1, source_target_pairs={{0,1},{1,0},{2,3},{3,2},{4,5},{5,4},{6,7},{7,6},{8,9},{9,8},{10,11... | collective-permute-start | bytes 3145736 | tf_op jit(solution)/shard_map/ppermute | solution.py:585
  (49 other events, 886.1 us)
Sparse Core Ops, SparseCore 0:
  11.6 107.5 all-gather.4
  155.0 86.8 all-gather.10
  244.2 124.1 all-gather.8
  370.5 119.7 all-gather.6
